TPU v7x, 512 devices: a 4x2x32 block of a 4x8x32 slice. The times are simulated.
512 devices in a mesh: groups: 2 (over y), seq: 32 (over z), exp: 4 (over x), rep: 2 (over core).
Axes of the slice: x: 4, y: 2, z: 32, core: 2. Of those that a mesh axis runs over, the one named last changes fastest.
The devices are a block of a 4x8x32 slice.
Arguments:
- queries: bfloat16 [4096, 4096], P(('groups', 'seq'), ('exp', 'rep')), parts along dimension 0, may hold values from -4 to 4
- key_rows: bfloat16 [4096, 4096], P(('groups', 'seq'), ('exp', 'rep')), parts along dimension 0, may hold values from -4 to 4
- value_rows: bfloat16 [4096, 4096], P(('groups', 'seq'), ('exp', 'rep')), parts along dimension 0, may hold values from -6 to 6
- decay_log: float32 [4096, 32], P(('groups', 'seq'), ('exp', 'rep')), parts along dimension 0, may hold values from -1.5 to 0
- residual: bfloat16 [4096, 4096], P(('groups', 'seq'), ('exp', 'rep')), parts along dimension 0, may hold values from -6 to 6
- out_gate: bfloat16 [4096, 4096], P(('groups', 'seq'), ('exp', 'rep')), parts along dimension 0, may hold values from -6 to 6
- attn_gain: float32 [4096], P(('exp', 'rep')), may hold values from 0.1 to 1.9
- moe_gain: float32 [4096], P(('exp', 'rep')), may hold values from 0.1 to 1.9
- routes: int32 [4096, 2], P(('groups', 'seq')), parts along dimension 0, may hold values from 0 to 31, as said below
- route_weights: float32 [4096, 2], P(('groups', 'seq')), parts along dimension 0, may hold values from 0.3 to 1
- w_gate: bfloat16 [4, 4608, 4096], P('exp', 'seq'), may hold values from -0.09375 to 0.09375
- w_up: bfloat16 [4, 4608, 4096], P('exp', 'seq'), may hold values from -0.09375 to 0.09375
- w_down: bfloat16 [4, 4608, 4096], P('exp', 'seq'), may hold values from -0.09375 to 0.09375
Outputs:
- layer_out: bfloat16 [4096, 4096], P(('groups', 'seq'), ('exp', 'rep')), parts along dimension 0
There are 2 independent parts, one for each index of `groups`. A program takes and returns all parts, laid end to end along the dimension named above; an argument that names none is the same for every part. Nothing has to cross between parts.
Inputs may be any that keep to these rules, and one draw needn't show every extreme that they name: `routes`: each row names two different experts. Within each aligned block of 64 rows no expert is named by more than 6 rows, every expert is named in every block, and one expert below 4 is named by exactly 6 rows in every block.
All inputs are finite; a program needn't handle non-finite values.
Results may differ from a plain program's by a relative error of at most 0.01.
Values may be sent and summed in bfloat16 or wider, within the bound.
No kernel may reach another device: no remote copies, remote signals or barrier semaphores. Data moves between devices by JAX's collectives and lax.ppermute only.
A program may use at most 64 MiB of HBM per device.

v0:
```python
import jax
import jax.numpy as jnp
from jax import lax
from jax.sharding import PartitionSpec as P

CAP = 6


EPSILON = 1e-06


def in_order(blocks, dim):
    blocks = jnp.moveaxis(blocks, 0, dim)
    dims = blocks.shape
    return blocks.reshape(*dims[:dim], dims[dim] * dims[dim + 1], *dims[dim + 2 :])


def from_everyone(x, axis):
    copies = jnp.broadcast_to(x, (lax.axis_size(axis), *x.shape))
    return lax.all_to_all(copies, axis, split_axis=0, concat_axis=0, tiled=True)


def gathered_copies(x, axis, dim):
    return in_order(from_everyone(x, axis), dim)


def of_everyone(x, axis):
    return from_everyone(x, axis).sum(axis=0)


def on_gathered_pieces(x, axis, dim, work, out_dim):
    span = x.shape[dim]
    pieces = jnp.split(x, 2, axis=dim) if span % 2 == 0 else [x]
    initial = jnp.arange(lax.axis_size(axis)) * span
    blocks = [lax.all_gather(slab, axis) for slab in pieces]
    made = [jax.vmap(work)(b, initial + k * (span // len(pieces))) for k, b in enumerate(blocks)]
    return in_order(jnp.concatenate(made, axis=out_dim + 1), out_dim)


def split_up(x, dim, length):
    dims = x.shape
    blocks = x.reshape(*dims[:dim], length, dims[dim] // length, *dims[dim + 1 :])
    return jnp.moveaxis(blocks, dim, 0)


def summed_on_arrival(x, axis, dim):
    length = lax.axis_size(axis)
    blocks = lax.all_to_all(split_up(x, dim, length), axis, 0, 0, tiled=True)
    return jnp.sum(blocks.astype(jnp.float32), axis=0)


def slot_tables(route_block, weight_block, experts, capacity):
    expert_ids = jnp.arange(experts, dtype=jnp.int32)
    onehot = (route_block[:, :, None] == expert_ids[None, None, :]).astype(jnp.int32)
    tokens = route_block.shape[0]
    flat_hits = onehot.reshape(tokens * 2, experts)
    before = jnp.cumsum(flat_hits, axis=0) - flat_hits
    places = jnp.arange(capacity, dtype=jnp.int32)
    hit_table = flat_hits[:, :, None] * (before[:, :, None] == places[None, None, :]).astype(
        jnp.int32
    )
    hit_table = hit_table.astype(jnp.float32).reshape(tokens, 2, experts * capacity)
    dispatch = jnp.sum(hit_table, axis=1)
    combine = jnp.sum(hit_table * weight_block[:, :, None], axis=1)
    return (dispatch, combine)


def project_rows(slot_rows, weight_rows):
    return lax.dot_general(
        slot_rows, weight_rows, (((1,), (1,)), ((), ())), preferred_element_type=jnp.float32
    )


def shards(
    queries,
    key_rows,
    value_rows,
    decay_log,
    residual,
    out_gate,
    attn_gain,
    moe_gain,
    routes,
    route_weights,
    w_gate,
    w_up,
    w_down,
):
    tokens, columns = queries.shape
    heads_dev = decay_log.shape[1]
    head_dim = columns // heads_dev
    query_heads = queries.reshape(tokens, heads_dev, head_dim)
    key_heads = key_rows.reshape(tokens, heads_dev, head_dim)
    value_heads = value_rows.reshape(tokens, heads_dev, head_dim)
    cumulative = jnp.cumsum(decay_log, axis=0)
    token_positions = jnp.arange(tokens)
    causal = (token_positions[:, None] >= token_positions[None, :])[:, :, None]
    log_gaps = cumulative[:, None, :] - cumulative[None, :, :]
    decay_mask = jnp.where(causal, jnp.exp(jnp.where(causal, log_gaps, 0.0)), 0.0)
    scores = jnp.einsum("thd,jhd->htj", query_heads, key_heads, preferred_element_type=jnp.float32)
    mixing = (scores * jnp.transpose(decay_mask, (2, 0, 1))).astype(jnp.bfloat16)
    local_part = jnp.einsum("htj,jhd->thd", mixing, value_heads, preferred_element_type=jnp.float32)
    ending = cumulative[-1]
    faded_keys = key_heads.astype(jnp.float32) * jnp.exp(ending[None, :] - cumulative)[:, :, None]
    block_state = jnp.einsum("jhd,jhe->hde", faded_keys, value_heads.astype(jnp.float32))
    zeros_state = jnp.zeros_like(block_state)
    every_ending = gathered_copies(ending[None, :], "seq", 0)
    totals = jnp.cumsum(every_ending, axis=0)
    my_index = lax.axis_index("seq")
    before_mine = totals[my_index] - ending
    earlier = (jnp.arange(every_ending.shape[0]) < my_index)[:, None]
    factors = jnp.where(
        earlier, jnp.exp(jnp.where(earlier, before_mine[None, :] - totals, 0.0)), 0.0
    )
    incoming = zeros_state + jnp.einsum(
        "nh,nhde->hde",
        factors,
        lax.all_gather(block_state[None].astype(jnp.bfloat16), "seq", axis=0, tiled=True).astype(
            jnp.float32
        ),
    )
    lifted = query_heads.astype(jnp.float32) * jnp.exp(cumulative)[:, :, None]
    carried_part = jnp.einsum("thd,hde->the", lifted, incoming)
    attended = (local_part + carried_part).reshape(tokens, columns)
    column_groups = lax.axis_size(("exp", "rep"))
    full_width = columns * column_groups
    attn_sumsq = of_everyone(jnp.sum(attended * attended, axis=1), ("exp", "rep"))
    attn_scale = lax.rsqrt(attn_sumsq[:, None] / full_width + EPSILON)
    hidden = residual.astype(jnp.float32) + jax.nn.sigmoid(out_gate.astype(jnp.float32)) * (
        attended * attn_scale * attn_gain
    )
    moe_sumsq = of_everyone(jnp.sum(hidden * hidden, axis=1), ("exp", "rep"))
    normed = (hidden * lax.rsqrt(moe_sumsq[:, None] / full_width + EPSILON) * moe_gain).astype(
        jnp.bfloat16
    )
    experts = lax.axis_size("exp")
    copies = lax.axis_size("rep")
    half_cap = CAP // copies
    dispatch, combine = slot_tables(routes, route_weights, experts, CAP)
    packed = jnp.dot(
        jnp.transpose(dispatch).astype(jnp.bfloat16), normed, preferred_element_type=jnp.float32
    ).astype(jnp.bfloat16)
    packed = packed.reshape(experts * copies, half_cap, columns)
    arrived = lax.all_to_all(packed, ("exp", "rep"), split_axis=0, concat_axis=2, tiled=True)
    rows_local = arrived.reshape(half_cap, full_width)
    gate_mat = w_gate[0]
    up_mat = w_up[0]
    down_mat = w_down[0]

    def activate(slot_rows):
        gate_val = project_rows(slot_rows, gate_mat)
        up_val = project_rows(slot_rows, up_mat)
        return (jax.nn.silu(gate_val) * up_val).astype(jnp.bfloat16)

    def activate_piece(piece, start):
        return activate(piece)

    inner_all = on_gathered_pieces(rows_local, "seq", 0, activate_piece, 0)
    summed = summed_on_arrival(
        jnp.dot(inner_all, down_mat, preferred_element_type=jnp.float32).astype(jnp.bfloat16),
        "seq",
        0,
    ).astype(jnp.bfloat16)
    coming_back = lax.all_to_all(
        summed.reshape(half_cap, column_groups, columns),
        ("exp", "rep"),
        split_axis=1,
        concat_axis=0,
        tiled=True,
    )
    coming_back = coming_back.reshape(experts * CAP, columns)
    expert_mix = jnp.dot(combine, coming_back.astype(jnp.float32))
    return (hidden + expert_mix).astype(jnp.bfloat16)


def solution(mesh):
    return jax.shard_map(
        shards,
        mesh=mesh,
        in_specs=(
            P(("groups", "seq"), ("exp", "rep")),
            P(("groups", "seq"), ("exp", "rep")),
            P(("groups", "seq"), ("exp", "rep")),
            P(("groups", "seq"), ("exp", "rep")),
            P(("groups", "seq"), ("exp", "rep")),
            P(("groups", "seq"), ("exp", "rep")),
            P(("exp", "rep")),
            P(("exp", "rep")),
            P(("groups", "seq"), None),
            P(("groups", "seq"), None),
            P("exp", "seq", None),
            P("exp", "seq", None),
            P("exp", "seq", None),
        ),
        out_specs=P(("groups", "seq"), ("exp", "rep")),
        check_vma=False,
    )
```

profile of v0, /device:TPU:33, one launch (start us, length us, event | category | flops | bytes accessed | tf_op | source)
XLA Modules:
  0.0 394.5 jit_solution(14819607440497474407)
XLA Ops:
  6.6 0.9 copy.82
  7.4 0.1 reduce_window_sum.33
  7.5 0.1 copy.89
  7.6 1.8 convolution_convert_fusion.1
  9.4 0.1 all-gather.3.cloned.1.call-update
  9.5 0.6 broadcast_in_dim.65
  10.1 46.3 %all-to-all-start = ((f32[32,1,4]{2,1,0:T(1,128)}), f32[32,1,4]{2,1,0:T(1,128)S(1)}, u32[]{:S(2)}, u32[]{:S(2)}) async-start(f32[32,1,4]{2,1,0:T(1,128)} %broadcast_in_dim.65), calls=%async_computation | async-start | bytes 32768 | tf_op jit(solution)/shard_map/all_to_all | solution.py:20
  56.4 0.1 copy.83
  56.5 0.8 copy.95
  57.3 0.1 eq.47
  57.4 0.1 fusion.45
  57.5 1.2 convolution_bitcast_fusion.1
  58.7 0.1 copy.92
  58.8 0.2 reduce_window_sum.35
  59.0 18.1 %all-to-all-done = f32[32,1,4]{2,1,0:T(1,128)S(1)} async-done(((f32[32,1,4]{2,1,0:T(1,128)}), f32[32,1,4]{2,1,0:T(1,128)S(1)}, u32[]{:S(2)}, u32[]{:S(2)}) %all-to-all-start) | async-done | bytes 544 | tf_op jit(solution)/shard_map/all_to_all | solution.py:20
  77.1 0.1 reduce_window_sum.34
  77.2 0.1 select_bitcast_fusion
  77.3 0.1 copy.101
  77.4 78.4 %all-gather.3.cloned.1.call-done = bf16[128,128,128]{2,1,0:T(8,128)(2,1)} async-done(((bf16[4,128,128]{2,1,0:T(8,128)(2,1)}), bf16[128,128,128]{2,1,0:T(8,128)(2,1)}) %all-gather.3.cloned.1.call-update) | async-done | bytes 4194320 | tf_op jit(solution)/shard_map/all_gather | solution.py:118
  155.8 4.6 %fusion = f32[4,1,128,128]{3,1,2,0:T(1,128)S(1)} fusion(bf16[32,4,1,1]{0,2,3,1:T(2,128)(2,1)S(1)} %copy.101, bf16[32,4,128,128]{3,2,1,0:T(8,128)(2,1)} %bitcast.109), kind=kOutput, calls=%fused_computation.1 | convolution fusion | flops 4194304 | bytes 4456704 | tf_op jit(solution)/shard_map/nh,nhde->hde/dot_general | solution.py:115
  160.4 0.3 multiply_reduce_fusion.1
  160.8 0.6 broadcast_in_dim.67
  161.4 25.2 %all-to-all-start.1 = ((f32[8,1,64]{2,1,0:T(1,128)}), f32[8,1,64]{2,1,0:T(1,128)S(1)}, u32[]{:S(2)}, u32[]{:S(2)}) async-start(f32[8,1,64]{2,1,0:T(1,128)} %broadcast_in_dim.67), calls=%async_computation.1 | async-start | bytes 8192 | tf_op jit(solution)/shard_map/all_to_all | solution.py:20
  186.6 0.1 fusion.55
  186.7 0.2 eq.51
  186.9 0.2 eq.52
  187.1 0.2 mul.97
  187.3 0.2 mul.98
  187.5 0.1 copy.96
  187.6 0.1 eq.54
  187.7 3.4 all-to-all-done.1
  191.2 0.2 multiply_reduce_fusion
  191.4 0.6 broadcast_in_dim.68
  192.0 3.9 all-to-all-start.2
  195.9 0.2 fusion.57
  196.1 4.4 %all-to-all-done.2 = f32[8,1,64]{2,1,0:T(1,128)S(1)} async-done(((f32[8,1,64]{2,1,0:T(1,128)}), f32[8,1,64]{2,1,0:T(1,128)S(1)}, u32[]{:S(2)}, u32[]{:S(2)}) %all-to-all-start.2) | async-done | bytes 2080 | tf_op jit(solution)/shard_map/all_to_all | solution.py:20
  200.5 0.2 convolution_convert_fusion.2
  200.7 7.8 %all_to_all.55 = bf16[8,3,512]{2,1,0:T(4,128)(2,1)S(1)} all-to-all(bf16[8,3,512]{2,1,0:T(4,128)(2,1)S(1)} %reshape.176), channel_id=1, replica_groups=mesh['groups'=2,'seq'=32,'exp'=4,'rep'=2] {'exp','rep'}, dimensions={0} | all-to-all | bytes 49152 | tf_op jit(solution)/shard_map/all_to_all | solution.py:144
  208.6 44.1 %all_gather.7 = bf16[32,3,4096]{2,1,0:T(4,128)(2,1)S(1)} all-gather(bf16[1,3,4096]{2,1,0:T(4,128)(2,1)S(1)} %bitcast.113), channel_id=1, replica_groups=mesh['groups'=2,'seq'=32,'exp'=4,'rep'=2] {'seq'}, dimensions={0}, use_global_device_ids=true | all-gather | bytes 811008 | tf_op jit(solution)/shard_map/all_gather | solution.py:35
  252.7 0.9 fusion.5
  253.6 0.3 copy-done.8
  254.0 0.9 fusion.13
  255.0 0.4 convolution_convert_fusion
  255.3 0.5 reshape.178
  255.8 103.6 %all_to_all.56 = bf16[32,3,4096]{2,1,0:T(4,128)(2,1)S(1)} all-to-all(bf16[32,3,4096]{2,1,0:T(4,128)(2,1)S(1)} %reshape.178), channel_id=1, replica_groups=mesh['groups'=2,'seq'=32,'exp'=4,'rep'=2] {'seq'}, dimensions={0} | all-to-all | bytes 1572864 | tf_op jit(solution)/shard_map/all_to_all | solution.py:48
  359.5 0.4 reduce_sum.72
  359.9 26.9 %all_to_all.57 = bf16[3,8,512]{2,0,1:T(4,128)(2,1)S(1)} all-to-all(bf16[3,8,512]{2,0,1:T(4,128)(2,1)S(1)} %bitcast.112), channel_id=1, replica_groups=mesh['groups'=2,'seq'=32,'exp'=4,'rep'=2] {'exp','rep'}, dimensions={1} | all-to-all | bytes 49152 | tf_op jit(solution)/shard_map/all_to_all | solution.py:164
  386.8 0.8 fusion.11
  (32 shorter events, 0.3 us)
Async XLA Ops:
  6.5 248.4 %copy-start = (bf16[1,144,4096]{2,1,0:T(8,128)(2,1)S(1)}, bf16[1,144,4096]{2,1,0:T(8,128)(2,1)}, u32[]{:S(2)}) copy-start(bf16[1,144,4096]{2,1,0:T(8,128)(2,1)} %param.25) | copy-start | bytes 3538948
  6.6 149.2 %all-gather.3.cloned.1.call-start = ((), (), s32[]{:S(2)}) async-start(), calls=%async_computation.6 | async-start | bytes 4325376 | tf_op jit(solution)/shard_map/all_gather | solution.py:118
  10.1 67.0 %all-to-all-start = ((f32[32,1,4]{2,1,0:T(1,128)}), f32[32,1,4]{2,1,0:T(1,128)S(1)}, u32[]{:S(2)}, u32[]{:S(2)}) async-start(f32[32,1,4]{2,1,0:T(1,128)} %broadcast_in_dim.65), calls=%async_computation | async-start | bytes 32768 | tf_op jit(solution)/shard_map/all_to_all | solution.py:20
  155.8 4.7 %copy-start.3 = (bf16[64,512]{1,0:T(8,128)(2,1)S(1)}, bf16[64,512]{1,0:T(8,128)(2,1)}, u32[]{:S(2)}) copy-start(bf16[64,512]{1,0:T(8,128)(2,1)} %param.13) | copy-start | bytes 196612
  160.4 27.1 %copy-start.6 = (f32[64,2]{0,1:T(2,128)S(1)}, f32[64,2]{0,1:T(2,128)}, u32[]{:S(2)}) copy-start(f32[64,2]{0,1:T(2,128)} %param.22) | copy-start | bytes 1540
  160.4 30.7 %copy-start.1 = (bf16[64,512]{1,0:T(8,128)(2,1)S(1)}, bf16[64,512]{1,0:T(8,128)(2,1)}, u32[]{:S(2)}) copy-start(bf16[64,512]{1,0:T(8,128)(2,1)} %param.18) | copy-start | bytes 196612
  160.4 30.7 %copy-start.2 = (bf16[64,512]{1,0:T(8,128)(2,1)S(1)}, bf16[64,512]{1,0:T(8,128)(2,1)}, u32[]{:S(2)}) copy-start(bf16[64,512]{1,0:T(8,128)(2,1)} %param.17) | copy-start | bytes 196612
  160.4 30.7 %copy-start.4 = (f32[512]{0:T(512)S(1)}, f32[512]{0:T(512)}, u32[]{:S(2)}) copy-start(f32[512]{0:T(512)} %param.19) | copy-start | bytes 6148
  160.7 39.7 %copy-start.5 = (f32[512]{0:T(512)S(1)}, f32[512]{0:T(512)}, u32[]{:S(2)}) copy-start(f32[512]{0:T(512)} %param.20) | copy-start | bytes 6148
  161.4 29.7 %all-to-all-start.1 = ((f32[8,1,64]{2,1,0:T(1,128)}), f32[8,1,64]{2,1,0:T(1,128)S(1)}, u32[]{:S(2)}, u32[]{:S(2)}) async-start(f32[8,1,64]{2,1,0:T(1,128)} %broadcast_in_dim.67), calls=%async_computation.1 | async-start | bytes 8192 | tf_op jit(solution)/shard_map/all_to_all | solution.py:20
  187.3 65.4 %copy-start.7 = (bf16[1,144,4096]{2,1,0:T(8,128)(2,1)S(1)}, bf16[1,144,4096]{2,1,0:T(8,128)(2,1)}, u32[]{:S(2)}) copy-start(bf16[1,144,4096]{2,1,0:T(8,128)(2,1)} %param.23) | copy-start | bytes 3538948
  192.0 8.5 %all-to-all-start.2 = ((f32[8,1,64]{2,1,0:T(1,128)}), f32[8,1,64]{2,1,0:T(1,128)S(1)}, u32[]{:S(2)}, u32[]{:S(2)}) async-start(f32[8,1,64]{2,1,0:T(1,128)} %broadcast_in_dim.68), calls=%async_computation.2 | async-start | bytes 8192 | tf_op jit(solution)/shard_map/all_to_all | solution.py:20
  252.7 1.3 copy-start.8
Sparse Core Ops, SparseCore 0:
  9.6 146.0 all-gather.2
where the time goes:
time: 395 us; the launch traced here: 394 us
  blocking collectives  182 us (46%)
  waiting for transfers between devices  104 us (26%)
  starting transfers between devices  75.4 us (19%)
  between operations  13.6 us (3%)
  matrix products  11.1 us (3%)
  local copies, waits for them, and re-layouts  5.91 us (1%)
    all_to_all x1, blocking collectives, summed_on_arrival(): blocks = lax.all_to_all(split_up(x, dim, length), axis, 0, 0, tiled=True)  104 us
    all_gather x1, waiting for transfers between devices, shards(): lax.all_gather(block_state[None].astype(jnp.bfloat16), 'seq', axis=0, til...  78.4 us
    all_to_all x3, starting transfers between devices, from_everyone(): return lax.all_to_all(copies, axis, split_axis=0, concat_axis=0, tiled=True)  75.4 us
    all_gather x1, blocking collectives, on_gathered_pieces(): blocks = [lax.all_gather(slab, axis) for slab in pieces]  44.1 us
    all_to_all x1, blocking collectives, shards(): lax.all_to_all(summed.reshape(half_cap, column_groups, columns), ('exp',...  26.9 us
    all_to_all x3, waiting for transfers between devices, from_everyone(): return lax.all_to_all(copies, axis, split_axis=0, concat_axis=0, tiled=True)  25.9 us
  transfers between devices with their start and end apart: 4, of which 4 were waited for; matrix products, arithmetic and copies ran while one was open for 1% of the time, Pallas kernels for 0%

commit v1 on v0

v1 whole, which is shorter than its diff:
```python
import jax
import jax.numpy as jnp
from jax import lax
from jax.sharding import PartitionSpec as P

CAP = 6


EPSILON = 1e-06

F32 = jnp.float32
BF16 = jnp.bfloat16


def three_terms(x):
    high = lax.reduce_precision(x, 8, 7)
    rest = x - high
    middle = lax.reduce_precision(rest, 8, 7)
    low = rest - middle
    return jnp.stack([high, middle, low]).astype(BF16)


def slot_tables(route_block, weight_block, experts, capacity):
    expert_ids = jnp.arange(experts, dtype=jnp.int32)
    onehot = (route_block[:, :, None] == expert_ids[None, None, :]).astype(jnp.int32)
    tokens = route_block.shape[0]
    flat_hits = onehot.reshape(tokens * 2, experts)
    before = jnp.cumsum(flat_hits, axis=0) - flat_hits
    places = jnp.arange(capacity, dtype=jnp.int32)
    hit_table = flat_hits[:, :, None] * (before[:, :, None] == places[None, None, :]).astype(
        jnp.int32
    )
    hit_table = hit_table.astype(jnp.float32).reshape(tokens, 2, experts * capacity)
    dispatch = jnp.sum(hit_table, axis=1)
    combine = jnp.sum(hit_table * weight_block[:, :, None], axis=1)
    return (dispatch, combine)


def padded_rows(x, rows):
    return jnp.pad(x, [(0, 0)] * (x.ndim - 2) + [(0, rows - x.shape[-2]), (0, 0)])


def project_rows(slot_rows, weight_rows):
    return lax.dot_general(
        slot_rows, weight_rows, (((1,), (1,)), ((), ())), preferred_element_type=jnp.float32
    )


def shards(
    queries,
    key_rows,
    value_rows,
    decay_log,
    residual,
    out_gate,
    attn_gain,
    moe_gain,
    routes,
    route_weights,
    w_gate,
    w_up,
    w_down,
):
    tokens, columns = queries.shape
    heads = decay_log.shape[1]
    lanes = columns // heads
    blocks = lax.axis_size("seq")
    near = heads
    far = blocks // near
    experts = lax.axis_size("exp")
    copies = lax.axis_size("rep")
    owners = experts * copies
    width = columns * owners
    half_cap = CAP // copies
    near_groups = [[near * i + k for k in range(near)] for i in range(far)]
    far_groups = [[i + near * k for k in range(far)] for i in range(near)]
    near_all = [[m * owners + j for m in group for j in range(owners)] for group in near_groups]
    my_far = lax.axis_index("seq") // near

    def by_head(x):
        return jnp.swapaxes(x.reshape(tokens, heads, lanes), 0, 1)

    cumulative = jnp.cumsum(decay_log, axis=0)
    terms = jnp.swapaxes(three_terms(cumulative), 0, 2)
    terms = jnp.swapaxes(terms, 1, 2)
    terms = jnp.pad(terms, ((0, 0), (0, 5), (0, lanes - tokens)))
    payload = jnp.concatenate(
        [by_head(queries), by_head(key_rows), by_head(value_rows), terms], axis=1
    )
    arrived = lax.all_to_all(payload, "seq", 0, 0, tiled=True, axis_index_groups=near_groups)
    span = near * tokens
    query = arrived[:, :tokens].reshape(span, lanes)
    key = arrived[:, tokens : 2 * tokens].reshape(span, lanes)
    value = arrived[:, 2 * tokens : 3 * tokens].reshape(span, lanes)
    within = arrived[:, 3 * tokens : 3 * tokens + 3, :tokens].astype(F32).sum(axis=1)
    ends = within[:, -1]
    starts = jnp.cumsum(ends) - ends
    total = jnp.sum(ends)
    cum = (within + starts[:, None]).reshape(span)
    faded = (key.astype(F32) * jnp.exp(total - cum)[:, None]).astype(BF16)
    state = lax.dot_general(faded, value, (((0,), (0,)), ((), ())), preferred_element_type=F32)
    total_rows = jnp.pad(jnp.broadcast_to(three_terms(total)[:, None], (3, lanes)), ((0, 5), (0, 0)))
    sent = jnp.concatenate([state.astype(BF16), total_rows], axis=0)
    states = lax.all_gather(sent, "seq", axis=0, tiled=False, axis_index_groups=far_groups)
    totals = states[:, lanes : lanes + 3, 0].astype(F32).sum(axis=1)
    reached = jnp.cumsum(totals)
    order = jnp.arange(far)
    before_mine = jnp.sum(jnp.where(order < my_far, totals, 0.0))
    earlier = order < my_far
    factors = jnp.where(earlier, jnp.exp(jnp.where(earlier, before_mine - reached, 0.0)), 0.0)
    incoming = jnp.sum(factors[:, None, None] * states[:, :lanes].astype(F32), axis=0)
    scores = lax.dot_general(query, key, (((1,), (1,)), ((), ())), preferred_element_type=F32)
    places = jnp.arange(span)
    causal = places[:, None] >= places[None, :]
    decays = jnp.where(causal, jnp.exp(jnp.where(causal, cum[:, None] - cum[None, :], 0.0)), 0.0)
    mixing = (scores * decays).astype(BF16)
    lifted = (query.astype(F32) * jnp.exp(cum)[:, None]).astype(BF16)
    attended = jnp.dot(mixing, value, preferred_element_type=F32) + jnp.dot(
        lifted, incoming.astype(BF16), preferred_element_type=F32
    )
    attended = attended.astype(BF16).reshape(near, tokens, lanes)
    attended = lax.all_to_all(attended, "seq", 0, 0, tiled=True, axis_index_groups=near_groups)
    attended = jnp.swapaxes(attended, 0, 1).reshape(tokens, columns).astype(F32)

    sumsq = jnp.sum(attended * attended, axis=1)
    branch = jax.nn.sigmoid(out_gate.astype(F32)) * attended * attn_gain
    dispatch, combine = slot_tables(routes, route_weights, experts, CAP)
    both = jnp.concatenate([residual, branch.astype(BF16)], axis=1)
    packed = jnp.dot(jnp.transpose(dispatch).astype(BF16), both, preferred_element_type=F32)
    packed = packed.astype(BF16).reshape(owners, half_cap * 2 * heads, lanes)
    sums = jnp.pad(three_terms(sumsq), ((0, 0), (0, lanes - tokens)))
    gains = three_terms(moe_gain).reshape(3 * heads, lanes)
    extra = jnp.concatenate([sums, gains], axis=0)
    extra = padded_rows(extra, 16)
    extra = jnp.broadcast_to(extra[None], (owners, *extra.shape))
    payload = jnp.concatenate([packed, extra], axis=1)
    arrived = lax.all_to_all(payload, ("exp", "rep"), 0, 0, tiled=True)
    size = half_cap * 2 * heads
    rows = arrived[:, :size].reshape(owners, half_cap, 2, columns).astype(F32)
    sums = arrived[:, size : size + 3, :tokens].astype(F32).sum(axis=(0, 1))
    gains = arrived[:, size + 3 : size + 3 + 3 * heads].astype(F32)
    gains = gains.reshape(owners, 3, columns).sum(axis=1)
    attn_scale = lax.rsqrt(sums / width + EPSILON)
    me = lax.axis_index(("exp", "rep"))
    mine = lax.dynamic_slice_in_dim(dispatch, me * half_cap, half_cap, axis=1)
    slot_scale = jnp.sum(mine * attn_scale[:, None], axis=0)
    slot_hidden = rows[:, :, 0] + slot_scale[None, :, None] * rows[:, :, 1]
    moe_sumsq = jnp.sum(slot_hidden * slot_hidden, axis=(0, 2))
    moe_scale = lax.rsqrt(moe_sumsq / width + EPSILON)
    normed = (slot_hidden * moe_scale[None, :, None] * gains[:, None, :]).astype(BF16)
    normed = jnp.swapaxes(normed, 0, 1).reshape(half_cap * width // lanes, lanes)

    gathered = lax.all_gather(normed, "seq", axis=0, tiled=True, axis_index_groups=far_groups)
    gathered = lax.all_gather(gathered, "seq", axis=0, tiled=True, axis_index_groups=near_groups)
    slot_rows = gathered.reshape(blocks * half_cap, width)
    gate_val = project_rows(slot_rows, w_gate[0])
    up_val = project_rows(slot_rows, w_up[0])
    inner = (jax.nn.silu(gate_val) * up_val).astype(BF16)
    partial = jnp.dot(inner, w_down[0], preferred_element_type=F32).astype(BF16)
    pieces = partial.reshape(near, far * half_cap, owners, columns)
    pieces = jnp.swapaxes(pieces, 1, 2).reshape(near * owners, far * half_cap, columns)
    pieces = lax.all_to_all(
        pieces, ("seq", "exp", "rep"), 0, 0, tiled=True, axis_index_groups=near_all
    )
    pieces = pieces.reshape(near, owners, far, half_cap, columns).astype(F32).sum(axis=0)
    pieces = jnp.swapaxes(pieces.astype(BF16), 0, 1).reshape(far, owners * half_cap, columns)
    pieces = lax.all_to_all(pieces, "seq", 0, 0, tiled=True, axis_index_groups=far_groups)
    returned = pieces.astype(F32).sum(axis=0).astype(BF16)
    expert_mix = jnp.dot(combine, returned.astype(F32), precision=lax.Precision.HIGHEST)
    hidden = residual.astype(F32) + attn_scale[:, None] * branch
    return (hidden + expert_mix).astype(BF16)


def solution(mesh):
    return jax.shard_map(
        shards,
        mesh=mesh,
        in_specs=(
            P(("groups", "seq"), ("exp", "rep")),
            P(("groups", "seq"), ("exp", "rep")),
            P(("groups", "seq"), ("exp", "rep")),
            P(("groups", "seq"), ("exp", "rep")),
            P(("groups", "seq"), ("exp", "rep")),
            P(("groups", "seq"), ("exp", "rep")),
            P(("exp", "rep")),
            P(("exp", "rep")),
            P(("groups", "seq"), None),
            P(("groups", "seq"), None),
            P("exp", "seq", None),
            P("exp", "seq", None),
            P("exp", "seq", None),
        ),
        out_specs=P(("groups", "seq"), ("exp", "rep")),
        check_vma=False,
    )
```

time: 395 us -> 252 us (0.64)
  waiting for transfers between devices: 104 us -> 12.6 us
  starting transfers between devices: 75.4 us -> 27.1 us
  between operations: 13.6 us -> 5.51 us
  other arithmetic: 1.52 us -> 6.16 us
  matrix products: 11.1 us -> 6.71 us
  blocking collectives: 182 us -> 186 us
    all_gather x1 -> x0, waiting for transfers between devices: 78.4 us -> none  [shards(): lax.all_gather(block_state[None].astype(jnp.bfloat16), 'seq', axis=0, til...]
    all_gather x1 -> x3, blocking collectives: 44.1 us -> 109 us  [the longest x1 64.6 us: shards(): lax.all_gather(sent, 'seq', axis=0, tiled=False, axis_index_groups=far_gr...]
    all_to_all x3 -> x2, blocking collectives: 138 us -> 77.4 us  [the longest x1 42.6 us: shards(): lax.all_to_all(pieces, 'seq', 0, 0, tiled=True, axis_index_groups=far_gro...]
    all_to_all x3, starting transfers between devices: 75.4 us -> 27.1 us  [the longest x1 13.5 us: shards(): arrived = lax.all_to_all(payload, ('exp', 'rep'), 0, 0, tiled=True)]
    all_to_all x3, waiting for transfers between devices: 25.9 us -> 12.6 us  [the longest x1 4.77 us: shards(): arrived = lax.all_to_all(payload, ('exp', 'rep'), 0, 0, tiled=True)]
    dot_general x7 -> x6, matrix products: 9.3 us -> 4.97 us  [the longest x1 2.5 us: shards(): partial = jnp.dot(inner, w_down[0], preferred_element_type=F32).astype(BF16)]
  transfers between devices with their start and end apart: 4 -> 3, of which waited for: 4 -> 3; matrix products, arithmetic and copies ran while one was open for 1% -> 1% of each run, Pallas kernels for 0% -> 0%
where the time goes in v1:
time: 252 us; the launch traced here: 250 us
  blocking collectives  186 us (74%)
  starting transfers between devices  27.1 us (11%)
  waiting for transfers between devices  12.6 us (5%)
  matrix products  6.71 us (3%)
  other arithmetic  6.16 us (2%)
  local copies, waits for them, and re-layouts  5.53 us (2%)
  between operations  5.51 us (2%)
    all_gather x1, blocking collectives, shards(): lax.all_gather(sent, 'seq', axis=0, tiled=False, axis_index_groups=far_gr...  64.6 us
    all_to_all x1, blocking collectives, shards(): lax.all_to_all(pieces, 'seq', 0, 0, tiled=True, axis_index_groups=far_gro...  42.6 us
    all_to_all x1, blocking collectives, shards(): lax.all_to_all(pieces, ('seq', 'exp', 'rep'), 0, 0, tiled=True, axis_inde...  34.8 us
    all_gather x1, blocking collectives, shards(): lax.all_gather(normed, 'seq', axis=0, tiled=True, axis_index_groups=far_g...  30.1 us
    all_gather x1, blocking collectives, shards(): lax.all_gather(gathered, 'seq', axis=0, tiled=True, axis_index_groups=nea...  14.1 us
    all_to_all x1, starting transfers between devices, shards(): arrived = lax.all_to_all(payload, ('exp', 'rep'), 0, 0, tiled=True)  13.5 us
    all_to_all x1, starting transfers between devices, shards(): lax.all_to_all(payload, 'seq', 0, 0, tiled=True, axis_index_groups=near_g...  9.02 us
  transfers between devices with their start and end apart: 3, of which 3 were waited for; matrix products, arithmetic and copies ran while one was open for 1% of the time, Pallas kernels for 0%

profile of v1, /device:TPU:33, one launch (start us, length us, event | category | flops | bytes accessed | tf_op | source)
XLA Modules:
  0.0 249.9 jit_solution(15623896831576845503)
XLA Ops:
  0.0 0.9 copy.103
  0.9 0.1 reduce_window_sum.39
  1.1 0.9 bitcast_bitcast_fusion.2
  1.9 0.9 bitcast_bitcast_fusion
  2.8 0.7 fusion.24
  3.5 9.0 %all-to-all-start = ((bf16[4,200,128]{2,1,0:T(8,128)(2,1)}), bf16[4,200,128]{2,1,0:T(8,128)(2,1)S(1)}, u32[]{:S(2)}, u32[]{:S(2)}) async-start(bf16[4,200,128]{2,1,0:T(8,128)(2,1)} %fusion.24), calls=%async_computation | async-start | bytes 409600 | tf_op jit(solution)/shard_map/all_to_all | solution.py:90
  12.6 0.1 copy.99
  12.7 0.1 eq.47
  13.0 4.8 %all-to-all-done = bf16[4,200,128]{2,1,0:T(8,128)(2,1)S(1)} async-done(((bf16[4,200,128]{2,1,0:T(8,128)(2,1)}), bf16[4,200,128]{2,1,0:T(8,128)(2,1)S(1)}, u32[]{:S(2)}, u32[]{:S(2)}) %all-to-all-start) | async-done | bytes 204832 | tf_op jit(solution)/shard_map/all_to_all | solution.py:90
  17.9 0.7 slice_reduce_fusion
  23.6 0.7 subtract_exponential_fusion
  24.6 0.3 fusion.16
  24.8 0.1 pad_maximum_fusion.1
  24.9 64.6 %all-gather = bf16[1088,128]{1,0:T(8,128)(2,1)S(1)} all-gather(bf16[136,128]{1,0:T(8,128)(2,1)S(1)} %pad_maximum_fusion.1), channel_id=2, replica_groups={{0,32,64,96,128,160,192,224},{8,40,72,104,136,168,200,232},{16,48,80,11..., dimensions={0}, use_global_device_ids=true | all-gather | bytes 313344 | tf_op jit(solution)/shard_map/all_gather | solution.py:104
  89.6 0.1 convert_reduce_fusion.1
  89.7 0.6 fusion.63
  90.3 0.2 reduce-window.14
  90.5 0.7 fusion.62
  91.2 0.1 multiply_reduce_fusion
  91.3 0.2 fusion.39
  91.5 1.0 fusion.8
  92.5 4.6 %all-to-all-start.1 = ((bf16[4,64,128]{2,1,0:T(8,128)(2,1)}), bf16[4,64,128]{2,1,0:T(8,128)(2,1)S(1)}, u32[]{:S(2)}, u32[]{:S(2)}) async-start(bf16[4,64,128]{2,1,0:T(8,128)(2,1)} %bitcast.15), calls=%async_computation.1 | async-start | bytes 131072 | tf_op jit(solution)/shard_map/all_to_all | solution.py:122
  97.2 0.1 copy.107
  97.3 0.2 reduce_window_sum.38
  97.6 0.2 eq.51
  97.8 0.2 eq.52
  98.0 0.2 mul.118
  98.2 0.2 mul.119
  98.4 0.2 fusion.57
  98.6 3.1 %all-to-all-done.1 = bf16[4,64,128]{2,1,0:T(8,128)(2,1)S(1)} async-done(((bf16[4,64,128]{2,1,0:T(8,128)(2,1)}), bf16[4,64,128]{2,1,0:T(8,128)(2,1)S(1)}, u32[]{:S(2)}, u32[]{:S(2)}) %all-to-all-start.1) | async-done | bytes 65568 | tf_op jit(solution)/shard_map/all_to_all | solution.py:122
  101.7 0.1 fusion.25
  101.9 0.2 convolution_convert_fusion.1
  102.2 0.6 pad_maximum_fusion
  102.8 13.5 %all-to-all-start.2 = ((bf16[8,40,128]{2,1,0:T(8,128)(2,1)}), bf16[8,40,128]{2,1,0:T(8,128)(2,1)S(1)}, u32[]{:S(2)}, u32[]{:S(2)}) async-start(bf16[8,40,128]{2,1,0:T(8,128)(2,1)} %pad_maximum_fusion), calls=%async_computation.2 | async-start | bytes 163840 | tf_op jit(solution)/shard_map/all_to_all | solution.py:137
  116.4 4.8 %all-to-all-done.2 = bf16[8,40,128]{2,1,0:T(8,128)(2,1)S(1)} async-done(((bf16[8,40,128]{2,1,0:T(8,128)(2,1)}), bf16[8,40,128]{2,1,0:T(8,128)(2,1)S(1)}, u32[]{:S(2)}, u32[]{:S(2)}) %all-to-all-start.2) | async-done | bytes 81952 | tf_op jit(solution)/shard_map/all_to_all | solution.py:137
  121.5 0.1 multiply_reduce_fusion.3
  121.6 0.2 multiply_reduce_fusion.2
  121.9 30.1 %all_gather.14 = bf16[768,128]{1,0:T(8,128)(2,1)S(1)} all-gather(bf16[96,128]{1,0:T(8,128)(2,1)S(1)} %reshape.315), channel_id=1, replica_groups={{0,32,64,96,128,160,192,224},{8,40,72,104,136,168,200,232},{16,48,80,11..., dimensions={0}, use_global_device_ids=true | all-gather | bytes 221184 | tf_op jit(solution)/shard_map/all_gather | solution.py:153
  152.0 14.1 %all_gather.15 = bf16[3072,128]{1,0:T(8,128)(2,1)S(1)} all-gather(bf16[768,128]{1,0:T(8,128)(2,1)S(1)} %all_gather.14), channel_id=1, replica_groups={{0,8,16,24},{32,40,48,56},{64,72,80,88},{96,104,112,120},{128,136,144,1..., dimensions={0}, use_global_device_ids=true | all-gather | bytes 983040 | tf_op jit(solution)/shard_map/all_gather | solution.py:154
  166.2 0.3 reshape.316
  166.5 1.7 fusion.3
  168.3 2.5 %convolution_convert_fusion = bf16[96,4096]{1,0:T(8,128)(2,1)S(1)} fusion(bf16[1,144,4096]{2,1,0:T(8,128)(2,1)S(1)} %copy-done, bf16[96,4096]{1,0:T(8,128)(2,1)S(1)} %reshape.316, bf16[1,144,4096]{2,1,0:T(8,128)(2,1)} %param.24, f32[96,144]{0,1:T(8,128)S(1)} %fusion.3), kind=kOutput, calls=%fused_computation | convolution fusion | flops 226968576 | bytes 3987456 | tf_op jit(solution)/shard_map/dot_general | solution.py:159
  170.8 0.3 copy.122
  171.1 0.2 copy.111
  171.3 34.8 %all_to_all.25 = bf16[32,24,512]{2,1,0:T(8,128)(2,1)S(1)} all-to-all(bf16[32,24,512]{2,1,0:T(8,128)(2,1)S(1)} %bitcast.121), channel_id=1, replica_groups={{0,1,2,3,4,5,6,7,8,9,10,11,12,13,14,15,16,17,18,19,20,21,22,23,24,25,26..., dimensions={0} | all-to-all | bytes 1572864 | tf_op jit(solution)/shard_map/all_to_all | solution.py:162
  206.1 0.1 reduce.6
  206.4 42.6 %all_to_all.26 = bf16[8,24,512]{2,1,0:T(8,128)(2,1)S(1)} all-to-all(bf16[8,24,512]{2,1,0:T(8,128)(2,1)S(1)} %copy.114), channel_id=1, replica_groups={{0,32,64,96,128,160,192,224},{8,40,72,104,136,168,200,232},{16,48,80,11..., dimensions={0} | all-to-all | bytes 393216 | tf_op jit(solution)/shard_map/all_to_all | solution.py:167
  249.1 0.8 fusion.9
  (59 shorter events, 1.6 us)
Async XLA Ops:
  0.0 168.3 %copy-start = (bf16[1,144,4096]{2,1,0:T(8,128)(2,1)S(1)}, bf16[1,144,4096]{2,1,0:T(8,128)(2,1)}, u32[]{:S(2)}) copy-start(bf16[1,144,4096]{2,1,0:T(8,128)(2,1)} %param.25) | copy-start | bytes 3538948
  0.0 12.6 %copy-start.4 = (f32[512]{0:T(512)S(1)}, f32[512]{0:T(512)}, u32[]{:S(2)}) copy-start(f32[512]{0:T(512)} %param.20) | copy-start | bytes 6148
  0.0 12.6 %copy-start.5 = (s32[64,2]{0,1:T(2,128)S(1)}, s32[64,2]{0,1:T(2,128)}, u32[]{:S(2)}) copy-start(s32[64,2]{0,1:T(2,128)} %param.21) | copy-start | bytes 1540
  3.5 14.2 %all-to-all-start = ((bf16[4,200,128]{2,1,0:T(8,128)(2,1)}), bf16[4,200,128]{2,1,0:T(8,128)(2,1)S(1)}, u32[]{:S(2)}, u32[]{:S(2)}) async-start(bf16[4,200,128]{2,1,0:T(8,128)(2,1)} %fusion.24), calls=%async_computation | async-start | bytes 409600 | tf_op jit(solution)/shard_map/all_to_all | solution.py:90
  24.6 72.7 %copy-start.6 = (f32[64,2]{0,1:T(2,128)S(1)}, f32[64,2]{0,1:T(2,128)}, u32[]{:S(2)}) copy-start(f32[64,2]{0,1:T(2,128)} %param.22) | copy-start | bytes 1540
  92.5 9.3 %copy-start.1 = (bf16[64,512]{1,0:T(8,128)(2,1)S(1)}, bf16[64,512]{1,0:T(8,128)(2,1)}, u32[]{:S(2)}) copy-start(bf16[64,512]{1,0:T(8,128)(2,1)} %param.18) | copy-start | bytes 196612
  92.5 9.3 %copy-start.3 = (f32[512]{0:T(512)S(1)}, f32[512]{0:T(512)}, u32[]{:S(2)}) copy-start(f32[512]{0:T(512)} %param.19) | copy-start | bytes 6148
  92.5 9.4 %copy-start.2 = (bf16[64,512]{1,0:T(8,128)(2,1)S(1)}, bf16[64,512]{1,0:T(8,128)(2,1)}, u32[]{:S(2)}) copy-start(bf16[64,512]{1,0:T(8,128)(2,1)} %param.17) | copy-start | bytes 196612
  92.5 9.2 %all-to-all-start.1 = ((bf16[4,64,128]{2,1,0:T(8,128)(2,1)}), bf16[4,64,128]{2,1,0:T(8,128)(2,1)S(1)}, u32[]{:S(2)}, u32[]{:S(2)}) async-start(bf16[4,64,128]{2,1,0:T(8,128)(2,1)} %bitcast.15), calls=%async_computation.1 | async-start | bytes 131072 | tf_op jit(solution)/shard_map/all_to_all | solution.py:122
  102.8 18.4 %all-to-all-start.2 = ((bf16[8,40,128]{2,1,0:T(8,128)(2,1)}), bf16[8,40,128]{2,1,0:T(8,128)(2,1)S(1)}, u32[]{:S(2)}, u32[]{:S(2)}) async-start(bf16[8,40,128]{2,1,0:T(8,128)(2,1)} %pad_maximum_fusion), calls=%async_computation.2 | async-start | bytes 163840 | tf_op jit(solution)/shard_map/all_to_all | solution.py:137

commit v2 on v1

--- a/solution.py
+++ b/solution.py
@@ -75,7 +75,6 @@
     near_groups = [[near * i + k for k in range(near)] for i in range(far)]
     far_groups = [[i + near * k for k in range(far)] for i in range(near)]
     near_all = [[m * owners + j for m in group for j in range(owners)] for group in near_groups]
-    my_far = lax.axis_index("seq") // near
 
     def by_head(x):
         return jnp.swapaxes(x.reshape(tokens, heads, lanes), 0, 1)
@@ -99,16 +98,12 @@
     cum = (within + starts[:, None]).reshape(span)
     faded = (key.astype(F32) * jnp.exp(total - cum)[:, None]).astype(BF16)
     state = lax.dot_general(faded, value, (((0,), (0,)), ((), ())), preferred_element_type=F32)
-    total_rows = jnp.pad(jnp.broadcast_to(three_terms(total)[:, None], (3, lanes)), ((0, 5), (0, 0)))
-    sent = jnp.concatenate([state.astype(BF16), total_rows], axis=0)
-    states = lax.all_gather(sent, "seq", axis=0, tiled=False, axis_index_groups=far_groups)
-    totals = states[:, lanes : lanes + 3, 0].astype(F32).sum(axis=1)
-    reached = jnp.cumsum(totals)
-    order = jnp.arange(far)
-    before_mine = jnp.sum(jnp.where(order < my_far, totals, 0.0))
-    earlier = order < my_far
-    factors = jnp.where(earlier, jnp.exp(jnp.where(earlier, before_mine - reached, 0.0)), 0.0)
-    incoming = jnp.sum(factors[:, None, None] * states[:, :lanes].astype(F32), axis=0)
+    carried = jnp.zeros_like(state)
+    for k in range(far - 1):
+        running = (jnp.exp(total) * carried + state).astype(BF16)
+        passed = [(near * k + i, near * (k + 1) + i) for i in range(near)]
+        carried = carried + lax.ppermute(running, "seq", passed).astype(F32)
+    incoming = carried
     scores = lax.dot_general(query, key, (((1,), (1,)), ((), ())), preferred_element_type=F32)
     places = jnp.arange(span)
     causal = places[:, None] >= places[None, :]

time: 252 us -> 246 us (0.976)
  starting transfers between devices: 27.1 us -> 49.9 us
  blocking collectives: 186 us -> 168 us
  between operations: 5.51 us -> 1.21 us
  waiting for transfers between devices: 12.6 us -> 8.94 us
    all_gather x1 -> x0, blocking collectives: 64.6 us -> none  [shards(): lax.all_gather(sent, 'seq', axis=0, tiled=False, axis_index_groups=far_gr...]
    all_gather x1, blocking collectives: 30.1 us -> 61.9 us  [shards(): lax.all_gather(normed, 'seq', axis=0, tiled=True, axis_index_groups=far_g...]
    ppermute x0 -> x7, starting transfers between devices: none -> 16.3 us  [shards(): carried = carried + lax.ppermute(running, 'seq', passed).astype(F32)]
    all_to_all x1, starting transfers between devices: 13.5 us -> 28.6 us  [shards(): arrived = lax.all_to_all(payload, ('exp', 'rep'), 0, 0, tiled=True)]
    all_to_all x0 -> x1, blocking collectives: none -> 14.5 us  [shards(): lax.all_to_all(payload, 'seq', 0, 0, tiled=True, axis_index_groups=near_g...]
    all_to_all x1 -> x0, starting transfers between devices: 9.02 us -> none  [shards(): lax.all_to_all(payload, 'seq', 0, 0, tiled=True, axis_index_groups=near_g...]
    all_to_all x1 -> x0, waiting for transfers between devices: 4.77 us -> none  [shards(): lax.all_to_all(payload, 'seq', 0, 0, tiled=True, axis_index_groups=near_g...]
  transfers between devices with their start and end apart: 3 -> 9, of which waited for: 3 -> 3; matrix products, arithmetic and copies ran while one was open for 1% -> 1% of each run, Pallas kernels for 0% -> 0%
where the time goes in v2:
time: 246 us; the launch traced here: 244 us
  blocking collectives  168 us (68%)
  starting transfers between devices  49.9 us (20%)
  waiting for transfers between devices  8.94 us (4%)
  matrix products  6.72 us (3%)
  local copies, waits for them, and re-layouts  5.54 us (2%)
  other arithmetic  3.77 us (2%)
    all_gather x1, blocking collectives, shards(): lax.all_gather(normed, 'seq', axis=0, tiled=True, axis_index_groups=far_g...  61.9 us
    all_to_all x1, blocking collectives, shards(): lax.all_to_all(pieces, 'seq', 0, 0, tiled=True, axis_index_groups=far_gro...  43 us
    all_to_all x1, blocking collectives, shards(): lax.all_to_all(pieces, ('seq', 'exp', 'rep'), 0, 0, tiled=True, axis_inde...  34.4 us
    all_to_all x1, starting transfers between devices, shards(): arrived = lax.all_to_all(payload, ('exp', 'rep'), 0, 0, tiled=True)  28.6 us
    ppermute x7, starting transfers between devices, shards(): carried = carried + lax.ppermute(running, 'seq', passed).astype(F32)  16.3 us
    all_gather x1, blocking collectives, shards(): lax.all_gather(gathered, 'seq', axis=0, tiled=True, axis_index_groups=nea...  14.6 us
    all_to_all x1, blocking collectives, shards(): lax.all_to_all(payload, 'seq', 0, 0, tiled=True, axis_index_groups=near_g...  14.5 us
    all_to_all x1, starting transfers between devices, shards(): lax.all_to_all(attended, 'seq', 0, 0, tiled=True, axis_index_groups=near_...  5.08 us
  transfers between devices with their start and end apart: 9, of which 3 were waited for; matrix products, arithmetic and copies ran while one was open for 1% of the time, Pallas kernels for 0%

profile of v2, /device:TPU:33, one launch (start us, length us, event | category | flops | bytes accessed | tf_op | source)
XLA Modules:
  0.0 244.4 jit_solution(3336374758753709650)
XLA Ops:
  0.0 0.9 copy.103
  0.9 0.1 reduce_window_sum.32
  1.1 0.9 bitcast_bitcast_fusion.2
  2.0 0.9 bitcast_bitcast_fusion
  2.9 14.5 %all_to_all.25 = bf16[4,200,128]{2,1,0:T(8,128)(2,1)S(1)} all-to-all(bf16[4,200,128]{2,1,0:T(8,128)(2,1)S(1)} %fusion.22), channel_id=1, replica_groups={{0,8,16,24},{32,40,48,56},{64,72,80,88},{96,104,112,120},{128,136,144,1..., dimensions={0} | all-to-all | bytes 409600 | tf_op jit(solution)/shard_map/all_to_all | solution.py:89
  17.5 0.7 slice_reduce_fusion
  18.9 0.7 subtract_exponential_fusion
  19.6 0.3 add_convert_fusion.6
  19.9 12.3 %collective-permute-start = (bf16[128,128]{1,0:T(8,128)(2,1)S(1)}, bf16[128,128]{1,0:T(8,128)(2,1)S(1)}, u32[]{:S(2)}, u32[]{:S(2)}) collective-permute-start(bf16[128,128]{1,0:T(8,128)(2,1)S(1)} %get-tuple-element.27), channel_id=1, source_target_pairs={{0,32},{8,40},{16,48},{24,56},{1,33},{9,41},{17,49},{25,57},{2,34}... | collective-permute-start | bytes 98312 | tf_op jit(solution)/shard_map/ppermute | solution.py:105
  32.2 1.0 collective-permute-done
  33.2 0.7 collective-permute-start.1
  33.9 0.7 collective-permute-start.2
  34.6 0.1 copy.99
  34.7 0.1 eq.47
  34.9 0.7 collective-permute-start.3
  35.7 0.7 collective-permute-start.4
  36.5 0.7 collective-permute-start.5
  37.3 0.7 collective-permute-start.6
  37.9 0.3 fusion.6
  38.3 0.9 fusion.7
  39.2 5.1 %all-to-all-start.1 = ((bf16[4,64,128]{2,1,0:T(8,128)(2,1)}), bf16[4,64,128]{2,1,0:T(8,128)(2,1)S(1)}, u32[]{:S(2)}, u32[]{:S(2)}) async-start(bf16[4,64,128]{2,1,0:T(8,128)(2,1)} %bitcast.9), calls=%async_computation.1 | async-start | bytes 131072 | tf_op jit(solution)/shard_map/all_to_all | solution.py:117
  44.4 0.1 copy.107
  44.5 0.2 reduce_window_sum.31
  44.8 0.2 eq.51
  45.0 0.2 eq.52
  45.2 0.2 mul.143
  45.4 0.2 mul.144
  45.6 0.2 fusion.55
  45.8 3.1 %all-to-all-done.1 = bf16[4,64,128]{2,1,0:T(8,128)(2,1)S(1)} async-done(((bf16[4,64,128]{2,1,0:T(8,128)(2,1)}), bf16[4,64,128]{2,1,0:T(8,128)(2,1)S(1)}, u32[]{:S(2)}, u32[]{:S(2)}) %all-to-all-start.1) | async-done | bytes 65568 | tf_op jit(solution)/shard_map/all_to_all | solution.py:117
  48.9 0.1 fusion.23
  49.1 0.2 convolution_convert_fusion.1
  49.3 0.6 pad_maximum_fusion
  50.0 28.6 %all-to-all-start.2 = ((bf16[8,40,128]{2,1,0:T(8,128)(2,1)}), bf16[8,40,128]{2,1,0:T(8,128)(2,1)S(1)}, u32[]{:S(2)}, u32[]{:S(2)}) async-start(bf16[8,40,128]{2,1,0:T(8,128)(2,1)} %pad_maximum_fusion), calls=%async_computation.2 | async-start | bytes 163840 | tf_op jit(solution)/shard_map/all_to_all | solution.py:132
  78.7 4.8 %all-to-all-done.2 = bf16[8,40,128]{2,1,0:T(8,128)(2,1)S(1)} async-done(((bf16[8,40,128]{2,1,0:T(8,128)(2,1)}), bf16[8,40,128]{2,1,0:T(8,128)(2,1)S(1)}, u32[]{:S(2)}, u32[]{:S(2)}) %all-to-all-start.2) | async-done | bytes 81952 | tf_op jit(solution)/shard_map/all_to_all | solution.py:132
  83.8 0.1 multiply_reduce_fusion.2
  83.9 0.2 multiply_reduce_fusion.1
  84.1 0.1 fusion.45
  84.2 61.9 %all_gather.6 = bf16[768,128]{1,0:T(8,128)(2,1)S(1)} all-gather(bf16[96,128]{1,0:T(8,128)(2,1)S(1)} %reshape.251), channel_id=1, replica_groups={{0,32,64,96,128,160,192,224},{8,40,72,104,136,168,200,232},{16,48,80,11..., dimensions={0}, use_global_device_ids=true | all-gather | bytes 221184 | tf_op jit(solution)/shard_map/all_gather | solution.py:148
  146.1 14.6 %all_gather.7 = bf16[3072,128]{1,0:T(8,128)(2,1)S(1)} all-gather(bf16[768,128]{1,0:T(8,128)(2,1)S(1)} %all_gather.6), channel_id=1, replica_groups={{0,8,16,24},{32,40,48,56},{64,72,80,88},{96,104,112,120},{128,136,144,1..., dimensions={0}, use_global_device_ids=true | all-gather | bytes 983040 | tf_op jit(solution)/shard_map/all_gather | solution.py:149
  160.7 0.3 reshape.252
  161.0 1.7 fusion.3
  162.8 2.5 %convolution_convert_fusion = bf16[96,4096]{1,0:T(8,128)(2,1)S(1)} fusion(bf16[1,144,4096]{2,1,0:T(8,128)(2,1)S(1)} %copy-done, bf16[96,4096]{1,0:T(8,128)(2,1)S(1)} %reshape.252, bf16[1,144,4096]{2,1,0:T(8,128)(2,1)} %param.24, f32[96,144]{0,1:T(8,128)S(1)} %fusion.3), kind=kOutput, calls=%fused_computation | convolution fusion | flops 226968576 | bytes 3987456 | tf_op jit(solution)/shard_map/dot_general | solution.py:154
  165.3 0.3 copy.122
  165.6 0.2 copy.111
  165.8 34.4 %all_to_all.26 = bf16[32,24,512]{2,1,0:T(8,128)(2,1)S(1)} all-to-all(bf16[32,24,512]{2,1,0:T(8,128)(2,1)S(1)} %bitcast.107), channel_id=1, replica_groups={{0,1,2,3,4,5,6,7,8,9,10,11,12,13,14,15,16,17,18,19,20,21,22,23,24,25,26..., dimensions={0} | all-to-all | bytes 1572864 | tf_op jit(solution)/shard_map/all_to_all | solution.py:157
  200.2 0.1 reduce.5
  200.6 43.0 %all_to_all.27 = bf16[8,24,512]{2,1,0:T(8,128)(2,1)S(1)} all-to-all(bf16[8,24,512]{2,1,0:T(8,128)(2,1)S(1)} %copy.114), channel_id=1, replica_groups={{0,32,64,96,128,160,192,224},{8,40,72,104,136,168,200,232},{16,48,80,11..., dimensions={0} | all-to-all | bytes 393216 | tf_op jit(solution)/shard_map/all_to_all | solution.py:162
  243.6 0.8 fusion.8
  (69 shorter events, 1.6 us)
Async XLA Ops:
  0.0 162.8 %copy-start = (bf16[1,144,4096]{2,1,0:T(8,128)(2,1)S(1)}, bf16[1,144,4096]{2,1,0:T(8,128)(2,1)}, u32[]{:S(2)}) copy-start(bf16[1,144,4096]{2,1,0:T(8,128)(2,1)} %param.25) | copy-start | bytes 3538948
  0.0 34.6 %copy-start.5 = (s32[64,2]{0,1:T(2,128)S(1)}, s32[64,2]{0,1:T(2,128)}, u32[]{:S(2)}) copy-start(s32[64,2]{0,1:T(2,128)} %param.21) | copy-start | bytes 1540
  1.1 35.3 %copy-start.4 = (f32[512]{0:T(512)S(1)}, f32[512]{0:T(512)}, u32[]{:S(2)}) copy-start(f32[512]{0:T(512)} %param.20) | copy-start | bytes 6148
  19.9 13.3 %collective-permute-start = (bf16[128,128]{1,0:T(8,128)(2,1)S(1)}, bf16[128,128]{1,0:T(8,128)(2,1)S(1)}, u32[]{:S(2)}, u32[]{:S(2)}) collective-permute-start(bf16[128,128]{1,0:T(8,128)(2,1)S(1)} %get-tuple-element.27), channel_id=1, source_target_pairs={{0,32},{8,40},{16,48},{24,56},{1,33},{9,41},{17,49},{25,57},{2,34}... | collective-permute-start | bytes 98312 | tf_op jit(solution)/shard_map/ppermute | solution.py:105
  33.2 0.7 collective-permute-start.1
  33.9 0.9 collective-permute-start.2
  34.9 0.8 collective-permute-start.3
  35.6 8.8 %copy-start.6 = (f32[64,2]{0,1:T(2,128)S(1)}, f32[64,2]{0,1:T(2,128)}, u32[]{:S(2)}) copy-start(f32[64,2]{0,1:T(2,128)} %param.22) | copy-start | bytes 1540
  35.7 0.7 collective-permute-start.4
  36.5 0.8 collective-permute-start.5
  37.3 1.1 collective-permute-start.6
  38.3 10.7 %copy-start.1 = (bf16[64,512]{1,0:T(8,128)(2,1)S(1)}, bf16[64,512]{1,0:T(8,128)(2,1)}, u32[]{:S(2)}) copy-start(bf16[64,512]{1,0:T(8,128)(2,1)} %param.18) | copy-start | bytes 196612
  38.3 10.7 %copy-start.3 = (f32[512]{0:T(512)S(1)}, f32[512]{0:T(512)}, u32[]{:S(2)}) copy-start(f32[512]{0:T(512)} %param.19) | copy-start | bytes 6148
  39.2 9.9 %copy-start.2 = (bf16[64,512]{1,0:T(8,128)(2,1)S(1)}, bf16[64,512]{1,0:T(8,128)(2,1)}, u32[]{:S(2)}) copy-start(bf16[64,512]{1,0:T(8,128)(2,1)} %param.17) | copy-start | bytes 196612
  39.2 9.7 %all-to-all-start.1 = ((bf16[4,64,128]{2,1,0:T(8,128)(2,1)}), bf16[4,64,128]{2,1,0:T(8,128)(2,1)S(1)}, u32[]{:S(2)}, u32[]{:S(2)}) async-start(bf16[4,64,128]{2,1,0:T(8,128)(2,1)} %bitcast.9), calls=%async_computation.1 | async-start | bytes 131072 | tf_op jit(solution)/shard_map/all_to_all | solution.py:117
  50.0 33.5 %all-to-all-start.2 = ((bf16[8,40,128]{2,1,0:T(8,128)(2,1)}), bf16[8,40,128]{2,1,0:T(8,128)(2,1)S(1)}, u32[]{:S(2)}, u32[]{:S(2)}) async-start(bf16[8,40,128]{2,1,0:T(8,128)(2,1)} %pad_maximum_fusion), calls=%async_computation.2 | async-start | bytes 163840 | tf_op jit(solution)/shard_map/all_to_all | solution.py:132

commit v3 on v2

--- a/solution.py
+++ b/solution.py
@@ -98,12 +98,28 @@
     cum = (within + starts[:, None]).reshape(span)
     faded = (key.astype(F32) * jnp.exp(total - cum)[:, None]).astype(BF16)
     state = lax.dot_general(faded, value, (((0,), (0,)), ((), ())), preferred_element_type=F32)
-    carried = jnp.zeros_like(state)
-    for k in range(far - 1):
-        running = (jnp.exp(total) * carried + state).astype(BF16)
+    my_far = lax.axis_index("seq") // near
+    fade = jnp.exp(total)
+    first = state.astype(BF16)
+    order = sorted(range(1, far), key=lambda g: (g != 1, min(g, far - g), -g))
+    from_first = []
+    for g in order:
+        from_first.append(
+            lax.ppermute(first, "seq", [(i, near * g + i) for i in range(near)])
+        )
+    scales = jnp.exp2(jnp.arange(8, dtype=F32) / 8)[:, None]
+    scales = jnp.broadcast_to(scales, (8, lanes))
+    own = jnp.pad(state, ((0, 8), (0, 0)))
+    opening = jnp.where(my_far <= 1, scales, 0.0)
+    carried = jnp.pad(opening, ((lanes, 0), (0, 0)))
+    for k in range(1, far - 1):
+        running = (fade * carried + own).astype(BF16)
         passed = [(near * k + i, near * (k + 1) + i) for i in range(near)]
-        carried = carried + lax.ppermute(running, "seq", passed).astype(F32)
-    incoming = carried
+        received = lax.ppermute(running, "seq", passed)
+        carried = carried + received.astype(F32)
+    factor = jnp.mean(carried[lanes:] / scales, axis=0)
+    from_first = sum(x.astype(F32) for x in from_first)
+    incoming = carried[:lanes] + factor * from_first
     scores = lax.dot_general(query, key, (((1,), (1,)), ((), ())), preferred_element_type=F32)
     places = jnp.arange(span)
     causal = places[:, None] >= places[None, :]

time: 246 us -> 246 us (level)
  blocking collectives: 168 us -> 125 us
  starting transfers between devices: 49.9 us -> 85.7 us
  waiting for transfers between devices: 8.94 us -> 14.8 us
    ppermute x7 -> x13, starting transfers between devices: 16.3 us -> 61.6 us  [the longest x7 57.6 us: shards(): lax.ppermute(first, 'seq', [(i, near * g + i) for i in range(near)])]
    all_gather x1, blocking collectives: 61.9 us -> 34 us  [shards(): lax.all_gather(normed, 'seq', axis=0, tiled=True, axis_index_groups=far_g...]
    all_to_all x1, starting transfers between devices: 28.6 us -> 10.6 us  [shards(): arrived = lax.all_to_all(payload, ('exp', 'rep'), 0, 0, tiled=True)]
    all_to_all x1 -> x0, blocking collectives: 14.5 us -> none  [shards(): lax.all_to_all(payload, 'seq', 0, 0, tiled=True, axis_index_groups=near_g...]
    all_to_all x0 -> x1, starting transfers between devices: none -> 9.02 us  [shards(): lax.all_to_all(payload, 'seq', 0, 0, tiled=True, axis_index_groups=near_g...]
    all_to_all x0 -> x1, waiting for transfers between devices: none -> 5.16 us  [shards(): lax.all_to_all(payload, 'seq', 0, 0, tiled=True, axis_index_groups=near_g...]
  transfers between devices with their start and end apart: 9 -> 16, of which waited for: 3 -> 4; matrix products, arithmetic and copies ran while one was open for 1% -> 1% of each run, Pallas kernels for 0% -> 0%
where the time goes in v3:
time: 246 us; the launch traced here: 244 us
  blocking collectives  125 us (51%)
  starting transfers between devices  85.7 us (35%)
  waiting for transfers between devices  14.8 us (6%)
  matrix products  6.71 us (3%)
  local copies, waits for them, and re-layouts  5.53 us (2%)
  other arithmetic  5.06 us (2%)
    ppermute x7, starting transfers between devices, shards(): lax.ppermute(first, 'seq', [(i, near * g + i) for i in range(near)])  57.6 us
    all_to_all x1, blocking collectives, shards(): lax.all_to_all(pieces, 'seq', 0, 0, tiled=True, axis_index_groups=far_gro...  42.7 us
    all_gather x1, blocking collectives, shards(): lax.all_gather(normed, 'seq', axis=0, tiled=True, axis_index_groups=far_g...  34 us
    all_to_all x1, blocking collectives, shards(): lax.all_to_all(pieces, ('seq', 'exp', 'rep'), 0, 0, tiled=True, axis_inde...  33.6 us
    all_gather x1, blocking collectives, shards(): lax.all_gather(gathered, 'seq', axis=0, tiled=True, axis_index_groups=nea...  14.6 us
    all_to_all x1, starting transfers between devices, shards(): arrived = lax.all_to_all(payload, ('exp', 'rep'), 0, 0, tiled=True)  10.6 us
    all_to_all x1, starting transfers between devices, shards(): lax.all_to_all(payload, 'seq', 0, 0, tiled=True, axis_index_groups=near_g...  9.02 us
    all_to_all x1, waiting for transfers between devices, shards(): lax.all_to_all(payload, 'seq', 0, 0, tiled=True, axis_index_groups=near_g...  5.16 us
  transfers between devices with their start and end apart: 16, of which 4 were waited for; matrix products, arithmetic and copies ran while one was open for 1% of the time, Pallas kernels for 0%

profile of v3, /device:TPU:33, one launch (start us, length us, event | category | flops | bytes accessed | tf_op | source)
XLA Modules:
  0.0 244.0 jit_solution(7383954005117510512)
XLA Ops:
  0.0 0.9 copy.103
  1.1 0.9 bitcast_bitcast_fusion.2
  2.0 0.9 bitcast_bitcast_fusion
  2.9 0.7 fusion.23
  3.5 9.0 %all-to-all-start = ((bf16[4,200,128]{2,1,0:T(8,128)(2,1)}), bf16[4,200,128]{2,1,0:T(8,128)(2,1)S(1)}, u32[]{:S(2)}, u32[]{:S(2)}) async-start(bf16[4,200,128]{2,1,0:T(8,128)(2,1)} %fusion.23), calls=%async_computation | async-start | bytes 409600 | tf_op jit(solution)/shard_map/all_to_all | solution.py:89
  12.6 5.2 %all-to-all-done = bf16[4,200,128]{2,1,0:T(8,128)(2,1)S(1)} async-done(((bf16[4,200,128]{2,1,0:T(8,128)(2,1)}), bf16[4,200,128]{2,1,0:T(8,128)(2,1)S(1)}, u32[]{:S(2)}, u32[]{:S(2)}) %all-to-all-start) | async-done | bytes 204832 | tf_op jit(solution)/shard_map/all_to_all | solution.py:89
  17.9 0.7 slice_reduce_fusion
  19.2 0.7 subtract_exponential_fusion
  20.0 0.3 fusion.72
  20.3 0.7 collective-permute-start
  21.1 0.7 collective-permute-start.1
  22.1 0.7 collective-permute-start.2
  23.0 0.7 collective-permute-start.3
  23.8 0.7 collective-permute-start.4
  24.6 49.6 %collective-permute-start.12 = (bf16[128,128]{1,0:T(8,128)(2,1)S(1)}, bf16[128,128]{1,0:T(8,128)(2,1)S(1)}, u32[]{:S(2)}, u32[]{:S(2)}) collective-permute-start(bf16[128,128]{1,0:T(8,128)(2,1)S(1)} %get-tuple-element.27), channel_id=1, source_target_pairs={{0,128},{8,136},{16,144},{24,152},{1,129},{9,137},{17,145},{25,153... | collective-permute-start | bytes 98312 | tf_op jit(solution)/shard_map/ppermute | solution.py:108
  74.2 1.3 collective-permute-start.11
  75.5 1.5 collective-permute-start.10
  77.0 1.3 collective-permute-start.9
  78.4 0.7 collective-permute-start.5
  79.2 1.3 collective-permute-start.8
  80.7 1.3 collective-permute-start.7
  82.1 1.3 collective-permute-start.6
  83.4 1.8 collective-permute-done.7
  85.2 0.2 fusion.38
  85.4 1.0 fusion.8
  86.4 4.5 %all-to-all-start.1 = ((bf16[4,64,128]{2,1,0:T(8,128)(2,1)}), bf16[4,64,128]{2,1,0:T(8,128)(2,1)S(1)}, u32[]{:S(2)}, u32[]{:S(2)}) async-start(bf16[4,64,128]{2,1,0:T(8,128)(2,1)} %bitcast.9), calls=%async_computation.1 | async-start | bytes 131072 | tf_op jit(solution)/shard_map/all_to_all | solution.py:133
  91.1 0.2 reduce_window_sum.31
  91.4 0.2 eq.51
  91.5 0.2 eq.52
  91.7 0.2 mul.147
  91.9 0.2 mul.148
  92.1 0.2 fusion.59
  92.4 3.1 %all-to-all-done.1 = bf16[4,64,128]{2,1,0:T(8,128)(2,1)S(1)} async-done(((bf16[4,64,128]{2,1,0:T(8,128)(2,1)}), bf16[4,64,128]{2,1,0:T(8,128)(2,1)S(1)}, u32[]{:S(2)}, u32[]{:S(2)}) %all-to-all-start.1) | async-done | bytes 65568 | tf_op jit(solution)/shard_map/all_to_all | solution.py:133
  95.7 0.2 convolution_convert_fusion.1
  95.9 0.6 pad_maximum_fusion
  96.6 10.6 %all-to-all-start.2 = ((bf16[8,40,128]{2,1,0:T(8,128)(2,1)}), bf16[8,40,128]{2,1,0:T(8,128)(2,1)S(1)}, u32[]{:S(2)}, u32[]{:S(2)}) async-start(bf16[8,40,128]{2,1,0:T(8,128)(2,1)} %pad_maximum_fusion), calls=%async_computation.2 | async-start | bytes 163840 | tf_op jit(solution)/shard_map/all_to_all | solution.py:148
  107.3 4.8 %all-to-all-done.2 = bf16[8,40,128]{2,1,0:T(8,128)(2,1)S(1)} async-done(((bf16[8,40,128]{2,1,0:T(8,128)(2,1)}), bf16[8,40,128]{2,1,0:T(8,128)(2,1)S(1)}, u32[]{:S(2)}, u32[]{:S(2)}) %all-to-all-start.2) | async-done | bytes 81952 | tf_op jit(solution)/shard_map/all_to_all | solution.py:148
  112.5 0.2 multiply_reduce_fusion.1
  112.8 34.0 %all_gather.6 = bf16[768,128]{1,0:T(8,128)(2,1)S(1)} all-gather(bf16[96,128]{1,0:T(8,128)(2,1)S(1)} %reshape.259), channel_id=1, replica_groups={{0,32,64,96,128,160,192,224},{8,40,72,104,136,168,200,232},{16,48,80,11..., dimensions={0}, use_global_device_ids=true | all-gather | bytes 221184 | tf_op jit(solution)/shard_map/all_gather | solution.py:164
  146.8 14.6 %all_gather.7 = bf16[3072,128]{1,0:T(8,128)(2,1)S(1)} all-gather(bf16[768,128]{1,0:T(8,128)(2,1)S(1)} %all_gather.6), channel_id=1, replica_groups={{0,8,16,24},{32,40,48,56},{64,72,80,88},{96,104,112,120},{128,136,144,1..., dimensions={0}, use_global_device_ids=true | all-gather | bytes 983040 | tf_op jit(solution)/shard_map/all_gather | solution.py:165
  161.4 0.3 reshape.260
  161.8 1.7 fusion.3
  163.5 2.5 %convolution_convert_fusion = bf16[96,4096]{1,0:T(8,128)(2,1)S(1)} fusion(bf16[1,144,4096]{2,1,0:T(8,128)(2,1)S(1)} %copy-done, bf16[96,4096]{1,0:T(8,128)(2,1)S(1)} %reshape.260, bf16[1,144,4096]{2,1,0:T(8,128)(2,1)} %param.24, f32[96,144]{0,1:T(8,128)S(1)} %fusion.3), kind=kOutput, calls=%fused_computation | convolution fusion | flops 226968576 | bytes 3987456 | tf_op jit(solution)/shard_map/dot_general | solution.py:170
  166.0 0.3 copy.122
  166.3 0.2 copy.111
  166.5 33.6 %all_to_all.25 = bf16[32,24,512]{2,1,0:T(8,128)(2,1)S(1)} all-to-all(bf16[32,24,512]{2,1,0:T(8,128)(2,1)S(1)} %bitcast.107), channel_id=1, replica_groups={{0,1,2,3,4,5,6,7,8,9,10,11,12,13,14,15,16,17,18,19,20,21,22,23,24,25,26..., dimensions={0} | all-to-all | bytes 1572864 | tf_op jit(solution)/shard_map/all_to_all | solution.py:173
  200.5 42.7 %all_to_all.26 = bf16[8,24,512]{2,1,0:T(8,128)(2,1)S(1)} all-to-all(bf16[8,24,512]{2,1,0:T(8,128)(2,1)S(1)} %copy.114), channel_id=1, replica_groups={{0,32,64,96,128,160,192,224},{8,40,72,104,136,168,200,232},{16,48,80,11..., dimensions={0} | all-to-all | bytes 393216 | tf_op jit(solution)/shard_map/all_to_all | solution.py:178
  243.2 0.8 fusion.9
  (88 shorter events, 3.1 us)
Async XLA Ops:
  0.0 163.5 %copy-start = (bf16[1,144,4096]{2,1,0:T(8,128)(2,1)S(1)}, bf16[1,144,4096]{2,1,0:T(8,128)(2,1)}, u32[]{:S(2)}) copy-start(bf16[1,144,4096]{2,1,0:T(8,128)(2,1)} %param.25) | copy-start | bytes 3538948
  0.0 21.8 %copy-start.5 = (s32[64,2]{0,1:T(2,128)S(1)}, s32[64,2]{0,1:T(2,128)}, u32[]{:S(2)}) copy-start(s32[64,2]{0,1:T(2,128)} %param.21) | copy-start | bytes 1540
  1.0 22.7 %copy-start.4 = (f32[512]{0:T(512)S(1)}, f32[512]{0:T(512)}, u32[]{:S(2)}) copy-start(f32[512]{0:T(512)} %param.20) | copy-start | bytes 6148
  3.5 14.2 %all-to-all-start = ((bf16[4,200,128]{2,1,0:T(8,128)(2,1)}), bf16[4,200,128]{2,1,0:T(8,128)(2,1)S(1)}, u32[]{:S(2)}, u32[]{:S(2)}) async-start(bf16[4,200,128]{2,1,0:T(8,128)(2,1)} %fusion.23), calls=%async_computation | async-start | bytes 409600 | tf_op jit(solution)/shard_map/all_to_all | solution.py:89
  20.3 0.7 collective-permute-start
  21.1 0.9 collective-permute-start.1
  22.1 0.8 collective-permute-start.2
  23.0 0.7 collective-permute-start.3
  23.8 54.5 %collective-permute-start.4 = (bf16[136,128]{1,0:T(8,128)(2,1)S(1)}, bf16[136,128]{1,0:T(8,128)(2,1)S(1)}, u32[]{:S(2)}, u32[]{:S(2)}) collective-permute-start(bf16[136,128]{1,0:T(8,128)(2,1)S(1)} %add_convert_fusion.1), channel_id=1, source_target_pairs={{160,192},{168,200},{176,208},{184,216},{161,193},{169,201},{177,2... | collective-permute-start | bytes 104456 | tf_op jit(solution)/shard_map/ppermute | solution.py:118
  24.5 66.5 %copy-start.6 = (f32[64,2]{0,1:T(2,128)S(1)}, f32[64,2]{0,1:T(2,128)}, u32[]{:S(2)}) copy-start(f32[64,2]{0,1:T(2,128)} %param.22) | copy-start | bytes 1540
  24.6 56.2 %collective-permute-start.12 = (bf16[128,128]{1,0:T(8,128)(2,1)S(1)}, bf16[128,128]{1,0:T(8,128)(2,1)S(1)}, u32[]{:S(2)}, u32[]{:S(2)}) collective-permute-start(bf16[128,128]{1,0:T(8,128)(2,1)S(1)} %get-tuple-element.27), channel_id=1, source_target_pairs={{0,128},{8,136},{16,144},{24,152},{1,129},{9,137},{17,145},{25,153... | collective-permute-start | bytes 98312 | tf_op jit(solution)/shard_map/ppermute | solution.py:108
  74.2 7.9 %collective-permute-start.11 = (bf16[128,128]{1,0:T(8,128)(2,1)S(1)}, bf16[128,128]{1,0:T(8,128)(2,1)S(1)}, u32[]{:S(2)}, u32[]{:S(2)}) collective-permute-start(bf16[128,128]{1,0:T(8,128)(2,1)S(1)} %get-tuple-element.27), channel_id=1, source_target_pairs={{0,96},{8,104},{16,112},{24,120},{1,97},{9,105},{17,113},{25,121},... | collective-permute-start | bytes 98312 | tf_op jit(solution)/shard_map/ppermute | solution.py:108
  75.5 7.9 %collective-permute-start.10 = (bf16[128,128]{1,0:T(8,128)(2,1)S(1)}, bf16[128,128]{1,0:T(8,128)(2,1)S(1)}, u32[]{:S(2)}, u32[]{:S(2)}) collective-permute-start(bf16[128,128]{1,0:T(8,128)(2,1)S(1)} %get-tuple-element.27), channel_id=1, source_target_pairs={{0,160},{8,168},{16,176},{24,184},{1,161},{9,169},{17,177},{25,185... | collective-permute-start | bytes 98312 | tf_op jit(solution)/shard_map/ppermute | solution.py:108
  77.0 6.4 %collective-permute-start.9 = (bf16[128,128]{1,0:T(8,128)(2,1)S(1)}, bf16[128,128]{1,0:T(8,128)(2,1)S(1)}, u32[]{:S(2)}, u32[]{:S(2)}) collective-permute-start(bf16[128,128]{1,0:T(8,128)(2,1)S(1)} %get-tuple-element.27), channel_id=1, source_target_pairs={{0,64},{8,72},{16,80},{24,88},{1,65},{9,73},{17,81},{25,89},{2,66}... | collective-permute-start | bytes 98312 | tf_op jit(solution)/shard_map/ppermute | solution.py:108
  78.4 0.8 collective-permute-start.5
  79.2 4.2 %collective-permute-start.8 = (bf16[128,128]{1,0:T(8,128)(2,1)S(1)}, bf16[128,128]{1,0:T(8,128)(2,1)S(1)}, u32[]{:S(2)}, u32[]{:S(2)}) collective-permute-start(bf16[128,128]{1,0:T(8,128)(2,1)S(1)} %get-tuple-element.27), channel_id=1, source_target_pairs={{0,192},{8,200},{16,208},{24,216},{1,193},{9,201},{17,209},{25,217... | collective-permute-start | bytes 98312 | tf_op jit(solution)/shard_map/ppermute | solution.py:108
  80.7 4.4 %collective-permute-start.7 = (bf16[128,128]{1,0:T(8,128)(2,1)S(1)}, bf16[128,128]{1,0:T(8,128)(2,1)S(1)}, u32[]{:S(2)}, u32[]{:S(2)}) collective-permute-start(bf16[128,128]{1,0:T(8,128)(2,1)S(1)} %get-tuple-element.27), channel_id=1, source_target_pairs={{0,224},{8,232},{16,240},{24,248},{1,225},{9,233},{17,241},{25,249... | collective-permute-start | bytes 98312 | tf_op jit(solution)/shard_map/ppermute | solution.py:108
  82.1 3.1 %collective-permute-start.6 = (bf16[128,128]{1,0:T(8,128)(2,1)S(1)}, bf16[128,128]{1,0:T(8,128)(2,1)S(1)}, u32[]{:S(2)}, u32[]{:S(2)}) collective-permute-start(bf16[128,128]{1,0:T(8,128)(2,1)S(1)} %get-tuple-element.27), channel_id=1, source_target_pairs={{0,32},{8,40},{16,48},{24,56},{1,33},{9,41},{17,49},{25,57},{2,34}... | collective-permute-start | bytes 98312 | tf_op jit(solution)/shard_map/ppermute | solution.py:108
  86.4 9.2 %copy-start.1 = (bf16[64,512]{1,0:T(8,128)(2,1)S(1)}, bf16[64,512]{1,0:T(8,128)(2,1)}, u32[]{:S(2)}) copy-start(bf16[64,512]{1,0:T(8,128)(2,1)} %param.18) | copy-start | bytes 196612
  86.4 9.2 %copy-start.3 = (f32[512]{0:T(512)S(1)}, f32[512]{0:T(512)}, u32[]{:S(2)}) copy-start(f32[512]{0:T(512)} %param.19) | copy-start | bytes 6148
  86.4 9.3 %copy-start.2 = (bf16[64,512]{1,0:T(8,128)(2,1)S(1)}, bf16[64,512]{1,0:T(8,128)(2,1)}, u32[]{:S(2)}) copy-start(bf16[64,512]{1,0:T(8,128)(2,1)} %param.17) | copy-start | bytes 196612
  86.4 9.1 %all-to-all-start.1 = ((bf16[4,64,128]{2,1,0:T(8,128)(2,1)}), bf16[4,64,128]{2,1,0:T(8,128)(2,1)S(1)}, u32[]{:S(2)}, u32[]{:S(2)}) async-start(bf16[4,64,128]{2,1,0:T(8,128)(2,1)} %bitcast.9), calls=%async_computation.1 | async-start | bytes 131072 | tf_op jit(solution)/shard_map/all_to_all | solution.py:133
  96.6 15.5 %all-to-all-start.2 = ((bf16[8,40,128]{2,1,0:T(8,128)(2,1)}), bf16[8,40,128]{2,1,0:T(8,128)(2,1)S(1)}, u32[]{:S(2)}, u32[]{:S(2)}) async-start(bf16[8,40,128]{2,1,0:T(8,128)(2,1)} %pad_maximum_fusion), calls=%async_computation.2 | async-start | bytes 163840 | tf_op jit(solution)/shard_map/all_to_all | solution.py:148

commit v4 on v3

--- a/solution.py
+++ b/solution.py
@@ -126,9 +126,10 @@
     decays = jnp.where(causal, jnp.exp(jnp.where(causal, cum[:, None] - cum[None, :], 0.0)), 0.0)
     mixing = (scores * decays).astype(BF16)
     lifted = (query.astype(F32) * jnp.exp(cum)[:, None]).astype(BF16)
-    attended = jnp.dot(mixing, value, preferred_element_type=F32) + jnp.dot(
-        lifted, incoming.astype(BF16), preferred_element_type=F32
-    )
+    local_part = lax.optimization_barrier(
+        jnp.dot(mixing, value, preferred_element_type=F32)
+    )
+    attended = local_part + jnp.dot(lifted, incoming.astype(BF16), preferred_element_type=F32)
     attended = attended.astype(BF16).reshape(near, tokens, lanes)
     attended = lax.all_to_all(attended, "seq", 0, 0, tiled=True, axis_index_groups=near_groups)
     attended = jnp.swapaxes(attended, 0, 1).reshape(tokens, columns).astype(F32)

time: 246 us -> 246 us (level)
  no operation moved by 1% of the time
where the time goes in v4:
time: 246 us; the launch traced here: 244 us
  blocking collectives  125 us (51%)
  starting transfers between devices  86.6 us (35%)
  waiting for transfers between devices  14 us (6%)
  matrix products  6.71 us (3%)
  local copies, waits for them, and re-layouts  5.52 us (2%)
  other arithmetic  5.06 us (2%)
    ppermute x7, starting transfers between devices, shards(): lax.ppermute(first, 'seq', [(i, near * g + i) for i in range(near)])  57.4 us
    all_to_all x1, blocking collectives, shards(): lax.all_to_all(pieces, 'seq', 0, 0, tiled=True, axis_index_groups=far_gro...  42.4 us
    all_gather x1, blocking collectives, shards(): lax.all_gather(normed, 'seq', axis=0, tiled=True, axis_index_groups=far_g...  34 us
    all_to_all x1, blocking collectives, shards(): lax.all_to_all(pieces, ('seq', 'exp', 'rep'), 0, 0, tiled=True, axis_inde...  33.2 us
    all_gather x1, blocking collectives, shards(): lax.all_gather(gathered, 'seq', axis=0, tiled=True, axis_index_groups=nea...  15.3 us
    all_to_all x1, starting transfers between devices, shards(): arrived = lax.all_to_all(payload, ('exp', 'rep'), 0, 0, tiled=True)  11.3 us
    all_to_all x1, starting transfers between devices, shards(): lax.all_to_all(payload, 'seq', 0, 0, tiled=True, axis_index_groups=near_g...  9.02 us
    all_to_all x1, waiting for transfers between devices, shards(): lax.all_to_all(payload, 'seq', 0, 0, tiled=True, axis_index_groups=near_g...  5.16 us
  transfers between devices with their start and end apart: 16, of which 4 were waited for; matrix products, arithmetic and copies ran while one was open for 1% of the time, Pallas kernels for 0%

profile of v4, /device:TPU:33, one launch (start us, length us, event | category | flops | bytes accessed | tf_op | source)
XLA Modules:
  0.0 244.0 jit_solution(851071730768098889)
XLA Ops:
  0.0 0.9 copy.103
  1.1 0.9 bitcast_bitcast_fusion.2
  1.9 0.9 bitcast_bitcast_fusion
  2.8 0.7 fusion.22
  3.5 9.0 %all-to-all-start = ((bf16[4,200,128]{2,1,0:T(8,128)(2,1)}), bf16[4,200,128]{2,1,0:T(8,128)(2,1)S(1)}, u32[]{:S(2)}, u32[]{:S(2)}) async-start(bf16[4,200,128]{2,1,0:T(8,128)(2,1)} %fusion.22), calls=%async_computation | async-start | bytes 409600 | tf_op jit(solution)/shard_map/all_to_all | solution.py:89
  12.6 5.2 %all-to-all-done = bf16[4,200,128]{2,1,0:T(8,128)(2,1)S(1)} async-done(((bf16[4,200,128]{2,1,0:T(8,128)(2,1)}), bf16[4,200,128]{2,1,0:T(8,128)(2,1)S(1)}, u32[]{:S(2)}, u32[]{:S(2)}) %all-to-all-start) | async-done | bytes 204832 | tf_op jit(solution)/shard_map/all_to_all | solution.py:89
  17.9 0.7 slice_reduce_fusion
  19.2 0.7 subtract_exponential_fusion
  19.9 0.3 fusion.70
  20.3 0.7 collective-permute-start
  21.4 0.7 collective-permute-start.1
  22.2 0.7 collective-permute-start.2
  23.0 0.7 collective-permute-start.3
  23.7 48.5 %collective-permute-start.12 = (bf16[128,128]{1,0:T(8,128)(2,1)S(1)}, bf16[128,128]{1,0:T(8,128)(2,1)S(1)}, u32[]{:S(2)}, u32[]{:S(2)}) collective-permute-start(bf16[128,128]{1,0:T(8,128)(2,1)S(1)} %get-tuple-element.27), channel_id=1, source_target_pairs={{0,128},{8,136},{16,144},{24,152},{1,129},{9,137},{17,145},{25,153... | collective-permute-start | bytes 98312 | tf_op jit(solution)/shard_map/ppermute | solution.py:108
  72.2 1.3 collective-permute-start.11
  73.6 1.3 collective-permute-start.10
  74.9 1.3 collective-permute-start.9
  76.3 0.7 collective-permute-start.4
  77.2 0.7 collective-permute-start.5
  77.9 0.3 fusion.6
  78.2 1.7 collective-permute-start.8
  80.2 1.9 collective-permute-start.7
  82.1 1.3 collective-permute-start.6
  83.5 1.0 collective-permute-done.6
  84.4 0.9 fusion.7
  85.3 4.9 %all-to-all-start.1 = ((bf16[4,64,128]{2,1,0:T(8,128)(2,1)}), bf16[4,64,128]{2,1,0:T(8,128)(2,1)S(1)}, u32[]{:S(2)}, u32[]{:S(2)}) async-start(bf16[4,64,128]{2,1,0:T(8,128)(2,1)} %bitcast.9), calls=%async_computation.1 | async-start | bytes 131072 | tf_op jit(solution)/shard_map/all_to_all | solution.py:134
  90.5 0.2 reduce_window_sum.31
  90.7 0.2 eq.51
  90.9 0.2 eq.52
  91.1 0.2 mul.147
  91.3 0.2 mul.148
  91.5 0.2 fusion.57
  91.7 3.1 %all-to-all-done.1 = bf16[4,64,128]{2,1,0:T(8,128)(2,1)S(1)} async-done(((bf16[4,64,128]{2,1,0:T(8,128)(2,1)}), bf16[4,64,128]{2,1,0:T(8,128)(2,1)S(1)}, u32[]{:S(2)}, u32[]{:S(2)}) %all-to-all-start.1) | async-done | bytes 65568 | tf_op jit(solution)/shard_map/all_to_all | solution.py:134
  95.0 0.2 convolution_convert_fusion.1
  95.3 0.6 pad_maximum_fusion
  95.9 11.3 %all-to-all-start.2 = ((bf16[8,40,128]{2,1,0:T(8,128)(2,1)}), bf16[8,40,128]{2,1,0:T(8,128)(2,1)S(1)}, u32[]{:S(2)}, u32[]{:S(2)}) async-start(bf16[8,40,128]{2,1,0:T(8,128)(2,1)} %pad_maximum_fusion), calls=%async_computation.2 | async-start | bytes 163840 | tf_op jit(solution)/shard_map/all_to_all | solution.py:149
  107.3 4.8 %all-to-all-done.2 = bf16[8,40,128]{2,1,0:T(8,128)(2,1)S(1)} async-done(((bf16[8,40,128]{2,1,0:T(8,128)(2,1)}), bf16[8,40,128]{2,1,0:T(8,128)(2,1)S(1)}, u32[]{:S(2)}, u32[]{:S(2)}) %all-to-all-start.2) | async-done | bytes 81952 | tf_op jit(solution)/shard_map/all_to_all | solution.py:149
  112.5 0.2 multiply_reduce_fusion.1
  112.8 34.0 %all_gather.6 = bf16[768,128]{1,0:T(8,128)(2,1)S(1)} all-gather(bf16[96,128]{1,0:T(8,128)(2,1)S(1)} %reshape.259), channel_id=1, replica_groups={{0,32,64,96,128,160,192,224},{8,40,72,104,136,168,200,232},{16,48,80,11..., dimensions={0}, use_global_device_ids=true | all-gather | bytes 221184 | tf_op jit(solution)/shard_map/all_gather | solution.py:165
  146.8 15.3 %all_gather.7 = bf16[3072,128]{1,0:T(8,128)(2,1)S(1)} all-gather(bf16[768,128]{1,0:T(8,128)(2,1)S(1)} %all_gather.6), channel_id=1, replica_groups={{0,8,16,24},{32,40,48,56},{64,72,80,88},{96,104,112,120},{128,136,144,1..., dimensions={0}, use_global_device_ids=true | all-gather | bytes 983040 | tf_op jit(solution)/shard_map/all_gather | solution.py:166
  162.1 0.3 reshape.260
  162.4 1.7 fusion.3
  164.2 2.5 %convolution_convert_fusion = bf16[96,4096]{1,0:T(8,128)(2,1)S(1)} fusion(bf16[1,144,4096]{2,1,0:T(8,128)(2,1)S(1)} %copy-done, bf16[96,4096]{1,0:T(8,128)(2,1)S(1)} %reshape.260, bf16[1,144,4096]{2,1,0:T(8,128)(2,1)} %param.24, f32[96,144]{0,1:T(8,128)S(1)} %fusion.3), kind=kOutput, calls=%fused_computation | convolution fusion | flops 226968576 | bytes 3987456 | tf_op jit(solution)/shard_map/dot_general | solution.py:171
  166.7 0.3 copy.122
  167.0 0.2 copy.111
  167.2 33.2 %all_to_all.25 = bf16[32,24,512]{2,1,0:T(8,128)(2,1)S(1)} all-to-all(bf16[32,24,512]{2,1,0:T(8,128)(2,1)S(1)} %bitcast.107), channel_id=1, replica_groups={{0,1,2,3,4,5,6,7,8,9,10,11,12,13,14,15,16,17,18,19,20,21,22,23,24,25,26..., dimensions={0} | all-to-all | bytes 1572864 | tf_op jit(solution)/shard_map/all_to_all | solution.py:174
  200.7 42.4 %all_to_all.26 = bf16[8,24,512]{2,1,0:T(8,128)(2,1)S(1)} all-to-all(bf16[8,24,512]{2,1,0:T(8,128)(2,1)S(1)} %copy.114), channel_id=1, replica_groups={{0,32,64,96,128,160,192,224},{8,40,72,104,136,168,200,232},{16,48,80,11..., dimensions={0} | all-to-all | bytes 393216 | tf_op jit(solution)/shard_map/all_to_all | solution.py:179
  243.2 0.8 fusion.8
  (88 shorter events, 3.1 us)
Async XLA Ops:
  0.0 164.2 %copy-start = (bf16[1,144,4096]{2,1,0:T(8,128)(2,1)S(1)}, bf16[1,144,4096]{2,1,0:T(8,128)(2,1)}, u32[]{:S(2)}) copy-start(bf16[1,144,4096]{2,1,0:T(8,128)(2,1)} %param.25) | copy-start | bytes 3538948
  0.0 21.0 %copy-start.5 = (s32[64,2]{0,1:T(2,128)S(1)}, s32[64,2]{0,1:T(2,128)}, u32[]{:S(2)}) copy-start(s32[64,2]{0,1:T(2,128)} %param.21) | copy-start | bytes 1540
  0.0 22.9 %copy-start.4 = (f32[512]{0:T(512)S(1)}, f32[512]{0:T(512)}, u32[]{:S(2)}) copy-start(f32[512]{0:T(512)} %param.20) | copy-start | bytes 6148
  3.5 14.2 %all-to-all-start = ((bf16[4,200,128]{2,1,0:T(8,128)(2,1)}), bf16[4,200,128]{2,1,0:T(8,128)(2,1)S(1)}, u32[]{:S(2)}, u32[]{:S(2)}) async-start(bf16[4,200,128]{2,1,0:T(8,128)(2,1)} %fusion.22), calls=%async_computation | async-start | bytes 409600 | tf_op jit(solution)/shard_map/all_to_all | solution.py:89
  20.3 0.9 collective-permute-start
  21.4 0.8 collective-permute-start.1
  22.2 0.7 collective-permute-start.2
  23.0 53.2 %collective-permute-start.3 = (bf16[136,128]{1,0:T(8,128)(2,1)S(1)}, bf16[136,128]{1,0:T(8,128)(2,1)S(1)}, u32[]{:S(2)}, u32[]{:S(2)}) collective-permute-start(bf16[136,128]{1,0:T(8,128)(2,1)S(1)} %add_convert_fusion.2), channel_id=1, source_target_pairs={{128,160},{136,168},{144,176},{152,184},{129,161},{137,169},{145,1... | collective-permute-start | bytes 104456 | tf_op jit(solution)/shard_map/ppermute | solution.py:118
  23.7 56.4 %collective-permute-start.12 = (bf16[128,128]{1,0:T(8,128)(2,1)S(1)}, bf16[128,128]{1,0:T(8,128)(2,1)S(1)}, u32[]{:S(2)}, u32[]{:S(2)}) collective-permute-start(bf16[128,128]{1,0:T(8,128)(2,1)S(1)} %get-tuple-element.27), channel_id=1, source_target_pairs={{0,128},{8,136},{16,144},{24,152},{1,129},{9,137},{17,145},{25,153... | collective-permute-start | bytes 98312 | tf_op jit(solution)/shard_map/ppermute | solution.py:108
  72.2 9.9 %collective-permute-start.11 = (bf16[128,128]{1,0:T(8,128)(2,1)S(1)}, bf16[128,128]{1,0:T(8,128)(2,1)S(1)}, u32[]{:S(2)}, u32[]{:S(2)}) collective-permute-start(bf16[128,128]{1,0:T(8,128)(2,1)S(1)} %get-tuple-element.27), channel_id=1, source_target_pairs={{0,96},{8,104},{16,112},{24,120},{1,97},{9,105},{17,113},{25,121},... | collective-permute-start | bytes 98312 | tf_op jit(solution)/shard_map/ppermute | solution.py:108
  73.6 9.9 %collective-permute-start.10 = (bf16[128,128]{1,0:T(8,128)(2,1)S(1)}, bf16[128,128]{1,0:T(8,128)(2,1)S(1)}, u32[]{:S(2)}, u32[]{:S(2)}) collective-permute-start(bf16[128,128]{1,0:T(8,128)(2,1)S(1)} %get-tuple-element.27), channel_id=1, source_target_pairs={{0,160},{8,168},{16,176},{24,184},{1,161},{9,169},{17,177},{25,185... | collective-permute-start | bytes 98312 | tf_op jit(solution)/shard_map/ppermute | solution.py:108
  74.9 8.6 %collective-permute-start.9 = (bf16[128,128]{1,0:T(8,128)(2,1)S(1)}, bf16[128,128]{1,0:T(8,128)(2,1)S(1)}, u32[]{:S(2)}, u32[]{:S(2)}) collective-permute-start(bf16[128,128]{1,0:T(8,128)(2,1)S(1)} %get-tuple-element.27), channel_id=1, source_target_pairs={{0,64},{8,72},{16,80},{24,88},{1,65},{9,73},{17,81},{25,89},{2,66}... | collective-permute-start | bytes 98312 | tf_op jit(solution)/shard_map/ppermute | solution.py:108
  76.3 14.1 %copy-start.6 = (f32[64,2]{0,1:T(2,128)S(1)}, f32[64,2]{0,1:T(2,128)}, u32[]{:S(2)}) copy-start(f32[64,2]{0,1:T(2,128)} %param.22) | copy-start | bytes 1540
  76.3 0.8 collective-permute-start.4
  77.2 1.0 collective-permute-start.5
  78.2 5.2 %collective-permute-start.8 = (bf16[128,128]{1,0:T(8,128)(2,1)S(1)}, bf16[128,128]{1,0:T(8,128)(2,1)S(1)}, u32[]{:S(2)}, u32[]{:S(2)}) collective-permute-start(bf16[128,128]{1,0:T(8,128)(2,1)S(1)} %get-tuple-element.27), channel_id=1, source_target_pairs={{0,192},{8,200},{16,208},{24,216},{1,193},{9,201},{17,209},{25,217... | collective-permute-start | bytes 98312 | tf_op jit(solution)/shard_map/ppermute | solution.py:108
  80.2 3.3 %collective-permute-start.7 = (bf16[128,128]{1,0:T(8,128)(2,1)S(1)}, bf16[128,128]{1,0:T(8,128)(2,1)S(1)}, u32[]{:S(2)}, u32[]{:S(2)}) collective-permute-start(bf16[128,128]{1,0:T(8,128)(2,1)S(1)} %get-tuple-element.27), channel_id=1, source_target_pairs={{0,224},{8,232},{16,240},{24,248},{1,225},{9,233},{17,241},{25,249... | collective-permute-start | bytes 98312 | tf_op jit(solution)/shard_map/ppermute | solution.py:108
  82.1 2.3 collective-permute-start.6
  85.3 9.7 %copy-start.1 = (bf16[64,512]{1,0:T(8,128)(2,1)S(1)}, bf16[64,512]{1,0:T(8,128)(2,1)}, u32[]{:S(2)}) copy-start(bf16[64,512]{1,0:T(8,128)(2,1)} %param.18) | copy-start | bytes 196612
  85.3 9.7 %copy-start.3 = (f32[512]{0:T(512)S(1)}, f32[512]{0:T(512)}, u32[]{:S(2)}) copy-start(f32[512]{0:T(512)} %param.19) | copy-start | bytes 6148
  85.3 9.7 %copy-start.2 = (bf16[64,512]{1,0:T(8,128)(2,1)S(1)}, bf16[64,512]{1,0:T(8,128)(2,1)}, u32[]{:S(2)}) copy-start(bf16[64,512]{1,0:T(8,128)(2,1)} %param.17) | copy-start | bytes 196612
  85.3 9.5 %all-to-all-start.1 = ((bf16[4,64,128]{2,1,0:T(8,128)(2,1)}), bf16[4,64,128]{2,1,0:T(8,128)(2,1)S(1)}, u32[]{:S(2)}, u32[]{:S(2)}) async-start(bf16[4,64,128]{2,1,0:T(8,128)(2,1)} %bitcast.9), calls=%async_computation.1 | async-start | bytes 131072 | tf_op jit(solution)/shard_map/all_to_all | solution.py:134
  95.9 16.2 %all-to-all-start.2 = ((bf16[8,40,128]{2,1,0:T(8,128)(2,1)}), bf16[8,40,128]{2,1,0:T(8,128)(2,1)S(1)}, u32[]{:S(2)}, u32[]{:S(2)}) async-start(bf16[8,40,128]{2,1,0:T(8,128)(2,1)} %pad_maximum_fusion), calls=%async_computation.2 | async-start | bytes 163840 | tf_op jit(solution)/shard_map/all_to_all | solution.py:149

commit v5 on v4

--- a/solution.py
+++ b/solution.py
@@ -1,6 +1,10 @@
+from functools import partial
+
 import jax
 import jax.numpy as jnp
 from jax import lax
+from jax.experimental import pallas as pl
+from jax.experimental.pallas import tpu as pltpu
 from jax.sharding import PartitionSpec as P
 
 CAP = 6
@@ -40,10 +44,101 @@
     return jnp.pad(x, [(0, 0)] * (x.ndim - 2) + [(0, rows - x.shape[-2]), (0, 0)])
 
 
-def project_rows(slot_rows, weight_rows):
-    return lax.dot_general(
-        slot_rows, weight_rows, (((1,), (1,)), ((), ())), preferred_element_type=jnp.float32
-    )
+def rounded(x):
+    return x.astype(BF16).astype(F32)
+
+
+def payload_body(
+    query_hbm, key_hbm, value_hbm, decay_hbm, out_ref, query_ref, key_ref, value_ref, decay_ref, arrivals
+):
+    fetches = [
+        pltpu.make_async_copy(source, target, arrivals.at[i])
+        for i, (source, target) in enumerate(
+            [
+                (decay_hbm, decay_ref),
+                (query_hbm, query_ref),
+                (key_hbm, key_ref),
+                (value_hbm, value_ref),
+            ]
+        )
+    ]
+    for fetch in fetches:
+        fetch.start()
+    tokens, columns = query_ref.shape
+    heads = out_ref.shape[0]
+    lanes = columns // heads
+    row = lax.broadcasted_iota(jnp.int32, (tokens, lanes), 0)
+    col = lax.broadcasted_iota(jnp.int32, (tokens, lanes), 1)
+    upto = jnp.where((row <= col) & (col < tokens), 1.0, 0.0)
+    fetches[0].wait()
+    cumulative = jnp.dot(
+        decay_ref[...], upto, precision=lax.Precision.HIGHEST, preferred_element_type=F32
+    )
+    high = rounded(cumulative)
+    middle = rounded(cumulative - high)
+    low = cumulative - high - middle
+    place = lax.broadcasted_iota(jnp.int32, (8, lanes), 0)
+    for fetch in fetches[1:]:
+        fetch.wait()
+    for h in range(heads):
+        here = slice(h * lanes, (h + 1) * lanes)
+        out_ref[h, :tokens] = query_ref[:, here]
+        out_ref[h, tokens : 2 * tokens] = key_ref[:, here]
+        out_ref[h, 2 * tokens : 3 * tokens] = value_ref[:, here]
+        tail = jnp.where(place == 0, high[h : h + 1], 0.0)
+        tail = jnp.where(place == 1, middle[h : h + 1], tail)
+        tail = jnp.where(place == 2, low[h : h + 1], tail)
+        out_ref[h, 3 * tokens :] = tail.astype(BF16)
+
+
+def state_body(tokens, arrived_ref, state_ref, fade_ref):
+    near, _, lanes = arrived_ref.shape
+    sums = [
+        jnp.sum(arrived_ref[b, 3 * tokens :].astype(F32), axis=0, keepdims=True)
+        for b in range(near)
+    ]
+    ends = [x[:, tokens - 1 : tokens] for x in sums]
+    left = jnp.zeros_like(ends[0])
+    state = jnp.zeros((lanes, lanes), F32)
+    for b in reversed(range(near)):
+        left = left + ends[b]
+        weight = jnp.exp(left - sums[b][:, :tokens])
+        key = jnp.transpose(arrived_ref[b, tokens : 2 * tokens].astype(F32))
+        state = state + jnp.dot(
+            (key * weight).astype(BF16),
+            arrived_ref[b, 2 * tokens : 3 * tokens],
+            preferred_element_type=F32,
+        )
+    state_ref[...] = state
+    fade_ref[...] = jnp.broadcast_to(jnp.exp(left), fade_ref.shape)
+
+
+def expert_body(near, rows_ref, gate_ref, up_ref, down_hbm, out_ref, down_ref, arrival):
+    pieces, height, columns = out_ref.shape
+    fetch = pltpu.make_async_copy(down_hbm, down_ref, arrival)
+    fetch.start()
+    owners = pieces // near
+    contract = (((1,), (1,)), ((), ()))
+    rows = rows_ref[...]
+    gate = lax.dot_general(rows, gate_ref[0], contract, preferred_element_type=F32)
+    up = lax.dot_general(rows, up_ref[0], contract, preferred_element_type=F32)
+    inner = (gate / (1.0 + jnp.exp(-gate)) * up).astype(BF16)
+    fetch.wait()
+    for j in range(owners):
+        part = jnp.dot(
+            inner,
+            down_ref[0, :, j * columns : (j + 1) * columns],
+            preferred_element_type=F32,
+        ).astype(BF16)
+        for r in range(near):
+            out_ref[r * owners + j] = part[r * height : (r + 1) * height]
+
+
+SMALL = pltpu.CompilerParams(vmem_limit_bytes=4 * 1024 * 1024)
+
+
+def whole(count):
+    return [pl.BlockSpec(memory_space=pltpu.VMEM)] * count
 
 
 def shards(
@@ -76,16 +171,18 @@
     far_groups = [[i + near * k for k in range(far)] for i in range(near)]
     near_all = [[m * owners + j for m in group for j in range(owners)] for group in near_groups]
 
-    def by_head(x):
-        return jnp.swapaxes(x.reshape(tokens, heads, lanes), 0, 1)
-
-    cumulative = jnp.cumsum(decay_log, axis=0)
-    terms = jnp.swapaxes(three_terms(cumulative), 0, 2)
-    terms = jnp.swapaxes(terms, 1, 2)
-    terms = jnp.pad(terms, ((0, 0), (0, 5), (0, lanes - tokens)))
-    payload = jnp.concatenate(
-        [by_head(queries), by_head(key_rows), by_head(value_rows), terms], axis=1
-    )
+    payload = pl.pallas_call(
+        payload_body,
+        out_shape=jax.ShapeDtypeStruct((heads, 3 * tokens + 8, lanes), BF16),
+        in_specs=[pl.BlockSpec(memory_space=pl.ANY)] * 4,
+        out_specs=whole(1)[0],
+        scratch_shapes=[
+            *[pltpu.VMEM((tokens, columns), BF16)] * 3,
+            pltpu.VMEM((heads, tokens), F32),
+            pltpu.SemaphoreType.DMA((4,)),
+        ],
+        name="payload",
+    )(queries, key_rows, value_rows, jnp.transpose(decay_log))
     arrived = lax.all_to_all(payload, "seq", 0, 0, tiled=True, axis_index_groups=near_groups)
     span = near * tokens
     query = arrived[:, :tokens].reshape(span, lanes)
@@ -94,12 +191,20 @@
     within = arrived[:, 3 * tokens : 3 * tokens + 3, :tokens].astype(F32).sum(axis=1)
     ends = within[:, -1]
     starts = jnp.cumsum(ends) - ends
-    total = jnp.sum(ends)
     cum = (within + starts[:, None]).reshape(span)
-    faded = (key.astype(F32) * jnp.exp(total - cum)[:, None]).astype(BF16)
-    state = lax.dot_general(faded, value, (((0,), (0,)), ((), ())), preferred_element_type=F32)
+    state, fade = pl.pallas_call(
+        partial(state_body, tokens),
+        out_shape=(
+            jax.ShapeDtypeStruct((lanes, lanes), F32),
+            jax.ShapeDtypeStruct((8, lanes), F32),
+        ),
+        in_specs=whole(1),
+        out_specs=tuple(whole(2)),
+        compiler_params=SMALL,
+        name="group_state",
+    )(arrived)
+    fade = fade[:1]
     my_far = lax.axis_index("seq") // near
-    fade = jnp.exp(total)
     first = state.astype(BF16)
     order = sorted(range(1, far), key=lambda g: (g != 1, min(g, far - g), -g))
     from_first = []
@@ -165,12 +270,15 @@
     gathered = lax.all_gather(normed, "seq", axis=0, tiled=True, axis_index_groups=far_groups)
     gathered = lax.all_gather(gathered, "seq", axis=0, tiled=True, axis_index_groups=near_groups)
     slot_rows = gathered.reshape(blocks * half_cap, width)
-    gate_val = project_rows(slot_rows, w_gate[0])
-    up_val = project_rows(slot_rows, w_up[0])
-    inner = (jax.nn.silu(gate_val) * up_val).astype(BF16)
-    partial = jnp.dot(inner, w_down[0], preferred_element_type=F32).astype(BF16)
-    pieces = partial.reshape(near, far * half_cap, owners, columns)
-    pieces = jnp.swapaxes(pieces, 1, 2).reshape(near * owners, far * half_cap, columns)
+    pieces = pl.pallas_call(
+        partial(expert_body, near),
+        out_shape=jax.ShapeDtypeStruct((near * owners, far * half_cap, columns), BF16),
+        in_specs=[*whole(3), pl.BlockSpec(memory_space=pl.ANY)],
+        out_specs=whole(1)[0],
+        scratch_shapes=[pltpu.VMEM(w_down.shape, BF16), pltpu.SemaphoreType.DMA],
+        compiler_params=pltpu.CompilerParams(vmem_limit_bytes=52_500_000),
+        name="experts",
+    )(slot_rows, w_gate, w_up, w_down)
     pieces = lax.all_to_all(
         pieces, ("seq", "exp", "rep"), 0, 0, tiled=True, axis_index_groups=near_all
     )

time: 246 us -> 244 us (level)
  matrix products: 6.71 us -> 2.19 us
  Pallas kernels: 0 us -> 3.58 us
  starting transfers between devices: 86.6 us -> 89.6 us
    dot_general x3 -> x0, matrix products: 4.52 us -> none  [the longest x1 2.5 us: shards(): partial = jnp.dot(inner, w_down[0], preferred_element_type=F32).astype(BF16)]
    pallas_call x0 -> x3, Pallas kernels: none -> 3.58 us  [the longest x1 1.66 us: shards(): pl.pallas_call(payload_body, out_shape=jax.ShapeDtypeStruct((heads, 3 * t...]
    ppermute x7, starting transfers between devices: 57.4 us -> 60.5 us  [shards(): lax.ppermute(first, 'seq', [(i, near * g + i) for i in range(near)])]
  transfers between devices with their start and end apart: 16 -> 16, of which waited for: 4 -> 4; matrix products, arithmetic and copies ran while one was open for 1% -> 2% of each run, Pallas kernels for 0% -> 0%
where the time goes in v5:
time: 244 us; the launch traced here: 242 us
  blocking collectives  126 us (52%)
  starting transfers between devices  89.6 us (37%)
  waiting for transfers between devices  12.3 us (5%)
  local copies, waits for them, and re-layouts  4.07 us (2%)
  other arithmetic  3.8 us (2%)
  Pallas kernels  3.58 us (1%)
    ppermute x7, starting transfers between devices, shards(): lax.ppermute(first, 'seq', [(i, near * g + i) for i in range(near)])  60.5 us
    all_to_all x1, blocking collectives, shards(): lax.all_to_all(pieces, 'seq', 0, 0, tiled=True, axis_index_groups=far_gro...  42.5 us
    all_to_all x1, blocking collectives, shards(): lax.all_to_all(pieces, ('seq', 'exp', 'rep'), 0, 0, tiled=True, axis_inde...  33.9 us
    all_gather x1, blocking collectives, shards(): lax.all_gather(normed, 'seq', axis=0, tiled=True, axis_index_groups=far_g...  33.7 us
    all_gather x1, blocking collectives, shards(): lax.all_gather(gathered, 'seq', axis=0, tiled=True, axis_index_groups=nea...  15.7 us
    all_to_all x1, starting transfers between devices, shards(): arrived = lax.all_to_all(payload, ('exp', 'rep'), 0, 0, tiled=True)  11.1 us
    all_to_all x1, starting transfers between devices, shards(): lax.all_to_all(payload, 'seq', 0, 0, tiled=True, axis_index_groups=near_g...  9.03 us
    all_to_all x1, starting transfers between devices, shards(): lax.all_to_all(attended, 'seq', 0, 0, tiled=True, axis_index_groups=near_...  4.93 us
  transfers between devices with their start and end apart: 16, of which 4 were waited for; matrix products, arithmetic and copies ran while one was open for 2% of the time, Pallas kernels for 0%

profile of v5, /device:TPU:33, one launch (start us, length us, event | category | flops | bytes accessed | tf_op | source)
XLA Modules:
  0.0 241.9 jit_solution(6857420124009225988)
XLA Ops:
  0.0 1.7 payload.1
  1.7 9.0 %all-to-all-start = ((bf16[4,200,128]{2,1,0:T(8,128)(2,1)}), bf16[4,200,128]{2,1,0:T(8,128)(2,1)S(1)}, u32[]{:S(2)}, u32[]{:S(2)}) async-start(bf16[4,200,128]{2,1,0:T(8,128)(2,1)} %payload.1), calls=%async_computation | async-start | bytes 409600 | tf_op jit(solution)/shard_map/all_to_all | solution.py:186
  10.7 0.8 copy.66
  11.5 0.1 eq.47
  11.6 0.7 reduce-precision_convert_fusion.1
  12.4 3.5 %all-to-all-done.arrived_ref = bf16[4,200,128]{2,1,0:T(8,128)(2,1)S(1)} async-done(((bf16[4,200,128]{2,1,0:T(8,128)(2,1)}), bf16[4,200,128]{2,1,0:T(8,128)(2,1)S(1)}, u32[]{:S(2)}, u32[]{:S(2)}) %all-to-all-start) | async-done | bytes 204832 | tf_op jit(solution)/shard_map/all_to_all | solution.py:186
  15.9 0.3 group_state.1
  16.2 0.7 collective-permute-start
  17.0 39.9 %collective-permute-start.12 = (bf16[128,128]{1,0:T(8,128)(2,1)S(1)}, bf16[128,128]{1,0:T(8,128)(2,1)S(1)}, u32[]{:S(2)}, u32[]{:S(2)}) collective-permute-start(bf16[128,128]{1,0:T(8,128)(2,1)S(1)} %convert_element_type.183), channel_id=1, source_target_pairs={{0,128},{8,136},{16,144},{24,152},{1,129},{9,137},{17,145},{25,153... | collective-permute-start | bytes 98312 | tf_op jit(solution)/shard_map/ppermute | solution.py:213
  56.9 1.3 collective-permute-start.11
  58.2 1.3 collective-permute-start.10
  59.5 1.3 collective-permute-start.9
  60.9 0.7 collective-permute-start.1
  61.7 0.7 collective-permute-start.2
  62.7 0.7 collective-permute-start.3
  63.3 0.2 subtract_reduce_fusion
  63.6 0.7 collective-permute-start.4
  64.5 0.1 add_convert_fusion
  64.6 0.7 collective-permute-start.5
  65.2 0.3 fusion.1
  65.6 13.4 %collective-permute-start.8 = (bf16[128,128]{1,0:T(8,128)(2,1)S(1)}, bf16[128,128]{1,0:T(8,128)(2,1)S(1)}, u32[]{:S(2)}, u32[]{:S(2)}) collective-permute-start(bf16[128,128]{1,0:T(8,128)(2,1)S(1)} %convert_element_type.183), channel_id=1, source_target_pairs={{0,192},{8,200},{16,208},{24,216},{1,193},{9,201},{17,209},{25,217... | collective-permute-start | bytes 98312 | tf_op jit(solution)/shard_map/ppermute | solution.py:213
  79.2 1.9 collective-permute-start.7
  81.2 1.3 collective-permute-start.6
  82.5 1.0 collective-permute-done.6
  83.5 0.9 fusion.2
  84.3 4.9 %all-to-all-start.1 = ((bf16[4,64,128]{2,1,0:T(8,128)(2,1)}), bf16[4,64,128]{2,1,0:T(8,128)(2,1)S(1)}, u32[]{:S(2)}, u32[]{:S(2)}) async-start(bf16[4,64,128]{2,1,0:T(8,128)(2,1)} %bitcast.5), calls=%async_computation.1 | async-start | bytes 131072 | tf_op jit(solution)/shard_map/all_to_all | solution.py:239
  89.5 0.2 reduce_window_sum.18
  89.8 0.2 eq.51
  90.0 0.2 eq.52
  90.2 0.2 mul.142
  90.4 0.2 mul.143
  90.6 0.2 fusion.34
  90.8 3.1 %all-to-all-done.1 = bf16[4,64,128]{2,1,0:T(8,128)(2,1)S(1)} async-done(((bf16[4,64,128]{2,1,0:T(8,128)(2,1)}), bf16[4,64,128]{2,1,0:T(8,128)(2,1)S(1)}, u32[]{:S(2)}, u32[]{:S(2)}) %all-to-all-start.1) | async-done | bytes 65568 | tf_op jit(solution)/shard_map/all_to_all | solution.py:239
  93.9 0.1 fusion.8
  94.1 0.2 convolution_convert_fusion
  94.3 0.6 pad_maximum_fusion
  95.0 11.1 %all-to-all-start.2 = ((bf16[8,40,128]{2,1,0:T(8,128)(2,1)}), bf16[8,40,128]{2,1,0:T(8,128)(2,1)S(1)}, u32[]{:S(2)}, u32[]{:S(2)}) async-start(bf16[8,40,128]{2,1,0:T(8,128)(2,1)} %pad_maximum_fusion), calls=%async_computation.2 | async-start | bytes 163840 | tf_op jit(solution)/shard_map/all_to_all | solution.py:254
  106.3 4.8 %all-to-all-done.2 = bf16[8,40,128]{2,1,0:T(8,128)(2,1)S(1)} async-done(((bf16[8,40,128]{2,1,0:T(8,128)(2,1)}), bf16[8,40,128]{2,1,0:T(8,128)(2,1)S(1)}, u32[]{:S(2)}, u32[]{:S(2)}) %all-to-all-start.2) | async-done | bytes 81952 | tf_op jit(solution)/shard_map/all_to_all | solution.py:254
  111.3 0.1 multiply_reduce_fusion.2
  111.4 0.2 multiply_reduce_fusion.1
  111.8 33.7 %all_gather.6 = bf16[768,128]{1,0:T(8,128)(2,1)S(1)} all-gather(bf16[96,128]{1,0:T(8,128)(2,1)S(1)} %reshape.205), channel_id=1, replica_groups={{0,32,64,96,128,160,192,224},{8,40,72,104,136,168,200,232},{16,48,80,11..., dimensions={0}, use_global_device_ids=true | all-gather | bytes 221184 | tf_op jit(solution)/shard_map/all_gather | solution.py:270
  145.4 15.7 %all_gather.7 = bf16[3072,128]{1,0:T(8,128)(2,1)} all-gather(bf16[768,128]{1,0:T(8,128)(2,1)S(1)} %all_gather.6), channel_id=1, replica_groups={{0,8,16,24},{32,40,48,56},{64,72,80,88},{96,104,112,120},{128,136,144,1..., dimensions={0}, use_global_device_ids=true | all-gather | bytes 983040 | tf_op jit(solution)/shard_map/all_gather | solution.py:271
  161.2 1.4 reshape.206.rows_ref
  162.6 1.7 experts.1
  164.3 33.9 %all_to_all.25 = bf16[32,24,512]{2,1,0:T(8,128)(2,1)S(1)} all-to-all(bf16[32,24,512]{2,1,0:T(8,128)(2,1)S(1)} %experts.1), channel_id=1, replica_groups={{0,1,2,3,4,5,6,7,8,9,10,11,12,13,14,15,16,17,18,19,20,21,22,23,24,25,26..., dimensions={0} | all-to-all | bytes 1572864 | tf_op jit(solution)/shard_map/all_to_all | solution.py:282
  198.2 0.1 reduce.4
  198.5 42.5 %all_to_all.26 = bf16[8,24,512]{2,1,0:T(8,128)(2,1)S(1)} all-to-all(bf16[8,24,512]{2,1,0:T(8,128)(2,1)S(1)} %copy.74), channel_id=1, replica_groups={{0,32,64,96,128,160,192,224},{8,40,72,104,136,168,200,232},{16,48,80,11..., dimensions={0} | all-to-all | bytes 393216 | tf_op jit(solution)/shard_map/all_to_all | solution.py:287
  241.1 0.8 fusion.3
  (77 shorter events, 2.3 us)
Async XLA Ops:
  1.7 14.2 %all-to-all-start = ((bf16[4,200,128]{2,1,0:T(8,128)(2,1)}), bf16[4,200,128]{2,1,0:T(8,128)(2,1)S(1)}, u32[]{:S(2)}, u32[]{:S(2)}) async-start(bf16[4,200,128]{2,1,0:T(8,128)(2,1)} %payload.1), calls=%async_computation | async-start | bytes 409600 | tf_op jit(solution)/shard_map/all_to_all | solution.py:186
  16.2 44.6 %collective-permute-start = (bf16[136,128]{1,0:T(8,128)(2,1)S(1)}, bf16[136,128]{1,0:T(8,128)(2,1)S(1)}, u32[]{:S(2)}, u32[]{:S(2)}) collective-permute-start(bf16[136,128]{1,0:T(8,128)(2,1)S(1)} %add_convert_fusion.5), channel_id=1, source_target_pairs={{32,64},{40,72},{48,80},{56,88},{33,65},{41,73},{49,81},{57,89},{3... | collective-permute-start | bytes 104456 | tf_op jit(solution)/shard_map/ppermute | solution.py:223
  17.0 62.2 %collective-permute-start.12 = (bf16[128,128]{1,0:T(8,128)(2,1)S(1)}, bf16[128,128]{1,0:T(8,128)(2,1)S(1)}, u32[]{:S(2)}, u32[]{:S(2)}) collective-permute-start(bf16[128,128]{1,0:T(8,128)(2,1)S(1)} %convert_element_type.183), channel_id=1, source_target_pairs={{0,128},{8,136},{16,144},{24,152},{1,129},{9,137},{17,145},{25,153... | collective-permute-start | bytes 98312 | tf_op jit(solution)/shard_map/ppermute | solution.py:213
  56.9 24.3 %collective-permute-start.11 = (bf16[128,128]{1,0:T(8,128)(2,1)S(1)}, bf16[128,128]{1,0:T(8,128)(2,1)S(1)}, u32[]{:S(2)}, u32[]{:S(2)}) collective-permute-start(bf16[128,128]{1,0:T(8,128)(2,1)S(1)} %convert_element_type.183), channel_id=1, source_target_pairs={{0,96},{8,104},{16,112},{24,120},{1,97},{9,105},{17,113},{25,121},... | collective-permute-start | bytes 98312 | tf_op jit(solution)/shard_map/ppermute | solution.py:213
  58.2 24.3 %collective-permute-start.10 = (bf16[128,128]{1,0:T(8,128)(2,1)S(1)}, bf16[128,128]{1,0:T(8,128)(2,1)S(1)}, u32[]{:S(2)}, u32[]{:S(2)}) collective-permute-start(bf16[128,128]{1,0:T(8,128)(2,1)S(1)} %convert_element_type.183), channel_id=1, source_target_pairs={{0,160},{8,168},{16,176},{24,184},{1,161},{9,169},{17,177},{25,185... | collective-permute-start | bytes 98312 | tf_op jit(solution)/shard_map/ppermute | solution.py:213
  59.5 23.0 %collective-permute-start.9 = (bf16[128,128]{1,0:T(8,128)(2,1)S(1)}, bf16[128,128]{1,0:T(8,128)(2,1)S(1)}, u32[]{:S(2)}, u32[]{:S(2)}) collective-permute-start(bf16[128,128]{1,0:T(8,128)(2,1)S(1)} %convert_element_type.183), channel_id=1, source_target_pairs={{0,64},{8,72},{16,80},{24,88},{1,65},{9,73},{17,81},{25,89},{2,66}... | collective-permute-start | bytes 98312 | tf_op jit(solution)/shard_map/ppermute | solution.py:213
  60.9 0.7 collective-permute-start.1
  61.7 0.8 collective-permute-start.2
  62.6 26.9 %copy-start.5 = (f32[64,2]{0,1:T(2,128)S(1)}, f32[64,2]{0,1:T(2,128)}, u32[]{:S(2)}) copy-start(f32[64,2]{0,1:T(2,128)} %param.22) | copy-start | bytes 1540
  62.7 0.9 collective-permute-start.3
  63.6 0.8 collective-permute-start.4
  64.6 1.0 collective-permute-start.5
  65.6 16.9 %collective-permute-start.8 = (bf16[128,128]{1,0:T(8,128)(2,1)S(1)}, bf16[128,128]{1,0:T(8,128)(2,1)S(1)}, u32[]{:S(2)}, u32[]{:S(2)}) collective-permute-start(bf16[128,128]{1,0:T(8,128)(2,1)S(1)} %convert_element_type.183), channel_id=1, source_target_pairs={{0,192},{8,200},{16,208},{24,216},{1,193},{9,201},{17,209},{25,217... | collective-permute-start | bytes 98312 | tf_op jit(solution)/shard_map/ppermute | solution.py:213
  79.2 3.3 %collective-permute-start.7 = (bf16[128,128]{1,0:T(8,128)(2,1)S(1)}, bf16[128,128]{1,0:T(8,128)(2,1)S(1)}, u32[]{:S(2)}, u32[]{:S(2)}) collective-permute-start(bf16[128,128]{1,0:T(8,128)(2,1)S(1)} %convert_element_type.183), channel_id=1, source_target_pairs={{0,224},{8,232},{16,240},{24,248},{1,225},{9,233},{17,241},{25,249... | collective-permute-start | bytes 98312 | tf_op jit(solution)/shard_map/ppermute | solution.py:213
  81.2 2.3 collective-permute-start.6
  84.3 9.7 %copy-start.2 = (bf16[64,512]{1,0:T(8,128)(2,1)S(1)}, bf16[64,512]{1,0:T(8,128)(2,1)}, u32[]{:S(2)}) copy-start(bf16[64,512]{1,0:T(8,128)(2,1)} %param.18) | copy-start | bytes 196612
  84.3 9.7 %copy-start.4 = (f32[512]{0:T(512)S(1)}, f32[512]{0:T(512)}, u32[]{:S(2)}) copy-start(f32[512]{0:T(512)} %param.19) | copy-start | bytes 6148
  84.3 9.7 %copy-start.3 = (bf16[64,512]{1,0:T(8,128)(2,1)S(1)}, bf16[64,512]{1,0:T(8,128)(2,1)}, u32[]{:S(2)}) copy-start(bf16[64,512]{1,0:T(8,128)(2,1)} %param.17) | copy-start | bytes 196612
  84.3 9.5 %all-to-all-start.1 = ((bf16[4,64,128]{2,1,0:T(8,128)(2,1)}), bf16[4,64,128]{2,1,0:T(8,128)(2,1)S(1)}, u32[]{:S(2)}, u32[]{:S(2)}) async-start(bf16[4,64,128]{2,1,0:T(8,128)(2,1)} %bitcast.5), calls=%async_computation.1 | async-start | bytes 131072 | tf_op jit(solution)/shard_map/all_to_all | solution.py:239
  95.0 16.1 %all-to-all-start.2 = ((bf16[8,40,128]{2,1,0:T(8,128)(2,1)}), bf16[8,40,128]{2,1,0:T(8,128)(2,1)S(1)}, u32[]{:S(2)}, u32[]{:S(2)}) async-start(bf16[8,40,128]{2,1,0:T(8,128)(2,1)} %pad_maximum_fusion), calls=%async_computation.2 | async-start | bytes 163840 | tf_op jit(solution)/shard_map/all_to_all | solution.py:254
  145.4 17.2 %copy-start = (bf16[1,144,4096]{2,1,0:T(8,128)(2,1)S(1)}, bf16[1,144,4096]{2,1,0:T(8,128)(2,1)}, u32[]{:S(2)}) copy-start(bf16[1,144,4096]{2,1,0:T(8,128)(2,1)} %gate_ref.1) | copy-start | bytes 3538948
  145.4 17.2 %copy-start.1 = (bf16[1,144,4096]{2,1,0:T(8,128)(2,1)S(1)}, bf16[1,144,4096]{2,1,0:T(8,128)(2,1)}, u32[]{:S(2)}) copy-start(bf16[1,144,4096]{2,1,0:T(8,128)(2,1)} %up_ref.1) | copy-start | bytes 3538948

commit v6 on v5

--- a/solution.py
+++ b/solution.py
@@ -91,7 +91,7 @@
         out_ref[h, 3 * tokens :] = tail.astype(BF16)
 
 
-def state_body(tokens, arrived_ref, state_ref, fade_ref):
+def state_body(tokens, arrived_ref, state_ref, fade_ref, own_ref):
     near, _, lanes = arrived_ref.shape
     sums = [
         jnp.sum(arrived_ref[b, 3 * tokens :].astype(F32), axis=0, keepdims=True)
@@ -110,20 +110,39 @@
             preferred_element_type=F32,
         )
     state_ref[...] = state
-    fade_ref[...] = jnp.broadcast_to(jnp.exp(left), fade_ref.shape)
-
-
-def expert_body(near, rows_ref, gate_ref, up_ref, down_hbm, out_ref, down_ref, arrival):
+    fade = jnp.broadcast_to(jnp.exp(left), fade_ref.shape)
+    fade_ref[...] = fade
+    high = rounded(fade)
+    middle = rounded(fade - high)
+    place = lax.broadcasted_iota(jnp.int32, fade.shape, 0)
+    tail = jnp.where(place == 2, fade - high - middle, 0.0)
+    tail = jnp.where(place == 1, middle, tail)
+    tail = jnp.where(place == 0, high, tail)
+    own_ref[:lanes] = state.astype(BF16)
+    own_ref[lanes:] = tail.astype(BF16)
+
+
+def expert_body(
+    near, rows_ref, gate_hbm, up_hbm, down_hbm, out_ref, gate_ref, up_ref, down_ref, arrivals
+):
     pieces, height, columns = out_ref.shape
-    fetch = pltpu.make_async_copy(down_hbm, down_ref, arrival)
-    fetch.start()
+    fetches = [
+        pltpu.make_async_copy(source, target, arrivals.at[i])
+        for i, (source, target) in enumerate(
+            [(gate_hbm, gate_ref), (up_hbm, up_ref), (down_hbm, down_ref)]
+        )
+    ]
+    for fetch in fetches:
+        fetch.start()
     owners = pieces // near
     contract = (((1,), (1,)), ((), ()))
     rows = rows_ref[...]
+    fetches[0].wait()
     gate = lax.dot_general(rows, gate_ref[0], contract, preferred_element_type=F32)
+    fetches[1].wait()
     up = lax.dot_general(rows, up_ref[0], contract, preferred_element_type=F32)
     inner = (gate / (1.0 + jnp.exp(-gate)) * up).astype(BF16)
-    fetch.wait()
+    fetches[2].wait()
     for j in range(owners):
         part = jnp.dot(
             inner,
@@ -192,39 +211,51 @@
     ends = within[:, -1]
     starts = jnp.cumsum(ends) - ends
     cum = (within + starts[:, None]).reshape(span)
-    state, fade = pl.pallas_call(
+    state, fade, own = pl.pallas_call(
         partial(state_body, tokens),
         out_shape=(
             jax.ShapeDtypeStruct((lanes, lanes), F32),
             jax.ShapeDtypeStruct((8, lanes), F32),
+            jax.ShapeDtypeStruct((lanes + 8, lanes), BF16),
         ),
         in_specs=whole(1),
-        out_specs=tuple(whole(2)),
+        out_specs=tuple(whole(3)),
         compiler_params=SMALL,
         name="group_state",
     )(arrived)
     fade = fade[:1]
     my_far = lax.axis_index("seq") // near
-    first = state.astype(BF16)
+
+    def passed(x, pairs):
+        return lax.ppermute(
+            x, "seq", [(near * p + i, near * q + i) for p, q in pairs for i in range(near)]
+        )
+
+    early = [(1, 2)] + [(g, g + 1) for g in range(4, far, 2)]
+    beside = passed(own, early)
+    first = own[:lanes]
     order = sorted(range(1, far), key=lambda g: (g != 1, min(g, far - g), -g))
     from_first = []
     for g in order:
-        from_first.append(
-            lax.ppermute(first, "seq", [(i, near * g + i) for i in range(near)])
-        )
+        from_first.append(passed(first, [(0, g)]))
+    joined = (my_far == 2) | ((my_far >= 5) & (my_far % 2 == 1))
+    beside = beside.astype(F32)
+    step = jnp.where(joined, beside[lanes] + beside[lanes + 1] + beside[lanes + 2], 1.0)[None]
     scales = jnp.exp2(jnp.arange(8, dtype=F32) / 8)[:, None]
     scales = jnp.broadcast_to(scales, (8, lanes))
-    own = jnp.pad(state, ((0, 8), (0, 0)))
-    opening = jnp.where(my_far <= 1, scales, 0.0)
-    carried = jnp.pad(opening, ((lanes, 0), (0, 0)))
-    for k in range(1, far - 1):
-        running = (fade * carried + own).astype(BF16)
-        passed = [(near * k + i, near * (k + 1) + i) for i in range(near)]
-        received = lax.ppermute(running, "seq", passed)
-        carried = carried + received.astype(F32)
-    factor = jnp.mean(carried[lanes:] / scales, axis=0)
+    carried = jnp.pad(jnp.where(my_far <= 2, scales, 0.0), ((lanes, 0), (0, 0)))
+    slope = fade * step
+    offset = jnp.pad(fade * beside[:lanes] + state, ((0, 8), (0, 0)))
+    running = (slope * carried + offset).astype(BF16)
+    carried = carried + passed(running, [(2, 3)]).astype(F32)
+    for g in range(3, far - 1, 2):
+        running = (slope * carried + offset).astype(BF16)
+        close = passed(running, [(g, g + 1)])
+        distant = passed(running, [(g, g + 2)])
+        carried = carried + close.astype(F32) + distant.astype(F32)
+    factor = jnp.mean(step * carried[lanes:] / scales, axis=0)
     from_first = sum(x.astype(F32) for x in from_first)
-    incoming = carried[:lanes] + factor * from_first
+    incoming = step * carried[:lanes] + beside[:lanes] + factor * from_first
     scores = lax.dot_general(query, key, (((1,), (1,)), ((), ())), preferred_element_type=F32)
     places = jnp.arange(span)
     causal = places[:, None] >= places[None, :]
@@ -273,10 +304,13 @@
     pieces = pl.pallas_call(
         partial(expert_body, near),
         out_shape=jax.ShapeDtypeStruct((near * owners, far * half_cap, columns), BF16),
-        in_specs=[*whole(3), pl.BlockSpec(memory_space=pl.ANY)],
+        in_specs=[*whole(1), *[pl.BlockSpec(memory_space=pl.ANY)] * 3],
         out_specs=whole(1)[0],
-        scratch_shapes=[pltpu.VMEM(w_down.shape, BF16), pltpu.SemaphoreType.DMA],
-        compiler_params=pltpu.CompilerParams(vmem_limit_bytes=52_500_000),
+        scratch_shapes=[
+            *[pltpu.VMEM(w.shape, BF16) for w in (w_gate, w_up, w_down)],
+            pltpu.SemaphoreType.DMA((3,)),
+        ],
+        compiler_params=pltpu.CompilerParams(vmem_limit_bytes=54_000_000),
         name="experts",
     )(slot_rows, w_gate, w_up, w_down)
     pieces = lax.all_to_all(

time: 244 us -> 251 us (1.029)
  starting transfers between devices: 89.6 us -> 98.1 us
    ppermute x13, starting transfers between devices: 64.5 us -> 72.9 us  [passed(): lax.ppermute(x, 'seq', [(near * p + i, near * q + i) for p, q in pairs fo...]
    all_to_all x1, starting transfers between devices: 4.93 us -> 8.76 us  [shards(): lax.all_to_all(attended, 'seq', 0, 0, tiled=True, axis_index_groups=near_...]
    all_to_all x1, starting transfers between devices: 11.1 us -> 7.38 us  [shards(): arrived = lax.all_to_all(payload, ('exp', 'rep'), 0, 0, tiled=True)]
where the time goes in v6:
time: 251 us; the launch traced here: 249 us
  blocking collectives  124 us (49%)
  starting transfers between devices  98.1 us (39%)
  waiting for transfers between devices  12.3 us (5%)
  Pallas kernels  5.1 us (2%)
  other arithmetic  3.54 us (1%)
  local copies, waits for them, and re-layouts  2.98 us (1%)
    ppermute x13, starting transfers between devices, passed(): lax.ppermute(x, 'seq', [(near * p + i, near * q + i) for p, q in pairs fo...  72.9 us
    all_to_all x1, blocking collectives, shards(): lax.all_to_all(pieces, 'seq', 0, 0, tiled=True, axis_index_groups=far_gro...  42.6 us
    all_gather x1, blocking collectives, shards(): lax.all_gather(normed, 'seq', axis=0, tiled=True, axis_index_groups=far_g...  33.6 us
    all_to_all x1, blocking collectives, shards(): lax.all_to_all(pieces, ('seq', 'exp', 'rep'), 0, 0, tiled=True, axis_inde...  33.6 us
    all_gather x1, blocking collectives, shards(): lax.all_gather(gathered, 'seq', axis=0, tiled=True, axis_index_groups=nea...  14.7 us
    all_to_all x1, starting transfers between devices, shards(): lax.all_to_all(payload, 'seq', 0, 0, tiled=True, axis_index_groups=near_g...  9.03 us
    all_to_all x1, starting transfers between devices, shards(): lax.all_to_all(attended, 'seq', 0, 0, tiled=True, axis_index_groups=near_...  8.76 us
    all_to_all x1, starting transfers between devices, shards(): arrived = lax.all_to_all(payload, ('exp', 'rep'), 0, 0, tiled=True)  7.38 us
  transfers between devices with their start and end apart: 16, of which 4 were waited for; matrix products, arithmetic and copies ran while one was open for 2% of the time, Pallas kernels for 0%

profile of v6, /device:TPU:33, one launch (start us, length us, event | category | flops | bytes accessed | tf_op | source)
XLA Modules:
  0.0 249.2 jit_solution(10110191323737354913)
XLA Ops:
  0.0 1.7 payload.1
  1.7 9.0 %all-to-all-start = ((bf16[4,200,128]{2,1,0:T(8,128)(2,1)}), bf16[4,200,128]{2,1,0:T(8,128)(2,1)S(1)}, u32[]{:S(2)}, u32[]{:S(2)}) async-start(bf16[4,200,128]{2,1,0:T(8,128)(2,1)} %payload.1), calls=%async_computation | async-start | bytes 409600 | tf_op jit(solution)/shard_map/all_to_all | solution.py:205
  10.7 0.7 reduce-precision_convert_fusion.1
  11.4 0.8 copy.66
  12.2 0.1 eq.55
  12.5 3.4 %all-to-all-done.arrived_ref = bf16[4,200,128]{2,1,0:T(8,128)(2,1)S(1)} async-done(((bf16[4,200,128]{2,1,0:T(8,128)(2,1)}), bf16[4,200,128]{2,1,0:T(8,128)(2,1)S(1)}, u32[]{:S(2)}, u32[]{:S(2)}) %all-to-all-start) | async-done | bytes 204832 | tf_op jit(solution)/shard_map/all_to_all | solution.py:205
  15.9 0.3 group_state.1
  16.2 39.9 %collective-permute-start.12 = (bf16[128,128]{1,0:T(8,128)(2,1)S(1)}, bf16[128,128]{1,0:T(8,128)(2,1)S(1)}, u32[]{:S(2)}, u32[]{:S(2)}) collective-permute-start(bf16[128,128]{1,0:T(8,128)(2,1)S(1)} %slice.67), channel_id=1, source_target_pairs={{0,128},{8,136},{16,144},{24,152},{1,129},{9,137},{17,145},{25,153... | collective-permute-start | bytes 98312 | tf_op jit(solution)/shard_map/ppermute | solution.py:230
  56.1 1.3 collective-permute-start.11
  57.4 1.3 collective-permute-start.10
  58.7 0.7 collective-permute-start
  59.7 0.7 collective-permute-start.1
  60.4 0.2 subtract_reduce_fusion
  60.6 0.7 collective-permute-start.3
  61.3 0.7 collective-permute-start.2
  62.2 0.1 add_convert_fusion
  62.3 0.7 collective-permute-start.5
  62.9 0.7 collective-permute-start.4
  63.6 0.3 fusion.1
  64.0 1.3 collective-permute-start.9
  65.3 22.5 %collective-permute-start.8 = (bf16[128,128]{1,0:T(8,128)(2,1)S(1)}, bf16[128,128]{1,0:T(8,128)(2,1)S(1)}, u32[]{:S(2)}, u32[]{:S(2)}) collective-permute-start(bf16[128,128]{1,0:T(8,128)(2,1)S(1)} %slice.67), channel_id=1, source_target_pairs={{0,192},{8,200},{16,208},{24,216},{1,193},{9,201},{17,209},{25,217... | collective-permute-start | bytes 98312 | tf_op jit(solution)/shard_map/ppermute | solution.py:230
  88.0 1.3 collective-permute-start.7
  89.3 1.3 collective-permute-start.6
  90.7 1.0 collective-permute-done.6
  91.6 0.9 fusion.2
  92.5 8.8 %all-to-all-start.1 = ((bf16[4,64,128]{2,1,0:T(8,128)(2,1)}), bf16[4,64,128]{2,1,0:T(8,128)(2,1)S(1)}, u32[]{:S(2)}, u32[]{:S(2)}) async-start(bf16[4,64,128]{2,1,0:T(8,128)(2,1)} %bitcast.7), calls=%async_computation.1 | async-start | bytes 131072 | tf_op jit(solution)/shard_map/all_to_all | solution.py:270
  101.5 0.2 reduce_window_sum.18
  101.7 0.2 eq.59
  101.9 0.2 eq.60
  102.1 0.2 mul.155
  102.3 0.2 mul.156
  102.5 0.2 fusion.38
  102.7 3.1 %all-to-all-done.1 = bf16[4,64,128]{2,1,0:T(8,128)(2,1)S(1)} async-done(((bf16[4,64,128]{2,1,0:T(8,128)(2,1)}), bf16[4,64,128]{2,1,0:T(8,128)(2,1)S(1)}, u32[]{:S(2)}, u32[]{:S(2)}) %all-to-all-start.1) | async-done | bytes 65568 | tf_op jit(solution)/shard_map/all_to_all | solution.py:270
  105.8 0.1 fusion.8
  106.1 0.2 convolution_convert_fusion
  106.3 0.6 pad_maximum_fusion
  107.0 7.4 %all-to-all-start.2 = ((bf16[8,40,128]{2,1,0:T(8,128)(2,1)}), bf16[8,40,128]{2,1,0:T(8,128)(2,1)S(1)}, u32[]{:S(2)}, u32[]{:S(2)}) async-start(bf16[8,40,128]{2,1,0:T(8,128)(2,1)} %pad_maximum_fusion), calls=%async_computation.2 | async-start | bytes 163840 | tf_op jit(solution)/shard_map/all_to_all | solution.py:285
  114.5 4.8 %all-to-all-done.2 = bf16[8,40,128]{2,1,0:T(8,128)(2,1)S(1)} async-done(((bf16[8,40,128]{2,1,0:T(8,128)(2,1)}), bf16[8,40,128]{2,1,0:T(8,128)(2,1)S(1)}, u32[]{:S(2)}, u32[]{:S(2)}) %all-to-all-start.2) | async-done | bytes 81952 | tf_op jit(solution)/shard_map/all_to_all | solution.py:285
  119.5 0.1 multiply_reduce_fusion.2
  119.7 0.2 multiply_reduce_fusion.1
  120.0 33.6 %all_gather.6 = bf16[768,128]{1,0:T(8,128)(2,1)S(1)} all-gather(bf16[96,128]{1,0:T(8,128)(2,1)S(1)} %reshape.205), channel_id=1, replica_groups={{0,32,64,96,128,160,192,224},{8,40,72,104,136,168,200,232},{16,48,80,11..., dimensions={0}, use_global_device_ids=true | all-gather | bytes 221184 | tf_op jit(solution)/shard_map/all_gather | solution.py:301
  153.6 14.7 %all_gather.7 = bf16[3072,128]{1,0:T(8,128)(2,1)S(1)} all-gather(bf16[768,128]{1,0:T(8,128)(2,1)S(1)} %all_gather.6), channel_id=1, replica_groups={{0,8,16,24},{32,40,48,56},{64,72,80,88},{96,104,112,120},{128,136,144,1..., dimensions={0}, use_global_device_ids=true | all-gather | bytes 983040 | tf_op jit(solution)/shard_map/all_gather | solution.py:302
  168.3 0.3 reshape.206.rows_ref
  168.6 3.2 %experts.1 = bf16[32,24,512]{2,1,0:T(8,128)(2,1)S(1)} custom-call(bf16[96,4096]{1,0:T(8,128)(2,1)S(1)} %reshape.206.rows_ref, bf16[1,144,4096]{2,1,0:T(8,128)(2,1)} %gate_hbm.1, bf16[1,144,4096]{2,1,0:T(8,128)(2,1)} %up_hbm.1, bf16[1,144,4096]{2,1,0:T(8,128)(2,1)} %down_hbm.1), custom_call_target="tpu_custom_call" | custom-call | tf_op jit(solution)/shard_map/experts/pallas_call | solution.py:304
  171.8 33.6 %all_to_all.25 = bf16[32,24,512]{2,1,0:T(8,128)(2,1)S(1)} all-to-all(bf16[32,24,512]{2,1,0:T(8,128)(2,1)S(1)} %experts.1), channel_id=1, replica_groups={{0,1,2,3,4,5,6,7,8,9,10,11,12,13,14,15,16,17,18,19,20,21,22,23,24,25,26..., dimensions={0} | all-to-all | bytes 1572864 | tf_op jit(solution)/shard_map/all_to_all | solution.py:316
  205.4 0.1 reduce.4
  205.7 42.6 %all_to_all.26 = bf16[8,24,512]{2,1,0:T(8,128)(2,1)S(1)} all-to-all(bf16[8,24,512]{2,1,0:T(8,128)(2,1)S(1)} %copy.74), channel_id=1, replica_groups={{0,32,64,96,128,160,192,224},{8,40,72,104,136,168,200,232},{16,48,80,11..., dimensions={0} | all-to-all | bytes 393216 | tf_op jit(solution)/shard_map/all_to_all | solution.py:321
  248.3 0.8 fusion.3
  (72 shorter events, 2.0 us)
Async XLA Ops:
  1.7 14.2 %all-to-all-start = ((bf16[4,200,128]{2,1,0:T(8,128)(2,1)}), bf16[4,200,128]{2,1,0:T(8,128)(2,1)S(1)}, u32[]{:S(2)}, u32[]{:S(2)}) async-start(bf16[4,200,128]{2,1,0:T(8,128)(2,1)} %payload.1), calls=%async_computation | async-start | bytes 409600 | tf_op jit(solution)/shard_map/all_to_all | solution.py:205
  16.2 71.8 %collective-permute-start.12 = (bf16[128,128]{1,0:T(8,128)(2,1)S(1)}, bf16[128,128]{1,0:T(8,128)(2,1)S(1)}, u32[]{:S(2)}, u32[]{:S(2)}) collective-permute-start(bf16[128,128]{1,0:T(8,128)(2,1)S(1)} %slice.67), channel_id=1, source_target_pairs={{0,128},{8,136},{16,144},{24,152},{1,129},{9,137},{17,145},{25,153... | collective-permute-start | bytes 98312 | tf_op jit(solution)/shard_map/ppermute | solution.py:230
  56.1 33.2 %collective-permute-start.11 = (bf16[128,128]{1,0:T(8,128)(2,1)S(1)}, bf16[128,128]{1,0:T(8,128)(2,1)S(1)}, u32[]{:S(2)}, u32[]{:S(2)}) collective-permute-start(bf16[128,128]{1,0:T(8,128)(2,1)S(1)} %slice.67), channel_id=1, source_target_pairs={{0,96},{8,104},{16,112},{24,120},{1,97},{9,105},{17,113},{25,121},... | collective-permute-start | bytes 98312 | tf_op jit(solution)/shard_map/ppermute | solution.py:230
  57.4 33.2 %collective-permute-start.10 = (bf16[128,128]{1,0:T(8,128)(2,1)S(1)}, bf16[128,128]{1,0:T(8,128)(2,1)S(1)}, u32[]{:S(2)}, u32[]{:S(2)}) collective-permute-start(bf16[128,128]{1,0:T(8,128)(2,1)S(1)} %slice.67), channel_id=1, source_target_pairs={{0,160},{8,168},{16,176},{24,184},{1,161},{9,169},{17,177},{25,185... | collective-permute-start | bytes 98312 | tf_op jit(solution)/shard_map/ppermute | solution.py:230
  58.7 0.8 collective-permute-start
  59.6 41.8 %copy-start.3 = (f32[64,2]{0,1:T(2,128)S(1)}, f32[64,2]{0,1:T(2,128)}, u32[]{:S(2)}) copy-start(f32[64,2]{0,1:T(2,128)} %param.22) | copy-start | bytes 1540
  59.7 0.9 collective-permute-start.1
  60.6 1.5 collective-permute-start.3
  61.3 0.8 collective-permute-start.2
  62.3 1.7 collective-permute-start.5
  62.9 2.3 collective-permute-start.4
  64.0 26.7 %collective-permute-start.9 = (bf16[128,128]{1,0:T(8,128)(2,1)S(1)}, bf16[128,128]{1,0:T(8,128)(2,1)S(1)}, u32[]{:S(2)}, u32[]{:S(2)}) collective-permute-start(bf16[128,128]{1,0:T(8,128)(2,1)S(1)} %slice.67), channel_id=1, source_target_pairs={{0,64},{8,72},{16,80},{24,88},{1,65},{9,73},{17,81},{25,89},{2,66}... | collective-permute-start | bytes 98312 | tf_op jit(solution)/shard_map/ppermute | solution.py:230
  65.3 25.4 %collective-permute-start.8 = (bf16[128,128]{1,0:T(8,128)(2,1)S(1)}, bf16[128,128]{1,0:T(8,128)(2,1)S(1)}, u32[]{:S(2)}, u32[]{:S(2)}) collective-permute-start(bf16[128,128]{1,0:T(8,128)(2,1)S(1)} %slice.67), channel_id=1, source_target_pairs={{0,192},{8,200},{16,208},{24,216},{1,193},{9,201},{17,209},{25,217... | collective-permute-start | bytes 98312 | tf_op jit(solution)/shard_map/ppermute | solution.py:230
  88.0 2.7 %collective-permute-start.7 = (bf16[128,128]{1,0:T(8,128)(2,1)S(1)}, bf16[128,128]{1,0:T(8,128)(2,1)S(1)}, u32[]{:S(2)}, u32[]{:S(2)}) collective-permute-start(bf16[128,128]{1,0:T(8,128)(2,1)S(1)} %slice.67), channel_id=1, source_target_pairs={{0,224},{8,232},{16,240},{24,248},{1,225},{9,233},{17,241},{25,249... | collective-permute-start | bytes 98312 | tf_op jit(solution)/shard_map/ppermute | solution.py:230
  89.3 2.3 collective-permute-start.6
  92.5 13.5 %copy-start = (bf16[64,512]{1,0:T(8,128)(2,1)S(1)}, bf16[64,512]{1,0:T(8,128)(2,1)}, u32[]{:S(2)}) copy-start(bf16[64,512]{1,0:T(8,128)(2,1)} %param.18) | copy-start | bytes 196612
  92.5 13.5 %copy-start.2 = (f32[512]{0:T(512)S(1)}, f32[512]{0:T(512)}, u32[]{:S(2)}) copy-start(f32[512]{0:T(512)} %param.19) | copy-start | bytes 6148
  92.5 13.6 %copy-start.1 = (bf16[64,512]{1,0:T(8,128)(2,1)S(1)}, bf16[64,512]{1,0:T(8,128)(2,1)}, u32[]{:S(2)}) copy-start(bf16[64,512]{1,0:T(8,128)(2,1)} %param.17) | copy-start | bytes 196612
  92.5 13.4 %all-to-all-start.1 = ((bf16[4,64,128]{2,1,0:T(8,128)(2,1)}), bf16[4,64,128]{2,1,0:T(8,128)(2,1)S(1)}, u32[]{:S(2)}, u32[]{:S(2)}) async-start(bf16[4,64,128]{2,1,0:T(8,128)(2,1)} %bitcast.7), calls=%async_computation.1 | async-start | bytes 131072 | tf_op jit(solution)/shard_map/all_to_all | solution.py:270
  107.0 12.3 %all-to-all-start.2 = ((bf16[8,40,128]{2,1,0:T(8,128)(2,1)}), bf16[8,40,128]{2,1,0:T(8,128)(2,1)S(1)}, u32[]{:S(2)}, u32[]{:S(2)}) async-start(bf16[8,40,128]{2,1,0:T(8,128)(2,1)} %pad_maximum_fusion), calls=%async_computation.2 | async-start | bytes 163840 | tf_op jit(solution)/shard_map/all_to_all | solution.py:285

commit v7 on v5

--- a/solution.py
+++ b/solution.py
@@ -91,7 +91,7 @@
         out_ref[h, 3 * tokens :] = tail.astype(BF16)
 
 
-def state_body(tokens, arrived_ref, state_ref, fade_ref):
+def state_body(tokens, arrived_ref, state_ref, fade_ref, own_ref):
     near, _, lanes = arrived_ref.shape
     sums = [
         jnp.sum(arrived_ref[b, 3 * tokens :].astype(F32), axis=0, keepdims=True)
@@ -110,7 +110,16 @@
             preferred_element_type=F32,
         )
     state_ref[...] = state
-    fade_ref[...] = jnp.broadcast_to(jnp.exp(left), fade_ref.shape)
+    fade = jnp.broadcast_to(jnp.exp(left), fade_ref.shape)
+    fade_ref[...] = fade
+    high = rounded(fade)
+    middle = rounded(fade - high)
+    place = lax.broadcasted_iota(jnp.int32, fade.shape, 0)
+    tail = jnp.where(place == 2, fade - high - middle, 0.0)
+    tail = jnp.where(place == 1, middle, tail)
+    tail = jnp.where(place == 0, high, tail)
+    own_ref[:lanes] = state.astype(BF16)
+    own_ref[lanes:] = tail.astype(BF16)
 
 
 def expert_body(near, rows_ref, gate_ref, up_ref, down_hbm, out_ref, down_ref, arrival):
@@ -192,39 +201,50 @@
     ends = within[:, -1]
     starts = jnp.cumsum(ends) - ends
     cum = (within + starts[:, None]).reshape(span)
-    state, fade = pl.pallas_call(
+    state, fade, own = pl.pallas_call(
         partial(state_body, tokens),
         out_shape=(
             jax.ShapeDtypeStruct((lanes, lanes), F32),
             jax.ShapeDtypeStruct((8, lanes), F32),
+            jax.ShapeDtypeStruct((lanes + 8, lanes), BF16),
         ),
         in_specs=whole(1),
-        out_specs=tuple(whole(2)),
+        out_specs=tuple(whole(3)),
         compiler_params=SMALL,
         name="group_state",
     )(arrived)
     fade = fade[:1]
     my_far = lax.axis_index("seq") // near
-    first = state.astype(BF16)
+
+    def passed(x, pairs):
+        return lax.ppermute(
+            x, "seq", [(near * p + i, near * q + i) for p, q in pairs for i in range(near)]
+        )
+
     order = sorted(range(1, far), key=lambda g: (g != 1, min(g, far - g), -g))
-    from_first = []
+    from_zero = jnp.zeros((lanes + 8, lanes), F32)
+    from_one = jnp.zeros((lanes + 8, lanes), F32)
+    direct = []
     for g in order:
-        from_first.append(
-            lax.ppermute(first, "seq", [(i, near * g + i) for i in range(near)])
-        )
+        other = g + 1 if g < far - 1 else 2
+        pairs = [(0, g)] if g == 1 else [(0, g), (1, other)]
+        direct.append((g, passed(own, pairs)))
     scales = jnp.exp2(jnp.arange(8, dtype=F32) / 8)[:, None]
     scales = jnp.broadcast_to(scales, (8, lanes))
-    own = jnp.pad(state, ((0, 8), (0, 0)))
-    opening = jnp.where(my_far <= 1, scales, 0.0)
-    carried = jnp.pad(opening, ((lanes, 0), (0, 0)))
-    for k in range(1, far - 1):
-        running = (fade * carried + own).astype(BF16)
-        passed = [(near * k + i, near * (k + 1) + i) for i in range(near)]
-        received = lax.ppermute(running, "seq", passed)
+    offset = jnp.pad(state, ((0, 8), (0, 0)))
+    carried = jnp.pad(jnp.where(my_far <= 2, scales, 0.0), ((lanes, 0), (0, 0)))
+    for k in range(2, far - 1):
+        running = (fade * carried + offset).astype(BF16)
+        received = passed(running, [(k, k + 1)])
         carried = carried + received.astype(F32)
-    factor = jnp.mean(carried[lanes:] / scales, axis=0)
-    from_first = sum(x.astype(F32) for x in from_first)
-    incoming = carried[:lanes] + factor * from_first
+    after_one = jnp.mean(carried[lanes:] / scales, axis=0)
+    for g, x in direct:
+        x = x.astype(F32)
+        from_zero = from_zero + jnp.where(my_far == g, x, 0.0)
+        from_one = from_one + jnp.where(my_far == g, 0.0, x)
+    one = from_one[lanes] + from_one[lanes + 1] + from_one[lanes + 2]
+    after_zero = after_one * jnp.where(my_far >= 2, one, 1.0)
+    incoming = carried[:lanes] + after_one * from_one[:lanes] + after_zero * from_zero[:lanes]
     scores = lax.dot_general(query, key, (((1,), (1,)), ((), ())), preferred_element_type=F32)
     places = jnp.arange(span)
     causal = places[:, None] >= places[None, :]

time: 244 us -> 237 us (0.971)
  starting transfers between devices: 89.6 us -> 81.7 us
    ppermute x13 -> x12, starting transfers between devices: 64.5 us -> 57.2 us  [passed(): lax.ppermute(x, 'seq', [(near * p + i, near * q + i) for p, q in pairs fo...]
    all_to_all x1, starting transfers between devices: 11.1 us -> 7.53 us  [shards(): arrived = lax.all_to_all(payload, ('exp', 'rep'), 0, 0, tiled=True)]
    all_to_all x1, starting transfers between devices: 4.93 us -> 7.87 us  [shards(): lax.all_to_all(attended, 'seq', 0, 0, tiled=True, axis_index_groups=near_...]
  transfers between devices with their start and end apart: 16 -> 15, of which waited for: 4 -> 5; matrix products, arithmetic and copies ran while one was open for 2% -> 2% of each run, Pallas kernels for 0% -> 0%
where the time goes in v7:
time: 237 us; the launch traced here: 235 us
  blocking collectives  126 us (53%)
  starting transfers between devices  81.7 us (34%)
  waiting for transfers between devices  13.5 us (6%)
  local copies, waits for them, and re-layouts  4.07 us (2%)
  other arithmetic  3.8 us (2%)
  Pallas kernels  3.59 us (2%)
    ppermute x12, starting transfers between devices, passed(): lax.ppermute(x, 'seq', [(near * p + i, near * q + i) for p, q in pairs fo...  57.2 us
    all_to_all x1, blocking collectives, shards(): lax.all_to_all(pieces, 'seq', 0, 0, tiled=True, axis_index_groups=far_gro...  42.7 us
    all_gather x1, blocking collectives, shards(): lax.all_gather(normed, 'seq', axis=0, tiled=True, axis_index_groups=far_g...  34.1 us
    all_to_all x1, blocking collectives, shards(): lax.all_to_all(pieces, ('seq', 'exp', 'rep'), 0, 0, tiled=True, axis_inde...  33.3 us
    all_gather x1, blocking collectives, shards(): lax.all_gather(gathered, 'seq', axis=0, tiled=True, axis_index_groups=nea...  15.9 us
    all_to_all x1, starting transfers between devices, shards(): lax.all_to_all(payload, 'seq', 0, 0, tiled=True, axis_index_groups=near_g...  9.03 us
    all_to_all x1, starting transfers between devices, shards(): lax.all_to_all(attended, 'seq', 0, 0, tiled=True, axis_index_groups=near_...  7.87 us
    all_to_all x1, starting transfers between devices, shards(): arrived = lax.all_to_all(payload, ('exp', 'rep'), 0, 0, tiled=True)  7.53 us
  transfers between devices with their start and end apart: 15, of which 5 were waited for; matrix products, arithmetic and copies ran while one was open for 2% of the time, Pallas kernels for 0%

profile of v7, /device:TPU:33, one launch (start us, length us, event | category | flops | bytes accessed | tf_op | source)
XLA Modules:
  0.0 235.3 jit_solution(10794261016005602751)
XLA Ops:
  0.0 1.7 payload.1
  1.7 9.0 %all-to-all-start = ((bf16[4,200,128]{2,1,0:T(8,128)(2,1)}), bf16[4,200,128]{2,1,0:T(8,128)(2,1)S(1)}, u32[]{:S(2)}, u32[]{:S(2)}) async-start(bf16[4,200,128]{2,1,0:T(8,128)(2,1)} %payload.1), calls=%async_computation | async-start | bytes 409600 | tf_op jit(solution)/shard_map/all_to_all | solution.py:195
  10.7 0.7 reduce-precision_convert_fusion.1
  11.4 0.8 copy.66
  12.2 0.1 eq.75
  12.5 3.4 %all-to-all-done.arrived_ref = bf16[4,200,128]{2,1,0:T(8,128)(2,1)S(1)} async-done(((bf16[4,200,128]{2,1,0:T(8,128)(2,1)}), bf16[4,200,128]{2,1,0:T(8,128)(2,1)S(1)}, u32[]{:S(2)}, u32[]{:S(2)}) %all-to-all-start) | async-done | bytes 204832 | tf_op jit(solution)/shard_map/all_to_all | solution.py:195
  15.9 0.3 group_state.1
  16.1 39.9 %collective-permute-start.11 = (bf16[136,128]{1,0:T(8,128)(2,1)S(1)}, bf16[136,128]{1,0:T(8,128)(2,1)S(1)}, u32[]{:S(2)}, u32[]{:S(2)}) collective-permute-start(bf16[136,128]{1,0:T(8,128)(2,1)S(1)} %get-tuple-element.10), channel_id=1, source_target_pairs={{0,128},{8,136},{16,144},{24,152},{32,160},{40,168},{48,176},{56,1... | collective-permute-start | bytes 104456 | tf_op jit(solution)/shard_map/ppermute | solution.py:220
  56.1 1.3 collective-permute-start.10
  57.4 1.3 collective-permute-start.9
  58.7 1.3 collective-permute-start.8
  60.1 0.7 collective-permute-start
  61.0 0.7 collective-permute-start.1
  61.7 0.2 subtract_reduce_fusion
  62.0 0.7 collective-permute-start.2
  62.9 0.7 collective-permute-start.3
  63.6 0.3 fusion.1
  64.0 1.3 collective-permute-start.7
  65.3 1.3 collective-permute-start.6
  66.6 7.5 %collective-permute-start.5 = (bf16[136,128]{1,0:T(8,128)(2,1)S(1)}, bf16[136,128]{1,0:T(8,128)(2,1)S(1)}, u32[]{:S(2)}, u32[]{:S(2)}) collective-permute-start(bf16[136,128]{1,0:T(8,128)(2,1)S(1)} %get-tuple-element.10), channel_id=1, source_target_pairs={{0,32},{8,40},{16,48},{24,56},{1,33},{9,41},{17,49},{25,57},{2,34}... | collective-permute-start | bytes 104456 | tf_op jit(solution)/shard_map/ppermute | solution.py:220
  74.2 0.7 collective-permute-start.4
  74.9 1.0 collective-permute-done.7
  75.9 1.3 collective-permute-done.6
  77.5 0.9 fusion.2
  78.4 7.9 %all-to-all-start.1 = ((bf16[4,64,128]{2,1,0:T(8,128)(2,1)}), bf16[4,64,128]{2,1,0:T(8,128)(2,1)S(1)}, u32[]{:S(2)}, u32[]{:S(2)}) async-start(bf16[4,64,128]{2,1,0:T(8,128)(2,1)} %bitcast.7), calls=%async_computation.1 | async-start | bytes 131072 | tf_op jit(solution)/shard_map/all_to_all | solution.py:259
  86.4 0.1 copy.68
  86.5 0.2 reduce_window_sum.18
  86.7 0.2 eq.79
  86.9 0.2 eq.80
  87.1 0.2 mul.150
  87.3 0.2 mul.151
  87.5 0.2 fusion.55
  87.7 3.1 %all-to-all-done.1 = bf16[4,64,128]{2,1,0:T(8,128)(2,1)S(1)} async-done(((bf16[4,64,128]{2,1,0:T(8,128)(2,1)}), bf16[4,64,128]{2,1,0:T(8,128)(2,1)S(1)}, u32[]{:S(2)}, u32[]{:S(2)}) %all-to-all-start.1) | async-done | bytes 65568 | tf_op jit(solution)/shard_map/all_to_all | solution.py:259
  90.8 0.1 fusion.8
  91.0 0.2 convolution_convert_fusion
  91.3 0.6 pad_maximum_fusion
  91.9 7.5 %all-to-all-start.2 = ((bf16[8,40,128]{2,1,0:T(8,128)(2,1)}), bf16[8,40,128]{2,1,0:T(8,128)(2,1)S(1)}, u32[]{:S(2)}, u32[]{:S(2)}) async-start(bf16[8,40,128]{2,1,0:T(8,128)(2,1)} %pad_maximum_fusion), calls=%async_computation.2 | async-start | bytes 163840 | tf_op jit(solution)/shard_map/all_to_all | solution.py:274
  99.6 4.8 %all-to-all-done.2 = bf16[8,40,128]{2,1,0:T(8,128)(2,1)S(1)} async-done(((bf16[8,40,128]{2,1,0:T(8,128)(2,1)}), bf16[8,40,128]{2,1,0:T(8,128)(2,1)S(1)}, u32[]{:S(2)}, u32[]{:S(2)}) %all-to-all-start.2) | async-done | bytes 81952 | tf_op jit(solution)/shard_map/all_to_all | solution.py:274
  104.7 0.1 multiply_reduce_fusion.2
  104.8 0.2 multiply_reduce_fusion.1
  105.1 34.1 %all_gather.6 = bf16[768,128]{1,0:T(8,128)(2,1)S(1)} all-gather(bf16[96,128]{1,0:T(8,128)(2,1)S(1)} %reshape.212), channel_id=1, replica_groups={{0,32,64,96,128,160,192,224},{8,40,72,104,136,168,200,232},{16,48,80,11..., dimensions={0}, use_global_device_ids=true | all-gather | bytes 221184 | tf_op jit(solution)/shard_map/all_gather | solution.py:290
  139.2 15.9 %all_gather.7 = bf16[3072,128]{1,0:T(8,128)(2,1)} all-gather(bf16[768,128]{1,0:T(8,128)(2,1)S(1)} %all_gather.6), channel_id=1, replica_groups={{0,8,16,24},{32,40,48,56},{64,72,80,88},{96,104,112,120},{128,136,144,1..., dimensions={0}, use_global_device_ids=true | all-gather | bytes 983040 | tf_op jit(solution)/shard_map/all_gather | solution.py:291
  155.1 1.4 reshape.213.rows_ref
  156.5 1.7 experts.1
  158.2 33.3 %all_to_all.25 = bf16[32,24,512]{2,1,0:T(8,128)(2,1)S(1)} all-to-all(bf16[32,24,512]{2,1,0:T(8,128)(2,1)S(1)} %experts.1), channel_id=1, replica_groups={{0,1,2,3,4,5,6,7,8,9,10,11,12,13,14,15,16,17,18,19,20,21,22,23,24,25,26..., dimensions={0} | all-to-all | bytes 1572864 | tf_op jit(solution)/shard_map/all_to_all | solution.py:302
  191.4 0.1 reduce.4
  191.8 42.7 %all_to_all.26 = bf16[8,24,512]{2,1,0:T(8,128)(2,1)S(1)} all-to-all(bf16[8,24,512]{2,1,0:T(8,128)(2,1)S(1)} %copy.74), channel_id=1, replica_groups={{0,32,64,96,128,160,192,224},{8,40,72,104,136,168,200,232},{16,48,80,11..., dimensions={0} | all-to-all | bytes 393216 | tf_op jit(solution)/shard_map/all_to_all | solution.py:307
  234.5 0.8 fusion.3
  (80 shorter events, 2.3 us)
Async XLA Ops:
  1.7 14.2 %all-to-all-start = ((bf16[4,200,128]{2,1,0:T(8,128)(2,1)}), bf16[4,200,128]{2,1,0:T(8,128)(2,1)S(1)}, u32[]{:S(2)}, u32[]{:S(2)}) async-start(bf16[4,200,128]{2,1,0:T(8,128)(2,1)} %payload.1), calls=%async_computation | async-start | bytes 409600 | tf_op jit(solution)/shard_map/all_to_all | solution.py:195
  16.1 47.8 %collective-permute-start.11 = (bf16[136,128]{1,0:T(8,128)(2,1)S(1)}, bf16[136,128]{1,0:T(8,128)(2,1)S(1)}, u32[]{:S(2)}, u32[]{:S(2)}) collective-permute-start(bf16[136,128]{1,0:T(8,128)(2,1)S(1)} %get-tuple-element.10), channel_id=1, source_target_pairs={{0,128},{8,136},{16,144},{24,152},{32,160},{40,168},{48,176},{56,1... | collective-permute-start | bytes 104456 | tf_op jit(solution)/shard_map/ppermute | solution.py:220
  56.1 9.2 %collective-permute-start.10 = (bf16[136,128]{1,0:T(8,128)(2,1)S(1)}, bf16[136,128]{1,0:T(8,128)(2,1)S(1)}, u32[]{:S(2)}, u32[]{:S(2)}) collective-permute-start(bf16[136,128]{1,0:T(8,128)(2,1)S(1)} %get-tuple-element.10), channel_id=1, source_target_pairs={{0,96},{8,104},{16,112},{24,120},{32,128},{40,136},{48,144},{56,15... | collective-permute-start | bytes 104456 | tf_op jit(solution)/shard_map/ppermute | solution.py:220
  57.4 16.8 %collective-permute-start.9 = (bf16[136,128]{1,0:T(8,128)(2,1)S(1)}, bf16[136,128]{1,0:T(8,128)(2,1)S(1)}, u32[]{:S(2)}, u32[]{:S(2)}) collective-permute-start(bf16[136,128]{1,0:T(8,128)(2,1)S(1)} %get-tuple-element.10), channel_id=1, source_target_pairs={{0,160},{8,168},{16,176},{24,184},{32,192},{40,200},{48,208},{56,2... | collective-permute-start | bytes 104456 | tf_op jit(solution)/shard_map/ppermute | solution.py:220
  58.7 16.2 %collective-permute-start.8 = (bf16[136,128]{1,0:T(8,128)(2,1)S(1)}, bf16[136,128]{1,0:T(8,128)(2,1)S(1)}, u32[]{:S(2)}, u32[]{:S(2)}) collective-permute-start(bf16[136,128]{1,0:T(8,128)(2,1)S(1)} %get-tuple-element.10), channel_id=1, source_target_pairs={{0,64},{8,72},{16,80},{24,88},{32,96},{40,104},{48,112},{56,120},{... | collective-permute-start | bytes 104456 | tf_op jit(solution)/shard_map/ppermute | solution.py:220
  60.1 0.8 collective-permute-start
  61.0 0.9 collective-permute-start.1
  62.0 0.8 collective-permute-start.2
  62.9 3.7 %collective-permute-start.3 = (bf16[136,128]{1,0:T(8,128)(2,1)S(1)}, bf16[136,128]{1,0:T(8,128)(2,1)S(1)}, u32[]{:S(2)}, u32[]{:S(2)}) collective-permute-start(bf16[136,128]{1,0:T(8,128)(2,1)S(1)} %add_convert_fusion.1), channel_id=1, source_target_pairs={{160,192},{168,200},{176,208},{184,216},{161,193},{169,201},{177,2... | collective-permute-start | bytes 104456 | tf_op jit(solution)/shard_map/ppermute | solution.py:220
  64.0 11.9 %collective-permute-start.7 = (bf16[136,128]{1,0:T(8,128)(2,1)S(1)}, bf16[136,128]{1,0:T(8,128)(2,1)S(1)}, u32[]{:S(2)}, u32[]{:S(2)}) collective-permute-start(bf16[136,128]{1,0:T(8,128)(2,1)S(1)} %get-tuple-element.10), channel_id=1, source_target_pairs={{0,192},{8,200},{16,208},{24,216},{32,224},{40,232},{48,240},{56,2... | collective-permute-start | bytes 104456 | tf_op jit(solution)/shard_map/ppermute | solution.py:220
  65.3 11.8 %collective-permute-start.6 = (bf16[136,128]{1,0:T(8,128)(2,1)S(1)}, bf16[136,128]{1,0:T(8,128)(2,1)S(1)}, u32[]{:S(2)}, u32[]{:S(2)}) collective-permute-start(bf16[136,128]{1,0:T(8,128)(2,1)S(1)} %get-tuple-element.10), channel_id=1, source_target_pairs={{0,224},{8,232},{16,240},{24,248},{32,64},{40,72},{48,80},{56,88},... | collective-permute-start | bytes 104456 | tf_op jit(solution)/shard_map/ppermute | solution.py:220
  66.6 10.5 %collective-permute-start.5 = (bf16[136,128]{1,0:T(8,128)(2,1)S(1)}, bf16[136,128]{1,0:T(8,128)(2,1)S(1)}, u32[]{:S(2)}, u32[]{:S(2)}) collective-permute-start(bf16[136,128]{1,0:T(8,128)(2,1)S(1)} %get-tuple-element.10), channel_id=1, source_target_pairs={{0,32},{8,40},{16,48},{24,56},{1,33},{9,41},{17,49},{25,57},{2,34}... | collective-permute-start | bytes 104456 | tf_op jit(solution)/shard_map/ppermute | solution.py:220
  74.2 12.2 %copy-start.5 = (f32[64,2]{0,1:T(2,128)S(1)}, f32[64,2]{0,1:T(2,128)}, u32[]{:S(2)}) copy-start(f32[64,2]{0,1:T(2,128)} %param.22) | copy-start | bytes 1540
  74.2 3.0 %collective-permute-start.4 = (bf16[136,128]{1,0:T(8,128)(2,1)S(1)}, bf16[136,128]{1,0:T(8,128)(2,1)S(1)}, u32[]{:S(2)}, u32[]{:S(2)}) collective-permute-start(bf16[136,128]{1,0:T(8,128)(2,1)S(1)} %add_convert_fusion), channel_id=1, source_target_pairs={{192,224},{200,232},{208,240},{216,248},{193,225},{201,233},{209,2... | collective-permute-start | bytes 104456 | tf_op jit(solution)/shard_map/ppermute | solution.py:220
  78.4 12.6 %copy-start.2 = (bf16[64,512]{1,0:T(8,128)(2,1)S(1)}, bf16[64,512]{1,0:T(8,128)(2,1)}, u32[]{:S(2)}) copy-start(bf16[64,512]{1,0:T(8,128)(2,1)} %param.18) | copy-start | bytes 196612
  78.4 12.6 %copy-start.4 = (f32[512]{0:T(512)S(1)}, f32[512]{0:T(512)}, u32[]{:S(2)}) copy-start(f32[512]{0:T(512)} %param.19) | copy-start | bytes 6148
  78.4 12.7 %copy-start.3 = (bf16[64,512]{1,0:T(8,128)(2,1)S(1)}, bf16[64,512]{1,0:T(8,128)(2,1)}, u32[]{:S(2)}) copy-start(bf16[64,512]{1,0:T(8,128)(2,1)} %param.17) | copy-start | bytes 196612
  78.4 12.5 %all-to-all-start.1 = ((bf16[4,64,128]{2,1,0:T(8,128)(2,1)}), bf16[4,64,128]{2,1,0:T(8,128)(2,1)S(1)}, u32[]{:S(2)}, u32[]{:S(2)}) async-start(bf16[4,64,128]{2,1,0:T(8,128)(2,1)} %bitcast.7), calls=%async_computation.1 | async-start | bytes 131072 | tf_op jit(solution)/shard_map/all_to_all | solution.py:259
  91.9 12.4 %all-to-all-start.2 = ((bf16[8,40,128]{2,1,0:T(8,128)(2,1)}), bf16[8,40,128]{2,1,0:T(8,128)(2,1)S(1)}, u32[]{:S(2)}, u32[]{:S(2)}) async-start(bf16[8,40,128]{2,1,0:T(8,128)(2,1)} %pad_maximum_fusion), calls=%async_computation.2 | async-start | bytes 163840 | tf_op jit(solution)/shard_map/all_to_all | solution.py:274
  139.2 17.3 %copy-start = (bf16[1,144,4096]{2,1,0:T(8,128)(2,1)S(1)}, bf16[1,144,4096]{2,1,0:T(8,128)(2,1)}, u32[]{:S(2)}) copy-start(bf16[1,144,4096]{2,1,0:T(8,128)(2,1)} %gate_ref.1) | copy-start | bytes 3538948
  139.2 17.3 %copy-start.1 = (bf16[1,144,4096]{2,1,0:T(8,128)(2,1)S(1)}, bf16[1,144,4096]{2,1,0:T(8,128)(2,1)}, u32[]{:S(2)}) copy-start(bf16[1,144,4096]{2,1,0:T(8,128)(2,1)} %up_ref.1) | copy-start | bytes 3538948

commit v8 on v5

--- a/solution.py
+++ b/solution.py
@@ -113,17 +113,24 @@
     fade_ref[...] = jnp.broadcast_to(jnp.exp(left), fade_ref.shape)
 
 
-def expert_body(near, rows_ref, gate_ref, up_ref, down_hbm, out_ref, down_ref, arrival):
+def expert_body(
+    near, rows_ref, gate_ref, up_hbm, down_hbm, out_ref, up_ref, down_ref, arrivals
+):
     pieces, height, columns = out_ref.shape
-    fetch = pltpu.make_async_copy(down_hbm, down_ref, arrival)
-    fetch.start()
+    fetches = [
+        pltpu.make_async_copy(up_hbm, up_ref, arrivals.at[0]),
+        pltpu.make_async_copy(down_hbm, down_ref, arrivals.at[1]),
+    ]
+    for fetch in fetches:
+        fetch.start()
     owners = pieces // near
     contract = (((1,), (1,)), ((), ()))
     rows = rows_ref[...]
     gate = lax.dot_general(rows, gate_ref[0], contract, preferred_element_type=F32)
+    fetches[0].wait()
     up = lax.dot_general(rows, up_ref[0], contract, preferred_element_type=F32)
     inner = (gate / (1.0 + jnp.exp(-gate)) * up).astype(BF16)
-    fetch.wait()
+    fetches[1].wait()
     for j in range(owners):
         part = jnp.dot(
             inner,
@@ -273,10 +280,13 @@
     pieces = pl.pallas_call(
         partial(expert_body, near),
         out_shape=jax.ShapeDtypeStruct((near * owners, far * half_cap, columns), BF16),
-        in_specs=[*whole(3), pl.BlockSpec(memory_space=pl.ANY)],
+        in_specs=[*whole(2), *[pl.BlockSpec(memory_space=pl.ANY)] * 2],
         out_specs=whole(1)[0],
-        scratch_shapes=[pltpu.VMEM(w_down.shape, BF16), pltpu.SemaphoreType.DMA],
-        compiler_params=pltpu.CompilerParams(vmem_limit_bytes=52_500_000),
+        scratch_shapes=[
+            *[pltpu.VMEM(w.shape, BF16) for w in (w_up, w_down)],
+            pltpu.SemaphoreType.DMA((2,)),
+        ],
+        compiler_params=pltpu.CompilerParams(vmem_limit_bytes=53_200_000),
         name="experts",
     )(slot_rows, w_gate, w_up, w_down)
     pieces = lax.all_to_all(

time: 244 us -> 243 us (level)
  no operation moved by 1% of the time
where the time goes in v8:
time: 243 us; the launch traced here: 241 us
  blocking collectives  125 us (51%)
  starting transfers between devices  89.6 us (37%)
  waiting for transfers between devices  12.3 us (5%)
  Pallas kernels  4.34 us (2%)
  other arithmetic  3.8 us (2%)
  local copies, waits for them, and re-layouts  2.98 us (1%)
    ppermute x7, starting transfers between devices, shards(): lax.ppermute(first, 'seq', [(i, near * g + i) for i in range(near)])  60.5 us
    all_to_all x1, blocking collectives, shards(): lax.all_to_all(pieces, 'seq', 0, 0, tiled=True, axis_index_groups=far_gro...  42.5 us
    all_to_all x1, blocking collectives, shards(): lax.all_to_all(pieces, ('seq', 'exp', 'rep'), 0, 0, tiled=True, axis_inde...  33.8 us
    all_gather x1, blocking collectives, shards(): lax.all_gather(normed, 'seq', axis=0, tiled=True, axis_index_groups=far_g...  33.7 us
    all_gather x1, blocking collectives, shards(): lax.all_gather(gathered, 'seq', axis=0, tiled=True, axis_index_groups=nea...  14.9 us
    all_to_all x1, starting transfers between devices, shards(): arrived = lax.all_to_all(payload, ('exp', 'rep'), 0, 0, tiled=True)  11.1 us
    all_to_all x1, starting transfers between devices, shards(): lax.all_to_all(payload, 'seq', 0, 0, tiled=True, axis_index_groups=near_g...  9.03 us
    all_to_all x1, starting transfers between devices, shards(): lax.all_to_all(attended, 'seq', 0, 0, tiled=True, axis_index_groups=near_...  4.93 us
  transfers between devices with their start and end apart: 16, of which 4 were waited for; matrix products, arithmetic and copies ran while one was open for 2% of the time, Pallas kernels for 0%

profile of v8, /device:TPU:33, one launch (start us, length us, event | category | flops | bytes accessed | tf_op | source)
XLA Modules:
  0.0 240.6 jit_solution(382331435220205856)
XLA Ops:
  0.0 1.7 payload.1
  1.7 9.0 %all-to-all-start = ((bf16[4,200,128]{2,1,0:T(8,128)(2,1)}), bf16[4,200,128]{2,1,0:T(8,128)(2,1)S(1)}, u32[]{:S(2)}, u32[]{:S(2)}) async-start(bf16[4,200,128]{2,1,0:T(8,128)(2,1)} %payload.1), calls=%async_computation | async-start | bytes 409600 | tf_op jit(solution)/shard_map/all_to_all | solution.py:193
  10.7 0.8 copy.66
  11.5 0.1 eq.47
  11.6 0.7 reduce-precision_convert_fusion.1
  12.4 3.5 %all-to-all-done.arrived_ref = bf16[4,200,128]{2,1,0:T(8,128)(2,1)S(1)} async-done(((bf16[4,200,128]{2,1,0:T(8,128)(2,1)}), bf16[4,200,128]{2,1,0:T(8,128)(2,1)S(1)}, u32[]{:S(2)}, u32[]{:S(2)}) %all-to-all-start) | async-done | bytes 204832 | tf_op jit(solution)/shard_map/all_to_all | solution.py:193
  15.9 0.3 group_state.1
  16.2 0.7 collective-permute-start
  17.0 39.9 %collective-permute-start.12 = (bf16[128,128]{1,0:T(8,128)(2,1)S(1)}, bf16[128,128]{1,0:T(8,128)(2,1)S(1)}, u32[]{:S(2)}, u32[]{:S(2)}) collective-permute-start(bf16[128,128]{1,0:T(8,128)(2,1)S(1)} %convert_element_type.183), channel_id=1, source_target_pairs={{0,128},{8,136},{16,144},{24,152},{1,129},{9,137},{17,145},{25,153... | collective-permute-start | bytes 98312 | tf_op jit(solution)/shard_map/ppermute | solution.py:220
  56.9 1.3 collective-permute-start.11
  58.2 1.3 collective-permute-start.10
  59.5 1.3 collective-permute-start.9
  60.9 0.7 collective-permute-start.1
  61.7 0.7 collective-permute-start.2
  62.7 0.7 collective-permute-start.3
  63.3 0.2 subtract_reduce_fusion
  63.6 0.7 collective-permute-start.4
  64.5 0.1 add_convert_fusion
  64.6 0.7 collective-permute-start.5
  65.2 0.3 fusion.1
  65.6 13.4 %collective-permute-start.8 = (bf16[128,128]{1,0:T(8,128)(2,1)S(1)}, bf16[128,128]{1,0:T(8,128)(2,1)S(1)}, u32[]{:S(2)}, u32[]{:S(2)}) collective-permute-start(bf16[128,128]{1,0:T(8,128)(2,1)S(1)} %convert_element_type.183), channel_id=1, source_target_pairs={{0,192},{8,200},{16,208},{24,216},{1,193},{9,201},{17,209},{25,217... | collective-permute-start | bytes 98312 | tf_op jit(solution)/shard_map/ppermute | solution.py:220
  79.2 1.9 collective-permute-start.7
  81.2 1.3 collective-permute-start.6
  82.5 1.0 collective-permute-done.6
  83.5 0.9 fusion.2
  84.3 4.9 %all-to-all-start.1 = ((bf16[4,64,128]{2,1,0:T(8,128)(2,1)}), bf16[4,64,128]{2,1,0:T(8,128)(2,1)S(1)}, u32[]{:S(2)}, u32[]{:S(2)}) async-start(bf16[4,64,128]{2,1,0:T(8,128)(2,1)} %bitcast.5), calls=%async_computation.1 | async-start | bytes 131072 | tf_op jit(solution)/shard_map/all_to_all | solution.py:246
  89.5 0.2 reduce_window_sum.18
  89.8 0.2 eq.51
  90.0 0.2 eq.52
  90.2 0.2 mul.142
  90.4 0.2 mul.143
  90.6 0.2 fusion.34
  90.8 3.1 %all-to-all-done.1 = bf16[4,64,128]{2,1,0:T(8,128)(2,1)S(1)} async-done(((bf16[4,64,128]{2,1,0:T(8,128)(2,1)}), bf16[4,64,128]{2,1,0:T(8,128)(2,1)S(1)}, u32[]{:S(2)}, u32[]{:S(2)}) %all-to-all-start.1) | async-done | bytes 65568 | tf_op jit(solution)/shard_map/all_to_all | solution.py:246
  93.9 0.1 fusion.8
  94.1 0.2 convolution_convert_fusion
  94.3 0.6 pad_maximum_fusion
  95.0 11.1 %all-to-all-start.2 = ((bf16[8,40,128]{2,1,0:T(8,128)(2,1)}), bf16[8,40,128]{2,1,0:T(8,128)(2,1)S(1)}, u32[]{:S(2)}, u32[]{:S(2)}) async-start(bf16[8,40,128]{2,1,0:T(8,128)(2,1)} %pad_maximum_fusion), calls=%async_computation.2 | async-start | bytes 163840 | tf_op jit(solution)/shard_map/all_to_all | solution.py:261
  106.3 4.8 %all-to-all-done.2 = bf16[8,40,128]{2,1,0:T(8,128)(2,1)S(1)} async-done(((bf16[8,40,128]{2,1,0:T(8,128)(2,1)}), bf16[8,40,128]{2,1,0:T(8,128)(2,1)S(1)}, u32[]{:S(2)}, u32[]{:S(2)}) %all-to-all-start.2) | async-done | bytes 81952 | tf_op jit(solution)/shard_map/all_to_all | solution.py:261
  111.3 0.1 multiply_reduce_fusion.2
  111.4 0.2 multiply_reduce_fusion.1
  111.8 33.7 %all_gather.6 = bf16[768,128]{1,0:T(8,128)(2,1)S(1)} all-gather(bf16[96,128]{1,0:T(8,128)(2,1)S(1)} %reshape.205), channel_id=1, replica_groups={{0,32,64,96,128,160,192,224},{8,40,72,104,136,168,200,232},{16,48,80,11..., dimensions={0}, use_global_device_ids=true | all-gather | bytes 221184 | tf_op jit(solution)/shard_map/all_gather | solution.py:277
  145.4 14.9 %all_gather.7 = bf16[3072,128]{1,0:T(8,128)(2,1)S(1)} all-gather(bf16[768,128]{1,0:T(8,128)(2,1)S(1)} %all_gather.6), channel_id=1, replica_groups={{0,8,16,24},{32,40,48,56},{64,72,80,88},{96,104,112,120},{128,136,144,1..., dimensions={0}, use_global_device_ids=true | all-gather | bytes 983040 | tf_op jit(solution)/shard_map/all_gather | solution.py:278
  160.4 0.3 reshape.206.rows_ref
  160.7 2.4 %experts.1 = bf16[32,24,512]{2,1,0:T(8,128)(2,1)S(1)} custom-call(bf16[96,4096]{1,0:T(8,128)(2,1)S(1)} %reshape.206.rows_ref, bf16[1,144,4096]{2,1,0:T(8,128)(2,1)S(1)} %copy-done, bf16[1,144,4096]{2,1,0:T(8,128)(2,1)} %up_hbm.1, bf16[1,144,4096]{2,1,0:T(8,128)(2,1)} %down_hbm.1), custom_call_target="tpu_custom_call" | custom-call | tf_op jit(solution)/shard_map/experts/pallas_call | solution.py:280
  163.1 33.8 %all_to_all.25 = bf16[32,24,512]{2,1,0:T(8,128)(2,1)S(1)} all-to-all(bf16[32,24,512]{2,1,0:T(8,128)(2,1)S(1)} %experts.1), channel_id=1, replica_groups={{0,1,2,3,4,5,6,7,8,9,10,11,12,13,14,15,16,17,18,19,20,21,22,23,24,25,26..., dimensions={0} | all-to-all | bytes 1572864 | tf_op jit(solution)/shard_map/all_to_all | solution.py:292
  196.9 0.1 reduce.4
  197.2 42.5 %all_to_all.26 = bf16[8,24,512]{2,1,0:T(8,128)(2,1)S(1)} all-to-all(bf16[8,24,512]{2,1,0:T(8,128)(2,1)S(1)} %copy.74), channel_id=1, replica_groups={{0,32,64,96,128,160,192,224},{8,40,72,104,136,168,200,232},{16,48,80,11..., dimensions={0} | all-to-all | bytes 393216 | tf_op jit(solution)/shard_map/all_to_all | solution.py:297
  239.7 0.8 fusion.3
  (75 shorter events, 2.3 us)
Async XLA Ops:
  1.7 14.2 %all-to-all-start = ((bf16[4,200,128]{2,1,0:T(8,128)(2,1)}), bf16[4,200,128]{2,1,0:T(8,128)(2,1)S(1)}, u32[]{:S(2)}, u32[]{:S(2)}) async-start(bf16[4,200,128]{2,1,0:T(8,128)(2,1)} %payload.1), calls=%async_computation | async-start | bytes 409600 | tf_op jit(solution)/shard_map/all_to_all | solution.py:193
  16.2 44.6 %collective-permute-start = (bf16[136,128]{1,0:T(8,128)(2,1)S(1)}, bf16[136,128]{1,0:T(8,128)(2,1)S(1)}, u32[]{:S(2)}, u32[]{:S(2)}) collective-permute-start(bf16[136,128]{1,0:T(8,128)(2,1)S(1)} %add_convert_fusion.5), channel_id=1, source_target_pairs={{32,64},{40,72},{48,80},{56,88},{33,65},{41,73},{49,81},{57,89},{3... | collective-permute-start | bytes 104456 | tf_op jit(solution)/shard_map/ppermute | solution.py:230
  17.0 62.2 %collective-permute-start.12 = (bf16[128,128]{1,0:T(8,128)(2,1)S(1)}, bf16[128,128]{1,0:T(8,128)(2,1)S(1)}, u32[]{:S(2)}, u32[]{:S(2)}) collective-permute-start(bf16[128,128]{1,0:T(8,128)(2,1)S(1)} %convert_element_type.183), channel_id=1, source_target_pairs={{0,128},{8,136},{16,144},{24,152},{1,129},{9,137},{17,145},{25,153... | collective-permute-start | bytes 98312 | tf_op jit(solution)/shard_map/ppermute | solution.py:220
  56.9 24.3 %collective-permute-start.11 = (bf16[128,128]{1,0:T(8,128)(2,1)S(1)}, bf16[128,128]{1,0:T(8,128)(2,1)S(1)}, u32[]{:S(2)}, u32[]{:S(2)}) collective-permute-start(bf16[128,128]{1,0:T(8,128)(2,1)S(1)} %convert_element_type.183), channel_id=1, source_target_pairs={{0,96},{8,104},{16,112},{24,120},{1,97},{9,105},{17,113},{25,121},... | collective-permute-start | bytes 98312 | tf_op jit(solution)/shard_map/ppermute | solution.py:220
  58.2 24.3 %collective-permute-start.10 = (bf16[128,128]{1,0:T(8,128)(2,1)S(1)}, bf16[128,128]{1,0:T(8,128)(2,1)S(1)}, u32[]{:S(2)}, u32[]{:S(2)}) collective-permute-start(bf16[128,128]{1,0:T(8,128)(2,1)S(1)} %convert_element_type.183), channel_id=1, source_target_pairs={{0,160},{8,168},{16,176},{24,184},{1,161},{9,169},{17,177},{25,185... | collective-permute-start | bytes 98312 | tf_op jit(solution)/shard_map/ppermute | solution.py:220
  59.5 23.0 %collective-permute-start.9 = (bf16[128,128]{1,0:T(8,128)(2,1)S(1)}, bf16[128,128]{1,0:T(8,128)(2,1)S(1)}, u32[]{:S(2)}, u32[]{:S(2)}) collective-permute-start(bf16[128,128]{1,0:T(8,128)(2,1)S(1)} %convert_element_type.183), channel_id=1, source_target_pairs={{0,64},{8,72},{16,80},{24,88},{1,65},{9,73},{17,81},{25,89},{2,66}... | collective-permute-start | bytes 98312 | tf_op jit(solution)/shard_map/ppermute | solution.py:220
  60.9 0.7 collective-permute-start.1
  61.7 0.8 collective-permute-start.2
  62.6 26.9 %copy-start.4 = (f32[64,2]{0,1:T(2,128)S(1)}, f32[64,2]{0,1:T(2,128)}, u32[]{:S(2)}) copy-start(f32[64,2]{0,1:T(2,128)} %param.22) | copy-start | bytes 1540
  62.7 0.9 collective-permute-start.3
  63.6 0.8 collective-permute-start.4
  64.6 1.0 collective-permute-start.5
  65.6 16.9 %collective-permute-start.8 = (bf16[128,128]{1,0:T(8,128)(2,1)S(1)}, bf16[128,128]{1,0:T(8,128)(2,1)S(1)}, u32[]{:S(2)}, u32[]{:S(2)}) collective-permute-start(bf16[128,128]{1,0:T(8,128)(2,1)S(1)} %convert_element_type.183), channel_id=1, source_target_pairs={{0,192},{8,200},{16,208},{24,216},{1,193},{9,201},{17,209},{25,217... | collective-permute-start | bytes 98312 | tf_op jit(solution)/shard_map/ppermute | solution.py:220
  79.2 3.3 %collective-permute-start.7 = (bf16[128,128]{1,0:T(8,128)(2,1)S(1)}, bf16[128,128]{1,0:T(8,128)(2,1)S(1)}, u32[]{:S(2)}, u32[]{:S(2)}) collective-permute-start(bf16[128,128]{1,0:T(8,128)(2,1)S(1)} %convert_element_type.183), channel_id=1, source_target_pairs={{0,224},{8,232},{16,240},{24,248},{1,225},{9,233},{17,241},{25,249... | collective-permute-start | bytes 98312 | tf_op jit(solution)/shard_map/ppermute | solution.py:220
  81.2 2.3 collective-permute-start.6
  84.3 9.7 %copy-start.1 = (bf16[64,512]{1,0:T(8,128)(2,1)S(1)}, bf16[64,512]{1,0:T(8,128)(2,1)}, u32[]{:S(2)}) copy-start(bf16[64,512]{1,0:T(8,128)(2,1)} %param.18) | copy-start | bytes 196612
  84.3 9.7 %copy-start.3 = (f32[512]{0:T(512)S(1)}, f32[512]{0:T(512)}, u32[]{:S(2)}) copy-start(f32[512]{0:T(512)} %param.19) | copy-start | bytes 6148
  84.3 9.7 %copy-start.2 = (bf16[64,512]{1,0:T(8,128)(2,1)S(1)}, bf16[64,512]{1,0:T(8,128)(2,1)}, u32[]{:S(2)}) copy-start(bf16[64,512]{1,0:T(8,128)(2,1)} %param.17) | copy-start | bytes 196612
  84.3 9.5 %all-to-all-start.1 = ((bf16[4,64,128]{2,1,0:T(8,128)(2,1)}), bf16[4,64,128]{2,1,0:T(8,128)(2,1)S(1)}, u32[]{:S(2)}, u32[]{:S(2)}) async-start(bf16[4,64,128]{2,1,0:T(8,128)(2,1)} %bitcast.5), calls=%async_computation.1 | async-start | bytes 131072 | tf_op jit(solution)/shard_map/all_to_all | solution.py:246
  95.0 16.1 %all-to-all-start.2 = ((bf16[8,40,128]{2,1,0:T(8,128)(2,1)}), bf16[8,40,128]{2,1,0:T(8,128)(2,1)S(1)}, u32[]{:S(2)}, u32[]{:S(2)}) async-start(bf16[8,40,128]{2,1,0:T(8,128)(2,1)} %pad_maximum_fusion), calls=%async_computation.2 | async-start | bytes 163840 | tf_op jit(solution)/shard_map/all_to_all | solution.py:261
  145.4 15.3 %copy-start = (bf16[1,144,4096]{2,1,0:T(8,128)(2,1)S(1)}, bf16[1,144,4096]{2,1,0:T(8,128)(2,1)}, u32[]{:S(2)}) copy-start(bf16[1,144,4096]{2,1,0:T(8,128)(2,1)} %gate_ref.1) | copy-start | bytes 3538948
